TPU v7x, 256 devices: a whole 4x4x8 slice. The times are simulated.
256 devices in a mesh: fsdp: 32 (over z, y), model: 8 (over x, core).
Axes of the slice: x: 4, y: 4, z: 8, core: 2. Of those that a mesh axis runs over, the one named last changes fastest.
Arguments:
- x_in: bfloat16 [32, 512, 3072], P('fsdp', 'model')
- dy_in: bfloat16 [32, 512, 3072], P('fsdp', 'model')
- norm_gain: float32 [3072], replicated
- w_qkv: bfloat16 [3072, 5120], P('fsdp', 'model')
- w_out: bfloat16 [3072, 3072], P('model', 'fsdp')
- w_gate: bfloat16 [3072, 8192], P('fsdp', 'model')
- w_up: bfloat16 [3072, 8192], P('fsdp', 'model')
- w_down: bfloat16 [8192, 3072], P('model', 'fsdp')
- rope_cos: float32 [512, 64], replicated
- rope_sin: float32 [512, 64], replicated
Outputs:
- output 1: bfloat16 [32, 512, 3072], P('fsdp', 'model')
- output 2: bfloat16 [32, 512, 3072], P('fsdp', 'model')
- output 3: float32 [3072, 5120], P('fsdp', 'model')
- output 4: float32 [3072, 3072], P('model', 'fsdp')
- output 5: float32 [3072, 8192], P('fsdp', 'model')
- output 6: float32 [3072, 8192], P('fsdp', 'model')
- output 7: float32 [8192, 3072], P('model', 'fsdp')
All inputs are finite; a program needn't handle non-finite values.
Results may differ from a plain program's by a relative error of at most 0.00904269.
Values are sent between devices in bfloat16 or wider.
A program may use at most 768 MiB of HBM per device.

v0:
```python
import jax
import jax.numpy as jnp
from jax import lax
from jax.sharding import PartitionSpec as P, NamedSharding

NORM_EPS = 1e-5


def norm_fwd(row_vals, norm_gain):
    return row_vals * lax.rsqrt(jnp.mean(row_vals * row_vals, axis=-1, keepdims=True) + NORM_EPS) * norm_gain


def swiglu(gate_val, up_val):
    return (jax.nn.silu(gate_val.astype(jnp.float32)) * up_val.astype(jnp.float32)).astype(jnp.bfloat16)


def rotate(tensor, cos_tab, sin_tab):
    half_dim = tensor.shape[-1] // 2
    wide = tensor.astype(jnp.float32)
    lower_half = wide[..., :half_dim]
    upper_half = wide[..., half_dim:]
    return jnp.concatenate([lower_half * cos_tab - upper_half * sin_tab, upper_half * cos_tab + lower_half * sin_tab], axis=-1).astype(jnp.bfloat16)


def attention(qkv_val, rope_cos, rope_sin):
    batch_loc, seq_len, kv_loc, slot_count, head_dim = qkv_val.shape
    group_size = slot_count - 2
    queries = rotate(qkv_val[:, :, :, :group_size, :], rope_cos[None, :, None, None, :], rope_sin[None, :, None, None, :])
    key_rot = rotate(qkv_val[:, :, :, group_size, :], rope_cos[None, :, None, :], rope_sin[None, :, None, :])
    values = qkv_val[:, :, :, group_size + 1, :]
    scores = jnp.einsum("bqkgh,bpkh->bkgqp", queries, key_rot, preferred_element_type=jnp.float32) * head_dim ** -0.5
    causal = jnp.arange(seq_len)[:, None] >= jnp.arange(seq_len)[None, :]
    attn_probs = jax.nn.softmax(jnp.where(causal, scores, -1e30), axis=-1).astype(jnp.bfloat16)
    attn_out = jnp.einsum("bkgqp,bpkh->bqkgh", attn_probs, values, preferred_element_type=jnp.float32)
    return attn_out.astype(jnp.bfloat16).reshape(batch_loc, seq_len, kv_loc * group_size * head_dim)


def solution(mesh):
    act_spec = P("fsdp", "model", None)
    col_spec = P("fsdp", "model")
    row_spec = P("model", "fsdp")

    def layer_body(x_in, dy_in, norm_gain, w_qkv, w_out, w_gate, w_up, w_down, rope_cos, rope_sin):
        full_qkv = lax.all_gather(w_qkv, "fsdp", axis=0, tiled=True)
        full_out = lax.all_gather(w_out, "fsdp", axis=1, tiled=True)
        full_gate = lax.all_gather(w_gate, "fsdp", axis=0, tiled=True)
        full_up = lax.all_gather(w_up, "fsdp", axis=0, tiled=True)
        full_down = lax.all_gather(w_down, "fsdp", axis=1, tiled=True)
        x_rows = x_in.astype(jnp.float32)
        normed, norm_pull = jax.vjp(lambda row_vals: norm_fwd(row_vals, norm_gain), x_rows)
        h_full = lax.all_gather(normed.astype(jnp.bfloat16), "model", axis=1, tiled=True)
        batch_loc = h_full.shape[0]
        seq_len = h_full.shape[1]
        head_dim = 2 * rope_cos.shape[1]
        heads_loc = w_out.shape[0] // head_dim
        kv_loc = (w_qkv.shape[1] // head_dim - heads_loc) // 2
        qkv_val = jnp.einsum("bsd,dc->bsc", h_full, full_qkv, preferred_element_type=jnp.float32).astype(jnp.bfloat16)
        qkv_heads = qkv_val.reshape(batch_loc, seq_len, kv_loc, heads_loc // kv_loc + 2, head_dim)
        attn_val, attn_pull = jax.vjp(lambda packed: attention(packed, rope_cos, rope_sin), qkv_heads)
        gate_val = jnp.einsum("bsd,df->bsf", h_full, full_gate, preferred_element_type=jnp.float32).astype(jnp.bfloat16)
        up_val = jnp.einsum("bsd,df->bsf", h_full, full_up, preferred_element_type=jnp.float32).astype(jnp.bfloat16)
        act_val, act_pull = jax.vjp(swiglu, gate_val, up_val)
        part_sum = jnp.einsum("bsc,cd->bsd", attn_val, full_out, preferred_element_type=jnp.float32) + jnp.einsum("bsf,fd->bsd", act_val, full_down, preferred_element_type=jnp.float32)
        mix_sum = lax.psum_scatter(part_sum, "model", scatter_dimension=1, tiled=True)
        y_out = (x_rows + mix_sum).astype(jnp.bfloat16)
        dy_full = lax.all_gather(dy_in, "model", axis=1, tiled=True)
        dw_out = jnp.einsum("bsc,bsd->cd", attn_val, dy_full, preferred_element_type=jnp.float32)
        dw_down = jnp.einsum("bsf,bsd->fd", act_val, dy_full, preferred_element_type=jnp.float32)
        d_attn = jnp.einsum("bsd,cd->bsc", dy_full, full_out, preferred_element_type=jnp.float32).astype(jnp.bfloat16)
        d_act = jnp.einsum("bsd,fd->bsf", dy_full, full_down, preferred_element_type=jnp.float32).astype(jnp.bfloat16)
        d_qkv = attn_pull(d_attn)[0].reshape(batch_loc, seq_len, -1)
        d_gate, d_up = act_pull(d_act)
        dw_qkv = jnp.einsum("bsd,bsc->dc", h_full, d_qkv, preferred_element_type=jnp.float32)
        dw_gate = jnp.einsum("bsd,bsf->df", h_full, d_gate, preferred_element_type=jnp.float32)
        dw_up = jnp.einsum("bsd,bsf->df", h_full, d_up, preferred_element_type=jnp.float32)
        dh_part = jnp.einsum("bsc,dc->bsd", d_qkv, full_qkv, preferred_element_type=jnp.float32) + jnp.einsum("bsf,df->bsd", d_gate, full_gate, preferred_element_type=jnp.float32) + jnp.einsum("bsf,df->bsd", d_up, full_up, preferred_element_type=jnp.float32)
        d_h = lax.psum_scatter(dh_part, "model", scatter_dimension=1, tiled=True).astype(jnp.bfloat16)
        dx_out = (dy_in.astype(jnp.float32) + norm_pull(d_h.astype(jnp.float32))[0]).astype(jnp.bfloat16)
        return (
            y_out,
            dx_out,
            lax.psum_scatter(dw_qkv, "fsdp", scatter_dimension=0, tiled=True),
            lax.psum_scatter(dw_out, "fsdp", scatter_dimension=1, tiled=True),
            lax.psum_scatter(dw_gate, "fsdp", scatter_dimension=0, tiled=True),
            lax.psum_scatter(dw_up, "fsdp", scatter_dimension=0, tiled=True),
            lax.psum_scatter(dw_down, "fsdp", scatter_dimension=1, tiled=True),
        )

    return jax.shard_map(
        layer_body,
        mesh=mesh,
        in_specs=(act_spec, act_spec, P(), col_spec, row_spec, col_spec, col_spec, row_spec, P(), P()),
        out_specs=(act_spec, act_spec, col_spec, row_spec, col_spec, col_spec, row_spec),
        check_vma=False,
    )
```

profile of v0, /device:TPU:1, one launch (start us, length us, event | category | flops | bytes accessed | tf_op | source)
XLA Modules:
  0.0 1799.8 jit_solution(16801916745577039595)
XLA Ops:
  8.7 1.2 fusion.78
  11.0 1.9 fusion.80
  15.5 1.0 copy.34
  16.7 0.8 iota_compare_fusion
  17.4 70.4 %all-gather.12.cloned.1.call-done = bf16[384,3072]{0,1:T(8,128)(2,1)} async-done(((bf16[384,96]{0,1:T(8,128)(2,1)}), bf16[384,3072]{0,1:T(8,128)(2,1)}) %all-gather.12.cloned.1.call-update) | async-done | bytes 2359312 | tf_op jit(solution)/shard_map/all_gather | solution.py:45
  87.9 33.9 %all-gather.20.cloned.1.call-done = bf16[1,512,3072]{2,1,0:T(8,128)(2,1)} async-done(((bf16[1,64,3072]{2,1,0:T(8,128)(2,1)}), bf16[1,512,3072]{2,1,0:T(8,128)(2,1)}) %all-gather.20.cloned.1.call-update) | async-done | bytes 3145744 | tf_op jit(solution)/shard_map/all_gather | solution.py:66
  121.8 4.8 fusion.57
  126.6 27.8 %all-gather.8.cloned.1.call-done = bf16[1,512,3072]{2,1,0:T(8,128)(2,1)} async-done(((bf16[1,64,3072]{2,1,0:T(8,128)(2,1)}), bf16[1,512,3072]{2,1,0:T(8,128)(2,1)}) %all-gather.8.cloned.1.call-update) | async-done | bytes 3145744 | tf_op jit(solution)/shard_map/all_gather | solution.py:51
  154.4 79.6 %all-gather.10.cloned.1.call-done = bf16[3072,640]{1,0:T(8,128)(2,1)} async-done(((bf16[96,640]{1,0:T(8,128)(2,1)}), bf16[3072,640]{1,0:T(8,128)(2,1)}) %all-gather.10.cloned.1.call-update) | async-done | bytes 3932176 | tf_op jit(solution)/shard_map/all_gather | solution.py:44
  234.0 5.7 fusion.51
  240.0 0.8 copy-done.11
  241.8 1.9 fusion.29
  244.4 2.1 fusion.8
  246.5 1.7 fusion.73
  248.6 1.7 fusion.61
  250.9 1.2 fusion.69
  252.1 0.9 pad_add_fusion
  253.0 2.2 copy.47
  255.2 69.2 %all-gather.14.cloned.1.call-done = bf16[3072,1024]{1,0:T(8,128)(2,1)} async-done(((bf16[96,1024]{1,0:T(8,128)(2,1)}), bf16[3072,1024]{1,0:T(8,128)(2,1)}) %all-gather.14.cloned.1.call-update) | async-done | bytes 6291472 | tf_op jit(solution)/shard_map/all_gather | solution.py:46
  324.3 8.2 fusion.42
  332.5 79.4 %all-gather.16.cloned.1.call-done = bf16[3072,1024]{1,0:T(8,128)(2,1)} async-done(((bf16[96,1024]{1,0:T(8,128)(2,1)}), bf16[3072,1024]{1,0:T(8,128)(2,1)}) %all-gather.16.cloned.1.call-update) | async-done | bytes 6291472 | tf_op jit(solution)/shard_map/all_gather | solution.py:47
  411.9 8.1 fusion.45
  420.0 79.6 %all-gather.18.cloned.1.call-done = bf16[1024,3072]{0,1:T(8,128)(2,1)} async-done(((bf16[1024,96]{0,1:T(8,128)(2,1)}), bf16[1024,3072]{0,1:T(8,128)(2,1)}) %all-gather.18.cloned.1.call-update) | async-done | bytes 6291472 | tf_op jit(solution)/shard_map/all_gather | solution.py:48
  499.6 7.3 fusion.48
  507.0 3.6 fusion.105
  510.6 7.0 fusion.111
  517.6 4.6 add_bitcast_fusion
  522.3 2.3 fusion.54
  524.7 6.2 fusion.108
  530.9 4.5 add_bitcast_fusion.1
  535.5 1.8 copy-done.7
  537.3 4.0 fusion.11
  541.6 0.8 copy-done.4
  542.4 7.6 fusion.21
  550.1 1.8 copy-done.6
  551.9 8.6 fusion.19
  560.6 8.2 fusion.17
  568.8 1.8 copy-done.8
  570.6 8.2 fusion.9
  578.9 0.9 copy-done.2
  579.8 1.3 fusion.82
  581.1 31.4 %reduce-scatter.8.cloned.1.call-done = f32[1,64,3072]{2,1,0:T(8,128)} async-done(((f32[1,512,3072]{2,1,0:T(8,128)}), f32[1,64,3072]{2,1,0:T(8,128)}) %reduce-scatter.8.cloned.1.call-update) | async-done | bytes 786448 | tf_op jit(solution)/shard_map/reduce_scatter | solution.py:64
  612.6 2.5 fusion.77
  615.1 222.9 %reduce-scatter.14.cloned.1.call-done = f32[384,96]{0,1:T(8,128)} async-done(((f32[384,3072]{0,1:T(8,128)}), f32[384,96]{0,1:T(8,128)}) %reduce-scatter.14.cloned.1.call-update) | async-done | bytes 147472 | tf_op jit(solution)/shard_map/reduce_scatter | solution.py:83
  838.1 231.8 %reduce-scatter.12.cloned.1.call-done = f32[96,640]{1,0:T(8,128)} async-done(((f32[3072,640]{1,0:T(8,128)}), f32[96,640]{1,0:T(8,128)}) %reduce-scatter.12.cloned.1.call-update) | async-done | bytes 245776 | tf_op jit(solution)/shard_map/reduce_scatter | solution.py:82
  1069.9 241.0 %reduce-scatter.16.cloned.1.call-done = f32[96,1024]{1,0:T(8,128)} async-done(((f32[3072,1024]{1,0:T(8,128)}), f32[96,1024]{1,0:T(8,128)}) %reduce-scatter.16.cloned.1.call-update) | async-done | bytes 393232 | tf_op jit(solution)/shard_map/reduce_scatter | solution.py:84
  1310.9 241.3 %reduce-scatter.18.cloned.1.call-done = f32[96,1024]{1,0:T(8,128)} async-done(((f32[3072,1024]{1,0:T(8,128)}), f32[96,1024]{1,0:T(8,128)}) %reduce-scatter.18.cloned.1.call-update) | async-done | bytes 393232 | tf_op jit(solution)/shard_map/reduce_scatter | solution.py:85
  1552.2 240.6 %reduce-scatter.20.cloned.1.call-done = f32[1024,96]{0,1:T(8,128)} async-done(((f32[1024,3072]{0,1:T(8,128)}), f32[1024,96]{0,1:T(8,128)}) %reduce-scatter.20.cloned.1.call-update) | async-done | bytes 393232 | tf_op jit(solution)/shard_map/reduce_scatter | solution.py:86
  (94 shorter events, 8.8 us)
Async XLA Ops:
  7.2 9.3 copy-start.13
  7.2 80.7 %all-gather.12.cloned.1.call-start = ((), (), s32[]{:S(2)}) async-start(), calls=%async_computation.9 | async-start | bytes 2433024 | tf_op jit(solution)/shard_map/all_gather | solution.py:45
  7.9 113.9 %all-gather.20.cloned.1.call-start = ((), (), s32[]{:S(2)}) async-start(), calls=%async_computation.14 | async-start | bytes 3538944 | tf_op jit(solution)/shard_map/all_gather | solution.py:66
  8.7 145.8 %all-gather.8.cloned.1.call-start = ((), (), s32[]{:S(2)}) async-start(), calls=%async_computation.7 | async-start | bytes 3538944 | tf_op jit(solution)/shard_map/all_gather | solution.py:51
  9.9 0.5 copy-start.17
  10.4 0.6 copy-start.15
  12.9 221.1 %all-gather.10.cloned.1.call-start = ((), (), s32[]{:S(2)}) async-start(), calls=%async_computation.8 | async-start | bytes 4055040 | tf_op jit(solution)/shard_map/all_gather | solution.py:44
  13.5 310.8 %all-gather.14.cloned.1.call-start = ((), (), s32[]{:S(2)}) async-start(), calls=%async_computation.10 | async-start | bytes 6488064 | tf_op jit(solution)/shard_map/all_gather | solution.py:46
  14.1 397.8 %all-gather.16.cloned.1.call-start = ((), (), s32[]{:S(2)}) async-start(), calls=%async_computation.11 | async-start | bytes 6488064 | tf_op jit(solution)/shard_map/all_gather | solution.py:47
  14.7 484.9 %all-gather.18.cloned.1.call-start = ((), (), s32[]{:S(2)}) async-start(), calls=%async_computation.12 | async-start | bytes 6488064 | tf_op jit(solution)/shard_map/all_gather | solution.py:48
  15.4 563.4 %reduce-scatter.10.cloned.1.call-start = ((), (), s32[]{:S(2)}) async-start(), calls=%async_computation.15 | async-start | bytes 7077888 | tf_op jit(solution)/shard_map/reduce_scatter | solution.py:77
  16.6 224.7 %copy-start = (f32[512,64]{1,0:T(8,128)}, f32[512,64]{1,0:T(8,128)S(1)}, u32[]{:S(2)}) copy-start(f32[512,64]{1,0:T(8,128)S(1)} %copy.35) | copy-start | bytes 393220
  239.9 0.9 copy-start.11
  241.4 2.3 copy-start.10
  241.8 2.7 copy-start.20
  246.5 1.8 copy-start.1
  499.6 7.3 copy-start.19
  499.6 7.3 copy-start.21
  506.9 3.6 copy-start.25
  506.9 3.6 copy-start.23
  510.6 7.0 copy-start.3
  510.6 7.0 copy-start.5
  522.3 90.3 %reduce-scatter.8.cloned.1.call-start = ((), (), s32[]{:S(2)}) async-start(), calls=%async_computation.13 | async-start | bytes 7077888 | tf_op jit(solution)/shard_map/reduce_scatter | solution.py:64
  522.3 2.3 copy-start.22
  522.3 2.3 copy-start.24
  524.6 6.2 copy-start.9
  535.4 1.9 copy-start.7
  535.4 302.6 %reduce-scatter.14.cloned.1.call-start = ((), (), s32[]{:S(2)}) async-start(), calls=%async_computation.17 | async-start | bytes 4866048 | tf_op jit(solution)/shard_map/reduce_scatter | solution.py:83
  541.3 1.1 copy-start.4
  541.3 528.6 %reduce-scatter.12.cloned.1.call-start = ((), (), s32[]{:S(2)}) async-start(), calls=%async_computation.16 | async-start | bytes 8110080 | tf_op jit(solution)/shard_map/reduce_scatter | solution.py:82
  550.0 1.9 copy-start.6
  550.0 760.9 %reduce-scatter.16.cloned.1.call-start = ((), (), s32[]{:S(2)}) async-start(), calls=%async_computation.18 | async-start | bytes 12976128 | tf_op jit(solution)/shard_map/reduce_scatter | solution.py:84
  560.5 991.7 %reduce-scatter.18.cloned.1.call-start = ((), (), s32[]{:S(2)}) async-start(), calls=%async_computation.19 | async-start | bytes 12976128 | tf_op jit(solution)/shard_map/reduce_scatter | solution.py:85
  568.7 1.9 copy-start.8
  568.7 1224.1 %reduce-scatter.20.cloned.1.call-start = ((), (), s32[]{:S(2)}) async-start(), calls=%async_computation.20 | async-start | bytes 12976128 | tf_op jit(solution)/shard_map/reduce_scatter | solution.py:86
  578.8 1.0 copy-start.2
  578.8 1.0 copy-start.14
  578.8 2.3 copy-start.18
  578.8 33.8 %copy-start.12 = (bf16[1,64,3072]{2,1,0:T(8,128)(2,1)S(1)}, bf16[1,64,3072]{2,1,0:T(8,128)(2,1)}, u32[]{:S(2)}) copy-start(bf16[1,64,3072]{2,1,0:T(8,128)(2,1)} %param.11) | copy-start | bytes 1179652
  578.8 33.8 %copy-start.16 = (f32[64]{0:T(128)S(1)}, f32[64]{0:T(128)}, u32[]{:S(2)}) copy-start(f32[64]{0:T(128)} %copy-done.15) | copy-start | bytes 772
Sparse Core Ops, SparseCore 0:
  10.6 77.2 all-gather.11
  89.7 32.0 all-gather.19
  124.2 30.1 all-gather.7
  156.9 77.0 all-gather.9
  236.4 87.8 all-gather.13
  326.7 85.1 all-gather.15
  414.5 85.1 all-gather.17
  522.4 42.7 reduce-scatter.9
  567.7 44.7 reduce-scatter.7
  616.9 221.0 reduce-scatter.13
  842.7 227.1 reduce-scatter.11
  1074.5 236.3 reduce-scatter.15
  1315.6 236.5 reduce-scatter.17
  1556.8 236.0 reduce-scatter.19
where the time goes:
time: 1810 us; the launch traced here: 1800 us
  waiting for transfers between devices  1650 us (91%)
  matrix products  107 us (6%)
    reduce_scatter x1, waiting for transfers between devices, layer_body(): lax.psum_scatter(dw_up, 'fsdp', scatter_dimension=0, tiled=True)  241 us
    reduce_scatter x1, waiting for transfers between devices, layer_body(): lax.psum_scatter(dw_gate, 'fsdp', scatter_dimension=0, tiled=True)  241 us
    reduce_scatter x1, waiting for transfers between devices, layer_body(): lax.psum_scatter(dw_down, 'fsdp', scatter_dimension=1, tiled=True)  241 us
    reduce_scatter x1, waiting for transfers between devices, layer_body(): lax.psum_scatter(dw_qkv, 'fsdp', scatter_dimension=0, tiled=True)  232 us
    reduce_scatter x1, waiting for transfers between devices, layer_body(): lax.psum_scatter(dw_out, 'fsdp', scatter_dimension=1, tiled=True)  223 us
    all_gather x1, waiting for transfers between devices, layer_body(): full_down = lax.all_gather(w_down, 'fsdp', axis=1, tiled=True)  79.6 us
    all_gather x1, waiting for transfers between devices, layer_body(): full_qkv = lax.all_gather(w_qkv, 'fsdp', axis=0, tiled=True)  79.6 us
    all_gather x1, waiting for transfers between devices, layer_body(): full_up = lax.all_gather(w_up, 'fsdp', axis=0, tiled=True)  79.4 us
  transfers between devices with their start and end apart: 14, of which 13 were waited for; matrix products, arithmetic and copies ran while one was open for 6% of the time, Pallas kernels for 0%

commit v1 on v0

v1 whole, which is shorter than its diff:
```python
import functools
import heapq

import jax
import jax.numpy as jnp
from jax import lax
from jax.experimental import pallas as pl
from jax.experimental.pallas import tpu as pltpu
from jax.sharding import PartitionSpec as P

NORM_EPS = 1e-5
NY, NX, NC = 4, 4, 2
MESH = pl.DeviceIdType.MESH
LINK = 46.6e3
PAIR = 330e3
HOP = 3.5
ADD = 0.4
VMEM_LIMIT = 62 * 1024 * 1024


class Place:
    def __init__(self, nz):
        i, j = lax.axis_index("fsdp"), lax.axis_index("model")
        self.size = {"z": nz, "y": NY, "x": NX, "c": NC}
        self.at = {"z": lax.div(i, NY), "y": lax.rem(i, NY), "x": lax.div(j, NC), "c": lax.rem(j, NC)}

    def get(self, axis, step=0):
        n = self.size[axis]
        return lax.rem(self.at[axis] + (step + 2 * n) % n, n)

    def device(self, axis, step):
        at = dict(self.at)
        at[axis] = self.get(axis, step)
        return {"fsdp": at["z"] * NY + at["y"], "model": at["x"] * NC + at["c"]}

    def meet(self, peers):
        barrier = pltpu.get_barrier_semaphore()
        for axis, step in peers:
            pl.semaphore_signal(barrier, inc=1, device_id=self.device(axis, step), device_id_type=MESH)
        pl.semaphore_wait(barrier, len(peers))


class Flow:
    def __init__(self, place, send_sem, recv_sem, emit=True):
        self.place, self.send_sem, self.recv_sem, self.emit = place, send_sem, recv_sem, emit
        self.now, self.free, self.events, self.copies = 0.0, {}, [], []

    def send(self, axis, step, src, dst, size, then=None, link=None):
        k = len(self.copies)
        link = link or (axis, step)
        begin = max(self.now, self.free.get(link, 0.0))
        rate, lag = (PAIR, 1.5) if axis == "c" else (LINK, HOP)
        self.free[link] = begin + size / rate
        copy = None
        if self.emit:
            copy = pltpu.make_async_remote_copy(
                src_ref=src(),
                dst_ref=dst(),
                send_sem=self.send_sem.at[k],
                recv_sem=self.recv_sem.at[k],
                device_id=self.place.device(axis, step),
                device_id_type=MESH,
            )
            copy.start()
        self.copies.append(copy)
        heapq.heappush(self.events, (self.free[link] + lag, k, then))

    def run(self):
        while self.events:
            when, k, then = heapq.heappop(self.events)
            self.now = max(self.now, when)
            if self.emit:
                self.copies[k].wait_recv()
            if then is not None:
                then()
        if self.emit:
            for copy in self.copies:
                copy.wait_send()


def after(count, then):
    left = [count]

    def one():
        left[0] -= 1
        if left[0] == 0:
            then()

    return one


def nbytes(ref, lead):
    n = 1
    for d in ref.shape[lead:]:
        n *= d
    return n * jnp.dtype(ref.dtype).itemsize


def gather_kernel(nz, h_ref, dy_ref, w_ref, h_all, dy_all, w_all, send_sem, recv_sem, own_sem):
    place = Place(nz)
    y, x, c, z = place.get("y"), place.get("x"), place.get("c"), place.get("z")
    place.meet([("x", 1), ("x", -1), ("y", 1), ("y", -1), ("y", 2), ("z", 1), ("z", -1), ("c", 1)])
    flow = Flow(place, send_sem, recv_sem)
    own = [
        pltpu.make_async_copy(h_ref, h_all.at[y, x, c], own_sem.at[0]),
        pltpu.make_async_copy(dy_ref, dy_all.at[y, x, c], own_sem.at[1]),
        pltpu.make_async_copy(w_ref.at[y], w_all.at[0, z, y], own_sem.at[2]),
    ]
    for copy in own:
        copy.start()
    piece = nbytes(h_ref, 1)

    def spot(ref, dy, dx, half):
        return lambda: ref.at[place.get("y", dy), place.get("x", dx), c, half]

    def spread(axis, half, offset, src, got):
        def come(step, onward):
            def then():
                if onward:
                    flow.send(axis, -step, got.spot(axis, step, offset, half), got.spot(axis, step, offset, half), piece, lambda: got(axis, 2, offset, half))
                got(axis, step, offset, half)

            return then

        flow.send(axis, 1, src, got.spot(axis, 0, offset, half), piece, come(-1, half == 0))
        flow.send(axis, -1, src, got.spot(axis, 0, offset, half), piece, come(1, half == 1))

    class Got:
        def __init__(self, ref, first):
            self.ref, self.first, self.second = ref, first, "y" if first == "x" else "x"

        def spot(self, axis, step, offset, half):
            d = {axis: step, ("y" if axis == "x" else "x"): offset}
            return spot(self.ref, d["y"], d["x"], half)

        def __call__(self, axis, step, offset, half):
            here = self.spot(axis, step, offset, half)
            if axis == self.first:
                spread(self.second, half, step, here, self)
            flow.send("c", 1, here, here, piece)

    arrays = [(h_ref, Got(h_all, "x")), (dy_ref, Got(dy_all, "y"))]
    for ref, got in arrays:
        for half in (0, 1):
            spread(got.first, half, 0, lambda ref=ref, half=half: ref.at[half], got)

    size = nbytes(w_ref, 1)

    def w_spot(who, dz, dy):
        return lambda: w_all.at[who, place.get("z", dz), place.get("y", dy)]

    def ring(step, dy):
        def pair(dz):
            flow.send("c", 1, w_spot(0, dz, dy), w_spot(1, dz, dy), size)

        def hop(n):
            def then():
                if n < nz - 1:
                    flow.send("z", step, w_spot(0, -step * n, dy), w_spot(0, -step * n, dy), size, hop(n + 1))
                pair(-step * n)

            return then

        return hop(0)

    flow.send("y", -1, lambda: w_ref.at[place.get("y", -1)], w_spot(0, 0, 0), size, ring(1, 1))
    flow.send("y", 1, lambda: w_ref.at[place.get("y", 1)], w_spot(0, 0, 0), size, ring(-1, -1))
    flow.send("y", 2, lambda: w_ref.at[place.get("y", 2)], w_spot(0, 0, 0), size, ring(-1, 2), link=("y", 1))
    for ref, got in arrays:
        for half in (0, 1):
            src = lambda ref=ref, half=half: ref.at[half]
            spread(got.second, half, 0, src, got)
            flow.send("c", 1, src, got.spot(got.second, 0, 0, half), piece)
    own[2].wait()
    ring(1, 0)()
    flow.run()
    own[0].wait()
    own[1].wait()


def any_specs(n):
    return [pl.BlockSpec(memory_space=pl.ANY)] * n


def gather(nz, h, dy, w):
    half, rows, width = h.shape
    everywhere = (NY, NX, NC) + h.shape
    count = 60 + 64 + 3 + 4 * (nz - 1) + 4 * nz
    vmem = pl.BlockSpec(memory_space=pltpu.VMEM)
    return pl.pallas_call(
        functools.partial(gather_kernel, nz),
        out_shape=(
            jax.ShapeDtypeStruct(everywhere, h.dtype),
            jax.ShapeDtypeStruct(everywhere, dy.dtype),
            jax.ShapeDtypeStruct((NC, nz) + w.shape, w.dtype),
        ),
        in_specs=[vmem] * 3,
        out_specs=tuple(any_specs(3)),
        scratch_shapes=[pltpu.SemaphoreType.DMA((count,)), pltpu.SemaphoreType.DMA((count,)), pltpu.SemaphoreType.DMA((3,))],
        compiler_params=pltpu.CompilerParams(collective_id=0, has_side_effects=True),
        name="gather",
    )(h, dy, w)


def exchange(flow, place, src, dst, far):
    size = nbytes(src, 1)

    def to(step):
        return lambda: src.at[place.get("y", step)]

    def spot(step):
        return lambda: dst.at[place.get("y", step)]

    def onward(step, half):
        def then():
            flow.send("y", step, lambda: far.at[half], lambda: dst.at[place.get("y", -step), half], size // 2)

        return then

    flow.send("y", 1, lambda: src.at[place.get("y", 2), 0], lambda: far.at[0], size // 2, onward(1, 0))
    flow.send("y", -1, lambda: src.at[place.get("y", 2), 1], lambda: far.at[1], size // 2, onward(-1, 1))
    flow.send("y", 1, to(1), spot(0), size)
    flow.send("y", -1, to(-1), spot(0), size)


def first_exchange_kernel(nz, src, dst, far, send_sem, recv_sem, own_sem):
    place = Place(nz)
    y = place.get("y")
    place.meet([("y", 1), ("y", -1)])
    flow = Flow(place, send_sem, recv_sem)
    own = pltpu.make_async_copy(src.at[y], dst.at[y], own_sem)
    own.start()
    exchange(flow, place, src, dst, far)
    flow.run()
    own.wait()


def first_exchange(nz, src):
    vmem = pl.BlockSpec(memory_space=pltpu.VMEM)
    return pl.pallas_call(
        functools.partial(first_exchange_kernel, nz),
        out_shape=jax.ShapeDtypeStruct(src.shape, src.dtype),
        in_specs=[vmem],
        out_specs=pl.BlockSpec(memory_space=pl.ANY),
        scratch_shapes=[pltpu.VMEM(src.shape[1:], src.dtype), pltpu.SemaphoreType.DMA((6,)), pltpu.SemaphoreType.DMA((6,)), pltpu.SemaphoreType.DMA],
        compiler_params=pltpu.CompilerParams(collective_id=1, has_side_effects=True),
        name="exchange_in",
    )(src)


def second_exchange_kernel(nz, src, acts, dst, pair_dst, pair_acts, far, send_sem, recv_sem, own_sem):
    place = Place(nz)
    y, c = place.get("y"), place.get("c")
    other = place.get("c", 1)
    place.meet([("y", 1), ("y", -1), ("c", 1)])
    flow = Flow(place, send_sem, recv_sem)
    own = pltpu.make_async_copy(src.at[y], dst.at[y], own_sem)
    own.start()
    exchange(flow, place, src, dst, far)
    for q in range(NY):
        flow.send("c", 1, lambda q=q: acts.at[q, :, other], lambda q=q: pair_acts.at[q], nbytes(pair_acts, 1))
    flow.run()
    own.wait()
    tail = Flow(place, send_sem, recv_sem)
    tail.copies = [None] * len(flow.copies)
    count = len(flow.copies)
    for q in range(NY):
        for p in range(2):
            tail.send("c", 1, lambda q=q, p=p: dst.at[q, p, :, other], lambda q=q, p=p: pair_dst.at[q, p], nbytes(pair_dst, 2))
    tail.copies = tail.copies
    while tail.events:
        _, k, _ = heapq.heappop(tail.events)
        tail.copies[k].wait_recv()
    for copy in tail.copies[count:]:
        copy.wait_send()


def second_exchange(nz, src, acts):
    vmem = pl.BlockSpec(memory_space=pltpu.VMEM)
    count = 6 + NY + 2 * NY
    return pl.pallas_call(
        functools.partial(second_exchange_kernel, nz),
        out_shape=(
            jax.ShapeDtypeStruct(src.shape, src.dtype),
            jax.ShapeDtypeStruct(src.shape[:3] + src.shape[4:], src.dtype),
            jax.ShapeDtypeStruct(acts.shape[:2] + acts.shape[3:], acts.dtype),
        ),
        in_specs=[vmem, vmem],
        out_specs=tuple(any_specs(3)),
        scratch_shapes=[pltpu.VMEM(src.shape[1:], src.dtype), pltpu.SemaphoreType.DMA((count,)), pltpu.SemaphoreType.DMA((count,)), pltpu.SemaphoreType.DMA],
        compiler_params=pltpu.CompilerParams(collective_id=2, has_side_effects=True),
        name="exchange_out",
    )(src, acts)


class Stage:
    def __init__(self, buffers, sem, depth, order=None):
        self.buffers, self.sem, self.depth, self.order = buffers, sem, depth, order
        self.used, self.copies = [], []

    def fetch(self):
        k = len(self.copies)
        if k < len(self.order):
            copy = pltpu.make_async_copy(self.order[k](), self.buffers.at[k % self.depth], self.sem.at[k % self.depth])
            copy.start()
            self.copies.append(copy)

    def begin(self):
        for _ in range(self.depth):
            self.fetch()

    def take(self, src, use):
        k = len(self.used)
        self.used.append(src)
        if self.order is not None:
            self.copies[k].wait()
            use(self.buffers.at[k % self.depth])
            self.fetch()


def scatter_plan(nz, place, flow, take, refs, add):
    y_part, d_part, g_part, y_sum, d_sum, g_all, land, z_land, far = refs
    piece = nbytes(y_part, 3)

    def reduce_ring(axis, raw, take_local, slot, done):
        def turn(s, goal, half, step):
            def then():
                take_local(goal, half, lambda ref: add(slot(s), ref))
                flow.send(axis, step, slot(s), slot(s + 4), piece, final[half])

            return then

        def finish(half):
            def then():
                mine, other = (slot(5), slot(2)) if half == 0 else (slot(4), slot(3))
                add(mine, other)
                take_local(0, half, lambda ref: add(mine, ref))
                done(half, mine)

            return then

        final = [after(2, finish(0)), after(2, finish(1))]

        def start(goal, half):
            if (goal, half) == (2, 1):
                flow.send(axis, 1, raw(2, 1), slot(0), piece, turn(0, 1, 1, 1))
            if (goal, half) == (2, 0):
                flow.send(axis, -1, raw(2, 0), slot(1), piece, turn(1, -1, 0, -1))
            if (goal, half) == (1, 0):
                flow.send(axis, 1, raw(1, 0), slot(2), piece, final[0])
            if (goal, half) == (-1, 1):
                flow.send(axis, -1, raw(-1, 1), slot(3), piece, final[1])

        return start

    sets = (2, 1, -1, 0)

    def plane(n, part, out, first):
        second = "y" if first == "x" else "x"
        sums = {}

        def slot_of(s):
            return lambda i: (lambda: land.at[n, s, i])

        def direct(step, half):
            return sums[step, half]

        def take_sum(step, half, use):
            use(sums[step, half])

        waits = {}

        def last(half, ref):
            if flow.emit:
                out[half] = ref()[...]

        def ready(step, half):
            return (step, half) in sums

        held = []

        def take_second(step, half, use):
            if ready(step, half):
                use(sums[step, half])
            else:
                raise AssertionError("order")

        second_start = reduce_ring(second, direct, take_second, slot_of(4), last)

        def first_done(step):
            def done(half, ref):
                sums[step, half] = ref
                second_start(step, half)

            return done

        starts = []
        for s, other in enumerate(sets):

            def raw(step, half, other=other):
                d = {first: step, second: other}
                return lambda: part.at[place.get("y", d["y"]), place.get("x", d["x"]), half]

            def take_local(step, half, use, raw=raw):
                take(raw(step, half), use)

            starts.append(reduce_ring(first, raw, take_local, slot_of(s), first_done(other)))
        return starts

    y_starts = plane(0, y_part, y_sum, "y")
    d_starts = plane(1, d_part, d_sum, "x")

    size = nbytes(g_part, 2)

    def g_raw(dz, dy):
        return lambda: g_part.at[place.get("z", dz), place.get("y", dy)]

    def home(dy, ref):
        mine = lambda: g_all.at[place.get("y")]
        if dy == 0:
            flow.keep(ref, mine)
        elif dy == 2:
            for half, step in ((0, 1), (1, -1)):

                def onward(half=half, step=step):
                    flow.send("y", step, lambda: far.at[half], lambda: g_all.at[place.get("y", -step), half], size // 2)

                flow.send("y", step, lambda half=half: ref().at[half], lambda half=half: far.at[half], size // 2, onward)
        else:
            flow.send("y", dy, ref, mine, size)

    def ring(step, lane, dy):
        n = 0 if step == 1 else 1

        def spot(s):
            return lambda: z_land.at[n, s, lane]

        def hop(s):
            def then():
                take_g(g_raw(-step * (s + 2), dy), spot(s))
                if s < nz - 2:
                    flow.send("z", step, spot(s), spot(s + 1), size, hop(s + 1))
                else:
                    home(dy, spot(s))

            return then

        flow.send("z", step, g_raw(-step, dy), spot(0), size, hop(0))

    def take_g(src, ref):
        take(src, lambda got: add(ref, got), True)

    ring(1, 0, 2)
    ring(-1, 0, 1)
    ring(1, 1, 0)
    ring(-1, 1, -1)
    for one, two in zip(y_starts, d_starts):
        for start in (one, two):
            start(2, 1)
            start(2, 0)
            start(1, 0)
            start(-1, 1)
    flow.run()


def add_into(mine, other, chunk=96):
    a, b = mine(), other
    if callable(b):
        b = b()
    flat = a.shape[:-2]
    index = tuple([slice(None)] * len(flat))
    a[...] = a[...] + b[...]


def scatter_kernel(nz, depth, y_part, d_part, g_part, y_sum, d_sum, g_all, land, z_land, far, stage, g_stage, send_sem, recv_sem, stage_sem, g_stage_sem, own_sem):
    place = Place(nz)
    refs = (y_part, d_part, g_part, y_sum, d_sum, g_all, land, z_land, far)

    def trial(flow, stages):
        def keep(ref, mine):
            if flow.emit:
                flow.own = pltpu.make_async_copy(ref(), mine(), own_sem)
                flow.own.start()

        flow.keep = keep

        def take(src, use, grad=False):
            flow.now += ADD
            stages[int(grad)].take(src, use)

        def add(mine, other):
            if flow.emit:
                add_into(mine, other)

        scatter_plan(nz, place, flow, take, refs, add)

    dry = [Stage(None, None, depth), Stage(None, None, depth)]
    trial(Flow(place, None, None, emit=False), dry)
    wet = [Stage(stage, stage_sem, depth, dry[0].used), Stage(g_stage, g_stage_sem, depth, dry[1].used)]
    for one in wet:
        one.begin()
    place.meet([("x", 1), ("x", -1), ("y", 1), ("y", -1), ("z", 1), ("z", -1)])
    flow = Flow(place, send_sem, recv_sem)
    trial(flow, wet)
    flow.own.wait()


def scatter(nz, y_part, d_part, g_part):
    depth = 6
    piece = y_part.shape[2:]
    block = g_part.shape[2:]
    count = 2 * 5 * 6 + 4 * (nz - 1) + 2 + 4
    vmem = pl.BlockSpec(memory_space=pltpu.VMEM)
    f32 = jnp.float32
    dma = pltpu.SemaphoreType.DMA
    return pl.pallas_call(
        functools.partial(scatter_kernel, nz, depth),
        out_shape=(
            jax.ShapeDtypeStruct(piece, f32),
            jax.ShapeDtypeStruct(piece, f32),
            jax.ShapeDtypeStruct((NY,) + block, f32),
        ),
        in_specs=any_specs(3),
        out_specs=(vmem, vmem, pl.BlockSpec(memory_space=pl.ANY)),
        scratch_shapes=[
            pltpu.VMEM((2, 5, 6) + piece[1:], f32),
            pltpu.VMEM((2, nz - 1, 2) + block, f32),
            pltpu.VMEM(block, f32),
            pltpu.VMEM((depth,) + piece[1:], f32),
            pltpu.VMEM((depth,) + block, f32),
            dma((count,)),
            dma((count,)),
            dma((depth,)),
            dma((depth,)),
            dma,
        ],
        compiler_params=pltpu.CompilerParams(collective_id=3, has_side_effects=True, vmem_limit_bytes=VMEM_LIMIT),
        name="scatter",
    )(y_part, d_part, g_part)


def norm_fwd(row_vals, norm_gain):
    return row_vals * lax.rsqrt(jnp.mean(row_vals * row_vals, axis=-1, keepdims=True) + NORM_EPS) * norm_gain


def swiglu(gate_val, up_val):
    return (jax.nn.silu(gate_val.astype(jnp.float32)) * up_val.astype(jnp.float32)).astype(jnp.bfloat16)


def rotate(tensor, cos_tab, sin_tab):
    half_dim = tensor.shape[-1] // 2
    wide = tensor.astype(jnp.float32)
    lower_half = wide[..., :half_dim]
    upper_half = wide[..., half_dim:]
    return jnp.concatenate([lower_half * cos_tab - upper_half * sin_tab, upper_half * cos_tab + lower_half * sin_tab], axis=-1).astype(jnp.bfloat16)


def attention(heads, rope_cos, rope_sin):
    seq_len, head_dim = heads.shape[1:]
    queries = rotate(heads[:-2], rope_cos[None], rope_sin[None])
    key_rot = rotate(heads[-2], rope_cos, rope_sin)
    values = heads[-1]
    scores = jnp.einsum("gqh,ph->gqp", queries, key_rot, preferred_element_type=jnp.float32) * head_dim ** -0.5
    causal = jnp.arange(seq_len)[:, None] >= jnp.arange(seq_len)[None, :]
    attn_probs = jax.nn.softmax(jnp.where(causal, scores, -1e30), axis=-1).astype(jnp.bfloat16)
    return jnp.einsum("gqp,ph->gqh", attn_probs, values, preferred_element_type=jnp.float32).astype(jnp.bfloat16)


def mm(a, b, ca, cb):
    return lax.dot_general(a, b, (((ca,), (cb,)), ((), ())), preferred_element_type=jnp.float32)


def solution(mesh):
    act_spec = P("fsdp", "model", None)
    col_spec = P("fsdp", "model")
    row_spec = P("model", "fsdp")
    nz = mesh.shape["fsdp"] // NY

    def layer_body(x_in, dy_in, norm_gain, w_qkv, w_out, w_gate, w_up, w_down, rope_cos, rope_sin):
        bf16 = jnp.bfloat16
        _, rows, width = x_in.shape
        slab = w_qkv.shape[0]
        head = 2 * rope_cos.shape[1]
        group = w_out.shape[0] // head
        seq = rows * NX * NC
        ff = w_gate.shape[1] // NY
        y = lax.rem(lax.axis_index("fsdp"), NY)
        c = lax.rem(lax.axis_index("model"), NC)
        last = y == NY - 1

        x_rows = x_in[0].astype(jnp.float32)
        normed, norm_pull = jax.vjp(lambda row_vals: norm_fwd(row_vals, norm_gain), x_rows)
        h_loc = normed.astype(bf16).reshape(2, rows // 2, width)
        dy_loc = dy_in.reshape(2, rows // 2, width)
        q, k, v = w_qkv[:, : group * head], w_qkv[:, group * head : -head], w_qkv[:, -head:]
        out_t, down_t = w_out.T, w_down.T
        parts = []
        for i in range(NY):
            at = slice(i * head, (i + 1) * head)
            ffs = slice(i * ff, (i + 1) * ff)
            heads = [q[:, at], out_t[:, at]] if i < NY - 1 else [k, v]
            parts.append(jnp.concatenate(heads + [w_gate[:, ffs], w_up[:, ffs], down_t[:, ffs]], axis=1))
        w_loc = jnp.stack(parts)

        h_all, dy_all, w_all = gather(nz, h_loc, dy_loc, w_loc)
        tokens = NY * seq
        h_all = h_all.reshape(tokens, width)
        dy_all = dy_all.reshape(tokens, width)
        w_all = w_all.reshape(NC, nz * NY * slab, w_loc.shape[2])
        w_own, w_pair = w_all[0], w_all[1]
        s0, s1, s2, s3, s4 = head, 2 * head, 2 * head + ff, 2 * head + 2 * ff, 2 * head + 3 * ff

        z_h = mm(h_all, w_own[:, :s1], 1, 0)
        z_d = mm(dy_all, w_own[:, s0:s1], 1, 0)
        heads_in = jnp.concatenate([z_h[:, :s0], jnp.where(last, z_h[:, s0:], z_d)], axis=1).astype(bf16)
        gate_val = mm(h_all, w_own[:, s1:s2], 1, 0).astype(bf16)
        up_val = mm(h_all, w_own[:, s2:s3], 1, 0).astype(bf16)
        d_act = mm(dy_all, w_own[:, s3:s4], 1, 0).astype(bf16)
        act_val, act_pull = jax.vjp(swiglu, gate_val, up_val)
        d_gate, d_up = act_pull(d_act)
        acts = jnp.concatenate([d_gate, d_up, act_val], axis=1)

        got = first_exchange(nz, heads_in.reshape(NY, 2, seq // 2, s1)).reshape(NY, seq, s1)
        heads = jnp.concatenate([got[:group, :, :s0], got[group:, :, :s0], got[group:, :, s0:]], axis=0)
        attn_val, attn_pull = jax.vjp(lambda packed: attention(packed, rope_cos, rope_sin), heads)
        d_heads = attn_pull(got[:group, :, s0:])[0]
        back = jnp.concatenate(
            [jnp.concatenate([d_heads[:group], d_heads[group : group + 1]], axis=0), jnp.concatenate([attn_val, d_heads[group + 1 :]], axis=0)], axis=2
        )
        heads_out, pair_heads, pair_acts = second_exchange(
            nz, back.reshape(NY, 2, NX // 2, NC, rows, s1), acts.reshape(NY, NX, NC, rows, 3 * ff)
        )
        heads_out = heads_out.reshape(NY * NX, NC, rows, s1)

        def mine(array):
            return lax.dynamic_index_in_dim(array, c, 1, keepdims=False).reshape(tokens // NC, -1)

        own_heads = mine(heads_out)
        own_acts = mine(acts.reshape(NY * NX, NC, rows, 3 * ff))
        pair_heads = pair_heads.reshape(tokens // NC, s1)
        pair_acts = pair_acts.reshape(tokens // NC, 3 * ff)
        zero = jnp.zeros((), bf16)

        def for_y(heads_val, acts_val):
            return [jnp.where(last, zero, heads_val[:, s0:]), acts_val[:, 2 * ff :]]

        def for_d(heads_val, acts_val):
            return [heads_val[:, :s0], jnp.where(last, heads_val[:, s0:], zero), acts_val[:, : 2 * ff]]

        y_part = mm(
            jnp.concatenate(for_y(own_heads, own_acts) + for_y(pair_heads, pair_acts), axis=1),
            jnp.concatenate([w_own[:, s0:s1], w_own[:, s3:], w_pair[:, s0:s1], w_pair[:, s3:]], axis=1),
            1,
            1,
        )
        d_part = mm(
            jnp.concatenate(for_d(own_heads, own_acts) + for_d(pair_heads, pair_acts), axis=1),
            jnp.concatenate([w_own[:, :s3], w_pair[:, :s3]], axis=1),
            1,
            1,
        )
        heads_out = heads_out.reshape(tokens, s1)
        g_h = mm(h_all, jnp.concatenate([heads_out, acts[:, : 2 * ff]], axis=1), 0, 0)
        g_d = mm(dy_all, jnp.concatenate([heads_out[:, s0:], acts[:, 2 * ff :]], axis=1), 0, 0)
        g_part = jnp.concatenate([g_h[:, :s0], jnp.where(last, g_h[:, s0:s1], g_d[:, :s0]), g_h[:, s1:], g_d[:, s0:]], axis=1)

        half = (NY, NX, 2, rows // 2, width)
        y_sum, d_sum, g_sum = scatter(nz, y_part.reshape(half), d_part.reshape(half), g_part.reshape(nz, NY, 2, slab // 2, s4))
        y_sum = y_sum.reshape(rows, width)
        d_sum = d_sum.reshape(rows, width)
        g_sum = g_sum.reshape(NY, slab, s4)

        y_out = (x_rows + y_sum).astype(bf16)
        d_h = d_sum.astype(bf16)
        dx_out = (dy_in[0].astype(jnp.float32) + norm_pull(d_h.astype(jnp.float32))[0]).astype(bf16)

        def cols(lo, hi, n=NY):
            return jnp.concatenate([g_sum[i, :, lo:hi] for i in range(n)], axis=1)

        return (
            y_out[None],
            dx_out[None],
            jnp.concatenate([cols(0, s0), g_sum[NY - 1, :, s0:s1]], axis=1),
            cols(s0, s1, group).T,
            cols(s1, s2),
            cols(s2, s3),
            cols(s3, s4).T,
        )

    return jax.shard_map(
        layer_body,
        mesh=mesh,
        in_specs=(act_spec, act_spec, P(), col_spec, row_spec, col_spec, col_spec, row_spec, P(), P()),
        out_specs=(act_spec, act_spec, col_spec, row_spec, col_spec, col_spec, row_spec),
        check_vma=False,
    )
```

time: 1810 us -> 467 us (0.26)
  waiting for transfers between devices: 1650 us -> 0 us
  Pallas kernels: 0 us -> 279 us
  local copies, waits for them, and re-layouts: 13.1 us -> 59.8 us
    reduce_scatter x7 -> x0, waiting for transfers between devices: 1210 us -> none  [the longest x1 241 us: layer_body(): lax.psum_scatter(dw_up, 'fsdp', scatter_dimension=0, tiled=True)]
    all_gather x7 -> x0, waiting for transfers between devices: 440 us -> none  [the longest x1 79.6 us: layer_body(): full_down = lax.all_gather(w_down, 'fsdp', axis=1, tiled=True)]
    pallas_call x0 -> x4, Pallas kernels: none -> 279 us  [the longest x1 152 us: scatter(): pl.pallas_call(functools.partial(scatter_kernel, nz, depth), out_shape=(j...]
    slice x2 -> x17, local copies, waits for them, and re-layouts: 0.04 us -> 23.6 us  [the longest x1 8.8 us: layer_body(): w_own, w_pair = (w_all[0], w_all[1])]
    concatenate x0 -> x7, local copies, waits for them, and re-layouts: none -> 20.2 us  [the longest x1 12.8 us: layer_body(): jnp.concatenate([g_h[:, :s0], jnp.where(last, g_h[:, s0:s1], g_d[:, :s0])...]
    dot_general x21 -> x14, matrix products: 107 us -> 102 us  [the longest x9 96 us: mm(): lax.dot_general(a, b, (((ca,), (cb,)), ((), ())), preferred_element_type=...]
  transfers between devices with their start and end apart: 14 -> 0, of which waited for: 13 -> 0; matrix products, arithmetic and copies ran while one was open for 6% -> 0% of each run, Pallas kernels for 0% -> 0%
where the time goes in v1:
time: 467 us; the launch traced here: 463 us
  Pallas kernels  279 us (60%)
  matrix products  105 us (22%)
  local copies, waits for them, and re-layouts  59.8 us (13%)
  other arithmetic  17.5 us (4%)
    pallas_call x1, Pallas kernels, scatter(): pl.pallas_call(functools.partial(scatter_kernel, nz, depth), out_shape=(j...  152 us
    dot_general x9, matrix products, mm(): lax.dot_general(a, b, (((ca,), (cb,)), ((), ())), preferred_element_type=...  96 us
    pallas_call x1, Pallas kernels, gather(): pl.pallas_call(functools.partial(gather_kernel, nz), out_shape=(jax.Shape...  91.7 us
    pallas_call x1, Pallas kernels, second_exchange(): pl.pallas_call(functools.partial(second_exchange_kernel, nz), out_shape=(...  19.6 us
    pallas_call x1, Pallas kernels, first_exchange(): pl.pallas_call(functools.partial(first_exchange_kernel, nz), out_shape=ja...  15.7 us
    concatenate x1, local copies, waits for them, and re-layouts, layer_body(): jnp.concatenate([g_h[:, :s0], jnp.where(last, g_h[:, s0:s1], g_d[:, :s0])...  12.8 us
    unnamed x65, local copies, waits for them, and re-layouts  10.8 us

profile of v1, /device:TPU:1, one launch (start us, length us, event | category | flops | bytes accessed | tf_op | source)
XLA Modules:
  0.0 463.1 jit_solution(4484243794920395582)
XLA Ops:
  0.7 0.8 constant_dynamic-update-slice_fusion.4
  2.3 0.9 constant_dynamic-update-slice_fusion.2
  3.2 0.9 constant_dynamic-update-slice_fusion.1
  4.1 0.9 constant_dynamic-update-slice_fusion
  5.0 0.8 slice.258
  5.8 1.0 pad_maximum_fusion.3.w_ref
  7.6 0.9 multiply_convert_fusion.h_ref
  8.5 91.7 %gather.1 = (bf16[4,4,2,2,32,3072]{5,4,3,2,1,0:T(8,128)(2,1)}, bf16[4,4,2,2,32,3072]{5,4,3,2,1,0:T(8,128)(2,1)}, bf16[2,8,4,96,1024]{4,3,2,1,0:T(8,128)(2,1)}) custom-call(bf16[2,32,3072]{2,1,0:T(8,128)(2,1)} %multiply_convert_fusion.h_ref, bf16[2,32,3072]{2,1,0:T(8,128)(2,1)} %bitcast.198, bf16[4,96,1024]{2,1,0:T(8,128)(2,1)} %pad_maximum_fusion.3.w_ref), custom_call_target="tpu_custom_call" | custom-call | tf_op jit(solution)/shard_map/gather/pallas_call | solution.py:190
  100.3 8.8 %fusion.88 = (bf16[1,8,4,96,1024]{4,3,2,1,0:T(8,128)(2,1)S(1)}, bf16[1,8,4,96,1024]{4,3,2,1,0:T(8,128)(2,1)}) fusion(bf16[2,8,4,96,1024]{4,3,2,1,0:T(8,128)(2,1)} %get-tuple-element.17), kind=kLoop, calls=%fused_computation.193 | loop fusion | bytes 25165824 | tf_op jit(solution)/shard_map/slice | solution.py:610
  109.1 11.4 %convolution_convert_fusion.2 = bf16[2048,256]{0,1:T(8,128)(2,1)} fusion(bf16[2048,3072]{1,0:T(8,128)(2,1)} %bitcast.208, bf16[3072,1024]{1,0:T(8,128)(2,1)S(1)} %bitcast.162), kind=kOutput, calls=%fused_computation.41 | convolution fusion | flops 3221749760 | bytes 15204352 | tf_op jit(solution)/shard_map/dot_general | solution.py:570
  120.4 9.1 %convolution_convert_fusion.1 = bf16[2048,256]{0,1:T(8,128)(2,1)} fusion(bf16[2048,3072]{1,0:T(8,128)(2,1)} %bitcast.211, bf16[3072,1024]{1,0:T(8,128)(2,1)S(1)} %bitcast.163), kind=kOutput, calls=%fused_computation.40 | convolution fusion | flops 3221749760 | bytes 15204352 | tf_op jit(solution)/shard_map/dot_general | solution.py:570
  129.5 11.4 %fusion.34 = (bf16[2048,256]{0,1:T(8,128)(2,1)}, bf16[2048,256]{0,1:T(8,128)(2,1)}, bf16[2048,256]{0,1:T(8,128)(2,1)}) fusion(bf16[2048,256]{0,1:T(8,128)(2,1)} %convolution_convert_fusion.1, bf16[2048,256]{0,1:T(8,128)(2,1)} %convolution_convert_fusion.2, bf16[2048,3072]{1,0:T(8,128)(2,1)} %bitcast.212, bf16[3072,1024]{1,0:T(8,128)(2,1)S(1)} %bitcast.164), kind=kOutput, calls=%fused_computation.52 | convolution fusion | flops 3231711232 | bytes 19398656 | tf_op jit(solution)/shard_map/dot_general | solution.py:570
  140.9 2.2 pad_maximum_fusion.1
  143.1 2.8 copy.83
  145.9 8.4 %fusion.37 = bf16[2048,256]{1,0:T(8,128)(2,1)S(1)} fusion(bf16[2048,3072]{1,0:T(8,128)(2,1)} %bitcast.213, bf16[3072,1024]{1,0:T(8,128)(2,1)} %bitcast.165), kind=kOutput, calls=%fused_computation.57 | convolution fusion | flops 3221225472 | bytes 15204352 | tf_op jit(solution)/shard_map/dot_general | solution.py:570
  154.4 8.1 %fusion.26 = bf16[2048,128]{1,0:T(8,128)(2,1)S(1)} fusion(bf16[2048,3072]{1,0:T(8,128)(2,1)} %bitcast.209, bf16[2048,256]{1,0:T(8,128)(2,1)S(1)} %fusion.37, pred[]{:T(512)S(6)} %eq.3, bf16[3072,1024]{1,0:T(8,128)(2,1)} %bitcast.166), kind=kOutput, calls=%fused_computation.44 | convolution fusion | flops 1610874880 | bytes 14417921 | tf_op jit(solution)/shard_map/dot_general | solution.py:570
  162.6 1.1 pad_maximum_fusion.2.src
  163.7 15.7 %exchange_in.1 = bf16[4,2,256,256]{3,2,1,0:T(8,128)(2,1)} custom-call(bf16[4,2,256,256]{3,2,1,0:T(8,128)(2,1)} %pad_maximum_fusion.2.src), custom_call_target="tpu_custom_call" | custom-call | tf_op jit(solution)/shard_map/exchange_in/pallas_call | solution.py:240
  179.4 1.1 slice.329
  181.3 2.9 fusion.90
  184.3 2.8 divide_convert_fusion
  187.7 1.1 fusion.55
  188.9 1.0 fusion.53
  190.8 1.7 copy.82
  192.5 19.6 %exchange_out.1 = (bf16[4,2,2,2,64,256]{5,4,3,2,1,0:T(8,128)(2,1)}, bf16[4,2,2,64,256]{4,3,2,1,0:T(8,128)(2,1)}, bf16[4,4,64,768]{3,2,1,0:T(8,128)(2,1)}) custom-call(bf16[4,2,2,2,64,256]{5,4,3,2,1,0:T(8,128)(2,1)} %bitcast.183, bf16[4,4,2,64,768]{4,3,2,1,0:T(8,128)(2,1)} %bitcast.170), custom_call_target="tpu_custom_call" | custom-call | tf_op jit(solution)/shard_map/exchange_out/pallas_call | solution.py:281
  212.1 1.5 copy.85
  213.7 12.5 %fusion.19 = f32[3072,768]{0,1:T(8,128)S(1)} fusion(bf16[2048,3072]{1,0:T(8,128)(2,1)} %bitcast.214, bf16[2048,256]{0,1:T(8,128)(2,1)S(1)} %copy-done.12, bf16[2048,256]{0,1:T(8,128)(2,1)S(1)} %copy-done.11, bf16[2048,256]{0,1:T(8,128)(2,1)S(1)} %copy.85), kind=kOutput, calls=%fused_computation.23 | convolution fusion | flops 9673113600 | bytes 25165824 | tf_op jit(solution)/shard_map/dot_general | solution.py:570
  226.3 11.4 %fusion.46 = f32[3072,384]{0,1:T(8,128)S(1)} fusion(bf16[2048,3072]{1,0:T(8,128)(2,1)} %bitcast.210, bf16[2048,256]{0,1:T(8,128)(2,1)S(1)} %copy-done.10, bf16[2048,128]{0,1:T(8,128)(2,1)S(1)} %slice.354), kind=kOutput, calls=%fused_computation.66 | convolution fusion | flops 4834983936 | bytes 18874368 | tf_op jit(solution)/shard_map/dot_general | solution.py:570
  238.3 2.6 slice-done.2
  240.9 5.3 %pad_maximum_fusion = f32[3072,1024]{0,1:T(8,128)} fusion(f32[3072,256]{0,1:T(8,128)S(1)} %slice.357, f32[3072,512]{0,1:T(8,128)S(1)} %slice-done.2, f32[3072,128]{0,1:T(8,128)S(1)} %get-tuple-element.28, f32[3072,128]{0,1:T(8,128)S(1)} %get-tuple-element.27), kind=kLoop, calls=%fused_computation.1 | loop fusion | flops 9437184 | bytes 25165824 | tf_op jit(solution)/shard_map/concatenate | solution.py:665
  246.2 12.8 %copy.87 = f32[3072,1024]{1,0:T(8,128)} copy(f32[3072,1024]{0,1:T(8,128)} %pad_maximum_fusion) | data formatting | bytes 25165824 | tf_op jit(solution)/shard_map/concatenate | solution.py:665
  259.0 1.1 constant_dynamic-slice_fusion.1
  260.8 0.8 select_dynamic-update-slice_fusion.1
  261.7 1.2 slice_dynamic-update-slice_fusion.1
  263.7 0.9 select_dynamic-update-slice_fusion
  264.6 1.1 slice_dynamic-update-slice_fusion
  265.7 3.2 slice.350
  269.4 2.7 slice.351
  272.1 15.5 %fusion.1 = f32[1024,3072]{1,0:T(8,128)} fusion(bf16[1024,1536]{1,0:T(8,128)(2,1)} %slice_dynamic-update-slice_fusion, bf16[3072,768]{1,0:T(8,128)(2,1)} %slice.351, bf16[3072,768]{1,0:T(8,128)(2,1)S(1)} %slice.350), kind=kOutput, calls=%fused_computation.2 | convolution fusion | flops 9682550784 | bytes 25165824 | tf_op jit(solution)/shard_map/dot_general | solution.py:570
  287.6 1.1 slice.343
  288.7 1.5 slice.337
  290.4 1.2 slice.328
  291.8 8.1 %fusion.5 = f32[1024,3072]{1,0:T(8,128)} fusion(bf16[3072,256]{1,0:T(8,128)(2,1)S(1)} %slice.345, bf16[3072,128]{1,0:T(8,128)(2,1)S(1)} %slice.344, bf16[3072,256]{1,0:T(8,128)(2,1)S(1)} %slice.337, bf16[3072,128]{1,0:T(8,128)(2,1)S(1)} %slice.328, bf16[1024,256]{1,0:T(8,128)(2,1)S(1)} %slice.343, bf16[1024,128]{1,0:T(8,128)(2,1)S(1)} %get-tuple-element.54, ...), kind=kOutput, calls=%fused_computation.6 | convolution fusion | flops 4857004032 | bytes 18874368 | tf_op jit(solution)/shard_map/dot_general | solution.py:570
  300.0 152.4 %scatter.1 = (f32[2,32,3072]{2,1,0:T(8,128)}, f32[2,32,3072]{2,1,0:T(8,128)}, f32[4,2,48,1024]{3,2,1,0:T(8,128)}) custom-call(f32[4,4,2,32,3072]{4,3,2,1,0:T(8,128)} %bitcast.173, f32[4,4,2,32,3072]{4,3,2,1,0:T(8,128)} %bitcast.172, f32[8,4,2,48,1024]{4,3,2,1,0:T(8,128)} %bitcast.156), custom_call_target="tpu_custom_call" | custom-call | tf_op jit(solution)/shard_map/scatter/pallas_call | solution.py:516
  452.4 1.6 slice_bitcast_fusion.6
  454.8 1.0 pad_maximum_fusion.5
  455.8 0.9 slice_bitcast_fusion.17
  461.7 1.2 fusion.59
  (99 shorter events, 12.9 us)
Async XLA Ops:
  0.6 6.2 %copy-start.3 = (bf16[1,64,3072]{2,1,0:T(8,128)(2,1)S(1)}, bf16[1,64,3072]{2,1,0:T(8,128)(2,1)}, u32[]{:S(2)}) copy-start(bf16[1,64,3072]{2,1,0:T(8,128)(2,1)} %param.10) | copy-start | bytes 1179652
  0.6 7.0 %copy-start.16 = (f32[3072]{0:T(1024)S(1)}, f32[3072]{0:T(1024)}, u32[]{:S(2)}) copy-start(f32[3072]{0:T(1024)} %param.12) | copy-start | bytes 36868
  7.0 0.5 copy-start.21
  7.5 92.7 %copy-start.19 = (f32[64]{0:T(128)}, f32[64]{0:T(128)S(1)}, u32[]{:S(2)}) copy-start(f32[64]{0:T(128)S(1)} %fusion.71) | copy-start | bytes 772
  109.1 20.4 %copy-start = (bf16[1,8,4,96,1024]{4,3,2,1,0:T(8,128)(2,1)}, bf16[1,8,4,96,1024]{4,3,2,1,0:T(8,128)(2,1)S(1)}, u32[]{:S(2)}) copy-start(bf16[1,8,4,96,1024]{4,3,2,1,0:T(8,128)(2,1)S(1)} %get-tuple-element.25) | copy-start | bytes 18874372
  162.6 18.2 %copy-start.6 = (f32[512,64]{0,1:T(8,128)S(1)}, f32[512,64]{0,1:T(8,128)}, u32[]{:S(2)}) copy-start(f32[512,64]{0,1:T(8,128)} %param.19) | copy-start | bytes 393220
  162.6 18.2 %copy-start.7 = (f32[512,64]{0,1:T(8,128)S(1)}, f32[512,64]{0,1:T(8,128)}, u32[]{:S(2)}) copy-start(f32[512,64]{0,1:T(8,128)} %param.18) | copy-start | bytes 393220
  179.4 1.6 copy-start.5
  184.3 3.4 copy-start.23
  192.5 21.1 %copy-start.11 = (bf16[2048,256]{0,1:T(8,128)(2,1)S(1)}, bf16[2048,256]{0,1:T(8,128)(2,1)}, u32[]{:S(2)}) copy-start(bf16[2048,256]{0,1:T(8,128)(2,1)} %get-tuple-element.31) | copy-start | bytes 3145732
  192.5 21.1 %copy-start.12 = (bf16[2048,256]{0,1:T(8,128)(2,1)S(1)}, bf16[2048,256]{0,1:T(8,128)(2,1)}, u32[]{:S(2)}) copy-start(bf16[2048,256]{0,1:T(8,128)(2,1)} %get-tuple-element.33) | copy-start | bytes 3145732
  213.6 12.6 %copy-start.10 = (bf16[2048,256]{0,1:T(8,128)(2,1)S(1)}, bf16[2048,256]{0,1:T(8,128)(2,1)}, u32[]{:S(2)}) copy-start(bf16[2048,256]{0,1:T(8,128)(2,1)} %get-tuple-element.32) | copy-start | bytes 3145732
  226.2 11.9 %copy-start.1 = (f32[3072,768]{0,1:T(8,128)}, f32[3072,768]{0,1:T(8,128)S(1)}, u32[]{:S(2)}) copy-start(f32[3072,768]{0,1:T(8,128)S(1)} %fusion.19) | copy-start | bytes 28311556
  238.1 2.8 slice-start.2
  246.2 15.4 %copy-start.2 = (bf16[2048,768]{1,0:T(8,128)(2,1)S(1)}, bf16[2048,768]{1,0:T(8,128)(2,1)}, u32[]{:S(2)}) copy-start(bf16[2048,768]{1,0:T(8,128)(2,1)} %copy.83) | copy-start | bytes 9437188
  260.8 2.1 copy-start.15
  261.6 3.0 copy-start.8
  264.6 4.3 slice-start
  265.7 3.7 slice-start.1
  452.4 9.0 %copy-start.13 = (f32[2,32,3072]{2,1,0:T(8,128)S(1)}, f32[2,32,3072]{2,1,0:T(8,128)}, u32[]{:S(2)}) copy-start(f32[2,32,3072]{2,1,0:T(8,128)} %get-tuple-element.23) | copy-start | bytes 2359300
  452.4 9.0 %copy-start.4 = (bf16[1,64,3072]{2,1,0:T(8,128)(2,1)S(1)}, bf16[1,64,3072]{2,1,0:T(8,128)(2,1)}, u32[]{:S(2)}) copy-start(bf16[1,64,3072]{2,1,0:T(8,128)(2,1)} %param.10) | copy-start | bytes 1179652
  452.4 9.0 %copy-start.17 = (f32[3072]{0:T(1024)S(1)}, f32[3072]{0:T(1024)}, u32[]{:S(2)}) copy-start(f32[3072]{0:T(1024)} %param.12) | copy-start | bytes 36868
  454.0 7.6 %copy-start.22 = (f32[64]{0:T(128)S(1)}, f32[64]{0:T(128)}, u32[]{:S(2)}) copy-start(f32[64]{0:T(128)} %copy-done.21) | copy-start | bytes 772
  454.0 7.7 %copy-start.9 = (bf16[1,64,3072]{2,1,0:T(8,128)(2,1)S(1)}, bf16[1,64,3072]{2,1,0:T(8,128)(2,1)}, u32[]{:S(2)}) copy-start(bf16[1,64,3072]{2,1,0:T(8,128)(2,1)} %param.11) | copy-start | bytes 1179652
  454.0 7.7 %copy-start.14 = (f32[2,32,3072]{2,1,0:T(8,128)S(1)}, f32[2,32,3072]{2,1,0:T(8,128)}, u32[]{:S(2)}) copy-start(f32[2,32,3072]{2,1,0:T(8,128)} %get-tuple-element.22) | copy-start | bytes 2359300
  454.0 7.7 %copy-start.20 = (f32[64]{0:T(128)S(1)}, f32[64]{0:T(128)}, u32[]{:S(2)}) copy-start(f32[64]{0:T(128)} %copy-done.19) | copy-start | bytes 772
  461.4 1.5 copy-start.18

commit v2 on v0

v2 whole, which is shorter than its diff:
```python
import functools
import heapq

import jax
import jax.numpy as jnp
from jax import lax
from jax.experimental import pallas as pl
from jax.experimental.pallas import tpu as pltpu
from jax.sharding import PartitionSpec as P

NORM_EPS = 1e-5
NY, NX, NC = 4, 4, 2
MESH = pl.DeviceIdType.MESH
LINK = 46.6e3
PAIR = 330e3
LOCAL = 1500e3
HOP = 3.5
ADD = 0.4
VMEM_LIMIT = 67043328


class Place:
    def __init__(self, nz):
        i, j = lax.axis_index("fsdp"), lax.axis_index("model")
        self.size = {"z": nz, "y": NY, "x": NX, "c": NC}
        self.at = {"z": lax.div(i, NY), "y": lax.rem(i, NY), "x": lax.div(j, NC), "c": lax.rem(j, NC)}

    def get(self, axis, step=0):
        n = self.size[axis]
        return lax.rem(self.at[axis] + (step + 2 * n) % n, n)

    def device(self, axis, step):
        at = dict(self.at)
        at[axis] = self.get(axis, step)
        return {"fsdp": at["z"] * NY + at["y"], "model": at["x"] * NC + at["c"]}

    def meet(self, peers):
        barrier = pltpu.get_barrier_semaphore()
        for axis, step in peers:
            pl.semaphore_signal(barrier, inc=1, device_id=self.device(axis, step), device_id_type=MESH)
        pl.semaphore_wait(barrier, len(peers))


class Flow:
    def __init__(self, place, send_sem, recv_sem, base=0, now=0.0):
        self.place, self.send_sem, self.recv_sem, self.base = place, send_sem, recv_sem, base
        self.now, self.free, self.events, self.copies, self.tasks, self.order = now, {}, [], [], [], 0
        self.sent = set()

    def event(self, when, wait, then):
        heapq.heappush(self.events, (when, self.order, wait, then))
        self.order += 1

    def send(self, axis, step, src, dst, size, then=None, link=None):
        k = len(self.copies)
        link = link or (axis, step)
        begin = max(self.now, self.free.get(link, 0.0))
        rate, lag = (PAIR, 1.5) if axis == "c" else (LINK, HOP)
        self.free[link] = begin + size / rate
        copy = pltpu.make_async_remote_copy(
            src_ref=src(),
            dst_ref=dst(),
            send_sem=self.send_sem.at[self.base + k],
            recv_sem=self.recv_sem.at[self.base + k],
            device_id=self.place.device(axis, step),
            device_id_type=MESH,
        )
        copy.start()
        self.copies.append(copy)
        self.event(self.free[link] + lag, copy.wait_recv, then)
        return k

    def local(self, copy, size, then):
        copy.start()
        self.event(self.now + size / LOCAL + 1.0, copy.wait, then)

    def task(self, cost, do):
        self.tasks.append((cost, do))

    def take(self):
        when, _, wait, then = heapq.heappop(self.events)
        self.now = max(self.now, when)
        wait()
        if then is not None:
            then()

    def spend(self, cost):
        self.now += cost
        while self.events and self.events[0][0] <= self.now:
            self.take()

    def wait_sent(self, k):
        if k not in self.sent:
            self.copies[k].wait_send()
        self.sent.add(k)

    def run(self):
        while self.events or self.tasks:
            if self.tasks and (not self.events or self.events[0][0] > self.now):
                cost, do = self.tasks.pop(0)
                do()
                self.now += cost
            else:
                self.take()

    def close(self):
        for k in range(len(self.copies)):
            self.wait_sent(k)


def after(count, then):
    left = [count]

    def one():
        left[0] -= 1
        if left[0] == 0:
            then()

    return one


def nbytes(ref, lead):
    n = 1
    for d in ref.shape[lead:]:
        n *= d
    return n * jnp.dtype(ref.dtype).itemsize


def gather_kernel(nz, h_ref, dy_ref, w_ref, h_all, dy_all, w_all, send_sem, recv_sem, own_sem):
    place = Place(nz)
    y, x, c, z = place.get("y"), place.get("x"), place.get("c"), place.get("z")
    place.meet([("x", 1), ("x", -1), ("y", 1), ("y", -1), ("y", 2), ("z", 1), ("z", -1), ("c", 1)])
    flow = Flow(place, send_sem, recv_sem)
    own = [
        pltpu.make_async_copy(h_ref, h_all.at[y, x, c], own_sem.at[0]),
        pltpu.make_async_copy(dy_ref, dy_all.at[y, x, c], own_sem.at[1]),
        pltpu.make_async_copy(w_ref.at[y], w_all.at[0, z, y], own_sem.at[2]),
    ]
    for copy in own:
        copy.start()
    piece = nbytes(h_ref, 1)

    def spot(ref, dy, dx, half):
        return lambda: ref.at[place.get("y", dy), place.get("x", dx), c, half]

    def spread(axis, half, offset, src, got):
        def come(step, onward):
            def then():
                if onward:
                    flow.send(axis, -step, got.spot(axis, step, offset, half), got.spot(axis, step, offset, half), piece, lambda: got(axis, 2, offset, half))
                got(axis, step, offset, half)

            return then

        flow.send(axis, 1, src, got.spot(axis, 0, offset, half), piece, come(-1, half == 0))
        flow.send(axis, -1, src, got.spot(axis, 0, offset, half), piece, come(1, half == 1))

    class Got:
        def __init__(self, ref, first):
            self.ref, self.first, self.second = ref, first, "y" if first == "x" else "x"

        def spot(self, axis, step, offset, half):
            d = {axis: step, ("y" if axis == "x" else "x"): offset}
            return spot(self.ref, d["y"], d["x"], half)

        def __call__(self, axis, step, offset, half):
            here = self.spot(axis, step, offset, half)
            if axis == self.first:
                spread(self.second, half, step, here, self)
            flow.send("c", 1, here, here, piece)

    size = nbytes(w_ref, 1)

    def w_spot(who, dz, dy):
        return lambda: w_all.at[who, place.get("z", dz), place.get("y", dy)]

    def ring(step, dy, src=None):
        def hop(n):
            def then():
                here = src if src and n == 0 else w_spot(0, -step * n, dy)
                if n < nz - 1:
                    flow.send("z", step, here, w_spot(0, -step * n, dy), size, hop(n + 1))
                flow.send("c", 1, here, w_spot(1, -step * n, dy), size)

            return then

        return hop(0)

    def w_at(dy):
        return lambda: w_ref.at[place.get("y", dy)]

    flow.send("y", -1, w_at(-1), w_spot(0, 0, 0), size, ring(1, 1))
    flow.send("y", 1, w_at(1), w_spot(0, 0, 0), size, ring(-1, -1))
    flow.send("y", 2, w_at(2), w_spot(0, 0, 0), size, ring(-1, 2), link=("y", 1))
    ring(1, 0, w_at(0))()
    arrays = [(h_ref, Got(h_all, "x")), (dy_ref, Got(dy_all, "y"))]
    for ref, got in arrays:
        for half in (0, 1):
            spread(got.first, half, 0, lambda ref=ref, half=half: ref.at[half], got)
    for ref, got in arrays:
        for half in (0, 1):
            src = lambda ref=ref, half=half: ref.at[half]
            spread(got.second, half, 0, src, got)
            flow.send("c", 1, src, got.spot(got.second, 0, 0, half), piece)
    flow.run()
    flow.close()
    for copy in own:
        copy.wait()


def any_specs(n):
    return [pl.BlockSpec(memory_space=pl.ANY)] * n


def gather(nz, h, dy, w):
    half, rows, width = h.shape
    everywhere = (NY, NX, NC) + h.shape
    count = 60 + 64 + 3 + 4 * (nz - 1) + 4 * nz
    vmem = pl.BlockSpec(memory_space=pltpu.VMEM)
    return pl.pallas_call(
        functools.partial(gather_kernel, nz),
        out_shape=(
            jax.ShapeDtypeStruct(everywhere, h.dtype),
            jax.ShapeDtypeStruct(everywhere, dy.dtype),
            jax.ShapeDtypeStruct((NC, nz) + w.shape, w.dtype),
        ),
        in_specs=[vmem] * 3,
        out_specs=tuple(any_specs(3)),
        scratch_shapes=[pltpu.SemaphoreType.DMA((count,)), pltpu.SemaphoreType.DMA((count,)), pltpu.SemaphoreType.DMA((3,))],
        compiler_params=pltpu.CompilerParams(collective_id=0, has_side_effects=True),
        name="gather",
    )(h, dy, w)


def mm(a, b, ca, cb):
    return lax.dot_general(a, b, (((ca,), (cb,)), ((), ())), preferred_element_type=jnp.float32)


def span(q, n):
    return pl.ds(pl.multiple_of(q * n, n), n)


def exchange(flow, place, src, dst, far, step, done=None):
    size = nbytes(src, 1)

    def onward(way, half):
        def then():
            flow.send("y", way, lambda: far.at[half], lambda: dst.at[place.get("y", -way), half], size // 2, done)

        return then

    if step == 2:
        flow.send("y", 1, lambda: src.at[place.get("y", 2), 0], lambda: far.at[0], size // 2, onward(1, 0))
        flow.send("y", -1, lambda: src.at[place.get("y", 2), 1], lambda: far.at[1], size // 2, onward(-1, 1))
    else:
        flow.send("y", step, lambda: src.at[place.get("y", step)], lambda: dst.at[place.get("y")], size, done)


ORDER = (2, 1, -1, 0)


def heads_kernel(nz, h_all, dy_all, w_all, z_got, h_v, dy_v, w_v, z_in, far, load_sem, own_sem, send_sem, recv_sem):
    bf16 = jnp.bfloat16
    place = Place(nz)
    y = place.get("y")
    last = y == NY - 1
    pair = z_in.shape[-1]
    head = pair // 2
    seq = h_v.shape[1]
    part = seq // 2
    lo = (w_all.shape[2] - pair) * 2 // 3
    w_load = pltpu.make_async_copy(w_all.at[0, :, lo : lo + pair], w_v, load_sem.at[0])
    w_load.start()
    loads = []
    for n, step in enumerate(ORDER):
        at = span(place.get("y", step), seq)
        loads.append([pltpu.make_async_copy(a.at[at], b.at[n], load_sem.at[1 + 2 * n + m]) for m, (a, b) in enumerate(((h_all, h_v), (dy_all, dy_v)))])
        for copy in loads[n]:
            copy.start()
    place.meet([("y", 1), ("y", -1)])
    flow = Flow(place, send_sem, recv_sem)
    w_load.wait()
    for n, step in enumerate(ORDER):
        for copy in loads[n]:
            copy.wait()
        q = place.get("y", step)

        @pl.loop(0, 2)
        def _(p):
            at = span(p, part)
            from_h = mm(h_v[n, at, :], w_v[...], 1, 0)
            from_dy = mm(dy_v[n, at, :], w_v[:, head:], 1, 0)
            z_in[q, p, :, :head] = from_h[:, :head].astype(bf16)
            z_in[q, p, :, head:] = jnp.where(last, from_h[:, head:], from_dy).astype(bf16)

        flow.spend(2.3)
        if step:
            exchange(flow, place, z_in, z_got, far, step)
    own = pltpu.make_async_copy(z_in.at[y], z_got.at[y], own_sem)
    own.start()
    flow.run()
    flow.close()
    own.wait()


def head_rows(nz, pair, seq, h_all, dy_all, w_all):
    tokens, width = h_all.shape
    bf16 = h_all.dtype
    dma = pltpu.SemaphoreType.DMA
    halves = (NY, 2, seq // 2, pair)
    return pl.pallas_call(
        functools.partial(heads_kernel, nz),
        out_shape=jax.ShapeDtypeStruct(halves, bf16),
        in_specs=any_specs(3),
        out_specs=pl.BlockSpec(memory_space=pl.ANY),
        scratch_shapes=[
            pltpu.VMEM((NY, seq, width), bf16),
            pltpu.VMEM((NY, seq, width), bf16),
            pltpu.VMEM((width, pair), bf16),
            pltpu.VMEM(halves, bf16),
            pltpu.VMEM(halves[1:], bf16),
            dma((1 + 2 * NY,)),
            dma,
            dma((6,)),
            dma((6,)),
        ],
        compiler_params=pltpu.CompilerParams(collective_id=1, has_side_effects=True, vmem_limit_bytes=VMEM_LIMIT),
        name="heads",
    )(h_all, dy_all, w_all)


SETS = (2, 1, -1, 0)


def attention(z_got, z_back, keys, vals, dk, dv, cos_ref, sin_ref):
    bf16 = jnp.bfloat16
    seq, head = keys.shape
    part = seq // 2
    count = z_got.shape[0] - 1
    scale = head**-0.5
    spread = z_back.shape[2:5] + (head,)
    halves = [pl.ds(p * part, part) for p in range(2)]

    def turn(values, at, sign):
        wide = values.astype(jnp.float32)
        swapped = pltpu.roll(wide, head // 2, 1)
        return (wide * cos_ref[at, :] + sign * (swapped * sin_ref[at, :])).astype(bf16)

    for p in range(2):
        keys[halves[p], :] = turn(z_got[count, p, :, :head], halves[p], 1.0)
        vals[halves[p], :] = z_got[count, p, :, head:]
    dk[...] = jnp.zeros_like(dk)
    dv[...] = jnp.zeros_like(dv)

    @pl.loop(0, count)
    def _(i):
        for p in range(2):
            n = (p + 1) * part
            query = turn(z_got[i, p, :, :head], halves[p], 1.0)
            d_out = z_got[i, p, :, head:]
            scores = mm(query, keys[:n, :], 1, 1) * scale
            causal = lax.broadcasted_iota(jnp.int32, scores.shape, 0) + p * part >= lax.broadcasted_iota(jnp.int32, scores.shape, 1)
            scores = jnp.where(causal, scores, -1e30)
            grown = jnp.exp(scores - jnp.max(scores, axis=1, keepdims=True))
            probs = grown / jnp.sum(grown, axis=1, keepdims=True)
            probs_low = probs.astype(bf16)
            z_back[i, p, :, :, :, head:] = mm(probs_low, vals[:n, :], 1, 0).astype(bf16).reshape(spread)
            d_probs = mm(d_out, vals[:n, :], 1, 1).astype(bf16).astype(jnp.float32)
            d_scores = (probs * (d_probs - jnp.sum(probs * d_probs, axis=1, keepdims=True)) * scale).astype(bf16)
            z_back[i, p, :, :, :, :head] = turn(mm(d_scores, keys[:n, :], 1, 0).astype(bf16), halves[p], -1.0).reshape(spread)
            dk[:n, :] += mm(d_scores, query, 0, 0)
            dv[:n, :] += mm(probs_low, d_out, 0, 0)

    for p in range(2):
        z_back[count, p, :, :, :, :head] = turn(dk[halves[p], :].astype(bf16), halves[p], -1.0).reshape(spread)
        z_back[count, p, :, :, :, head:] = dv[halves[p], :].astype(bf16).reshape(spread)


def gated(place, flow, h_all, dy_all, w_all, acts, row_sem, share, h_rows, dy_rows, w_v):
    bf16 = jnp.bfloat16
    ff = acts.shape[-1] // 3
    lo = 2 * ff
    part = h_rows.shape[1]
    shape = acts.shape[2:5] + (ff,)
    w_loads = [
        pltpu.make_async_copy(w_all.at[0, :, :lo], w_v.at[:, :lo], row_sem.at[2, 0]),
        pltpu.make_async_copy(w_all.at[0, :, w_all.shape[2] - ff :], w_v.at[:, lo:], row_sem.at[2, 1]),
    ]

    def loads(n, slot):
        return [pltpu.make_async_copy(a.at[span(n, part)], b.at[slot], row_sem.at[slot, m]) for m, (a, b) in enumerate(((h_all, h_rows), (dy_all, dy_rows)))]

    def begin():
        for copy in w_loads + loads(0, 0) + loads(1, 1):
            copy.start()

    def go():
        for copy in w_loads:
            copy.wait()
        for q in range(NY):

            @pl.loop(0, 2)
            def _(p):
                n = 2 * q + p
                for copy in loads(n, p):
                    copy.wait()
                gate = mm(h_rows[p], w_v[:, :ff], 1, 0).astype(bf16).astype(jnp.float32)
                up = mm(h_rows[p], w_v[:, ff:lo], 1, 0).astype(bf16).astype(jnp.float32)
                d_act = mm(dy_rows[p], w_v[:, lo:], 1, 0).astype(bf16).astype(jnp.float32)
                if q < NY - 1:
                    for copy in loads(n + 2, p):
                        copy.start()
                sig = jax.nn.sigmoid(gate)
                silu = gate * sig
                acts[q, p, :, :, :, :ff] = (d_act * up * (sig + silu * (1.0 - sig))).astype(bf16).reshape(shape)
                acts[q, p, :, :, :, ff:lo] = (d_act * silu).astype(bf16).reshape(shape)
                acts[q, p, :, :, :, lo:] = (silu * up).astype(bf16).reshape(shape)

            share(q)
            flow.spend(3.0)

    return begin, go


class Plane:
    def __init__(self, place, flow, tiles, land, first, finish, free):
        self.place, self.flow, self.tiles, self.land, self.first = place, flow, tiles, land, first
        self.second = "y" if first == "x" else "x"
        self.piece = nbytes(tiles, 3)
        self.sums, self.waiting, self.finished = {}, {}, [0] * len(SETS)
        self.free = free
        self.rings = []
        for s, other in enumerate(SETS):

            def raw(step, half, s=s):
                return lambda: tiles.at[s % 2, place.get(first, step), half]

            self.rings.append(self.ring(first, raw, lambda step, half, then: then(), s, self.first_done(s, other)))
        self.onward, _ = self.ring(self.second, lambda step, half: self.sums[step, half], self.need, len(SETS), finish)

    def need(self, step, half, then):
        if (step, half) in self.sums:
            then()
        else:
            self.waiting.setdefault((step, half), []).append(then)

    def first_done(self, s, step):
        def done(half, ref):
            self.sums[step, half] = ref
            for then in self.waiting.pop((step, half), []):
                then()
            self.onward(step, half)
            self.finished[s] += 1
            if self.finished[s] == 2:
                self.free(s)

        return done

    def add(self, mine, other):
        a, b = mine(), other()
        a[...] = a[...] + b[...]
        self.flow.now += ADD

    def ring(self, axis, raw, need, s, done):
        flow, add, sent = self.flow, self.add, []

        def slot(i):
            return lambda: self.land.at[s, i]

        def turn(i, goal, half, step):
            def then():
                add(slot(i), raw(goal, half))
                flow.send(axis, step, slot(i), slot(i + 4), self.piece, final[half])

            return lambda: need(goal, half, then)

        def ending(half):
            def then():
                mine, other = (slot(5), slot(2)) if half == 0 else (slot(4), slot(3))
                add(mine, other)
                add(mine, raw(0, half))
                done(half, mine)

            return lambda: need(0, half, then)

        final = [after(2, ending(0)), after(2, ending(1))]
        moves = {
            (2, 1): (1, 0, turn(0, 1, 1, 1)),
            (2, 0): (-1, 1, turn(1, -1, 0, -1)),
            (1, 0): (1, 2, final[0]),
            (-1, 1): (-1, 3, final[1]),
        }

        def start(goal, half):
            if (goal, half) in moves:
                step, i, then = moves[goal, half]
                sent.append(flow.send(axis, step, raw(goal, half), slot(i), self.piece, then))

        return start, sent

    def start(self, s):
        for goal, half in ((2, 1), (2, 0), (1, 0), (-1, 1)):
            self.rings[s][0](goal, half)

    def clear(self, s):
        for k in self.rings[s][1]:
            self.flow.wait_sent(k)


class Grads:
    def __init__(self, nz, place, flow, h_all, dy_all, acts, z_out, z_land, g_sum, far, h_plus, h_minus, dy_minus, tiles, stage, load_sem, stage_sem, own_sem):
        self.__dict__.update({k: v for k, v in locals().items() if k != "self"})
        self.ff = acts.shape[-1] // 3
        self.pair = z_out.shape[-1]
        lo = 2 * self.ff
        self.cols = [(0, self.ff), (self.ff, lo), (lo + self.pair, lo + self.pair + self.ff), (lo, lo + self.pair)]
        self.way = (1, 1, -1, -1)
        self.far_way = (1, -1, 1, -1)
        self.block = tiles.shape[2]
        self.size = nbytes(tiles, 2)
        self.ready, self.waiting, self.used = set(), {}, 0
        self.users = [[] for _ in range(stage.shape[0])]
        self.own = []
        self.idle, self.first = {}, {}

    def load(self, ref, src, index, step, n):
        b = self.place.get("z", -step * (n + 1))
        at = pl.ds(pl.multiple_of(b * self.block, self.block), self.block)
        return pltpu.make_async_copy(src.at[:, at], ref, self.load_sem.at[index])

    def loads_plus(self, n):
        return [self.load(self.h_plus, self.h_all, 0, 1, n)]

    def loads_minus(self, n):
        return [self.load(self.h_minus, self.h_all, 1, -1, n), self.load(self.dy_minus, self.dy_all, 2, -1, n)]

    def begin(self):
        for copy in self.loads_plus(0) + self.loads_minus(0):
            copy.start()

    def set_ready(self, lane, n):
        self.ready.add((lane, n))
        for then in self.waiting.pop((lane, n), []):
            then()
        if n == 0:
            k = self.flow.send("z", self.way[lane], lambda: self.tiles.at[0, lane], lambda: self.z_land.at[0, lane], self.size, self.hop(lane, 0))
            self.first[lane] = k

    def clear(self, lane, n):
        if n == 2:
            self.flow.wait_sent(self.first[lane])

    def tokens(self, ref):
        value = ref[...]
        return value.reshape(-1, value.shape[-1])

    def plus(self, n):
        def do():
            for lane in (0, 1):
                self.clear(lane, n)
            for copy in self.loads_plus(n):
                copy.wait()
            lo = 2 * self.ff
            act = self.acts[:, :, :, :, :, :lo].reshape(-1, lo)
            both = mm(self.h_plus[...], act, 0, 0)
            self.tiles[n % 2, 0] = both[:, : self.ff]
            self.tiles[n % 2, 1] = both[:, self.ff :]
            if n + 1 < self.nz:
                for copy in self.loads_plus(n + 1):
                    copy.start()
            self.set_ready(0, n)
            self.set_ready(1, n)

        self.flow.task(1.4, do)

    def minus(self, n):
        def do():
            for lane in (2, 3):
                self.clear(lane, n)
            for copy in self.loads_minus(n):
                copy.wait()
            last = self.place.get("y") == NY - 1
            head = self.pair // 2
            act = self.acts[:, :, :, :, :, 2 * self.ff :].reshape(-1, self.ff)
            self.tiles[n % 2, 2] = mm(self.dy_minus[...], act, 0, 0)
            out = self.tokens(self.z_out)
            tile = self.tiles.at[n % 2, 3]

            @pl.when(last)
            def _():
                tile[...] = mm(self.h_minus[...], out, 0, 0)

            @pl.when(jnp.logical_not(last))
            def _():
                tile[:, :head] = mm(self.h_minus[...], out[:, :head], 0, 0)
                tile[:, head:] = mm(self.dy_minus[...], out[:, head:], 0, 0)

            if n + 1 < self.nz:
                for copy in self.loads_minus(n + 1):
                    copy.start()
            self.set_ready(2, n)
            self.set_ready(3, n)

        self.flow.task(2.1, do)

    def need(self, lane, n, then):
        if (lane, n) in self.ready:
            then()
        else:
            self.waiting.setdefault((lane, n), []).append(then)

    def next(self, lane, n):
        if n + 2 >= self.nz:
            return
        key = (lane // 2, n)
        self.idle[key] = self.idle.get(key, 0) + 1
        if self.idle[key] == 2:
            (self.plus, self.minus)[lane // 2](n + 2)

    def hop(self, lane, s):
        flow, place = self.flow, self.place

        def come():
            slot = self.used % len(self.users)
            self.used += 1
            for wait in self.users[slot]:
                wait()
            self.users[slot] = []
            here = lambda: self.stage.at[slot]

            def staged():
                self.need(lane, s + 1, use)

            def use():
                ref = here()
                ref[...] = ref[...] + self.tiles[(s + 1) % 2, lane]
                flow.now += ADD
                if s == 0:
                    self.next(lane, 0)
                self.next(lane, s + 1)
                if s + 1 < self.nz - 1:
                    k = flow.send("z", self.way[lane], here, lambda: self.z_land.at[s + 1, lane], self.size, self.hop(lane, s + 1))
                    self.users[slot].append(lambda: flow.wait_sent(k))
                else:
                    self.home(lane, slot)

            flow.local(pltpu.make_async_copy(self.z_land.at[s, lane], here(), self.stage_sem.at[slot]), self.size, staged)

        return come

    def home(self, lane, slot):
        flow, place = self.flow, self.place
        slab = self.block // NY
        first, end = self.cols[lane]

        def rows(step):
            return lambda: self.stage.at[slot, pl.ds(pl.multiple_of(place.get("y", step) * slab, slab), slab)]

        def mine(step=0):
            return lambda: self.g_sum.at[place.get("y", step), :, first:end]

        size = self.size // NY
        way = self.far_way[lane]

        def onward():
            flow.send("y", way, lambda: self.far.at[lane], mine(-way), size)

        sent = [flow.send("y", way, rows(2), lambda: self.far.at[lane], size, onward)]
        sent += [flow.send("y", step, rows(step), mine(), size) for step in (1, -1)]
        copy = pltpu.make_async_copy(rows(0)(), mine()(), self.own_sem.at[lane])
        copy.start()
        self.users[slot] += [functools.partial(flow.wait_sent, k) for k in sent] + [copy.wait]

    def close(self):
        for users in self.users:
            for wait in users:
                wait()


def back_kernel(
    nz,
    z_in,
    h_all,
    dy_all,
    w_all,
    cos_ref,
    sin_ref,
    p_sum,
    q_sum,
    g_sum,
    z_land,
    z_got,
    z_back,
    z_out,
    far_back,
    acts,
    pair_acts,
    far,
    p_land,
    q_land,
    keys,
    vals,
    dk,
    dv,
    load_sem,
    row_sem,
    w_sem,
    g_load_sem,
    stage_sem,
    own_sem,
    send_sem,
    recv_sem,
):
    bf16, f32 = jnp.bfloat16, jnp.float32
    place = Place(nz)
    y, c = place.get("y"), place.get("c")
    other = place.get("c", 1)
    last = y == NY - 1
    seq, head = keys.shape
    pair = 2 * head
    rows, cols = pair_acts.shape[3:]
    ff = (cols - pair) // 3
    lo, hi = 2 * ff, 2 * ff + pair
    tokens, width = h_all.shape
    block = width // nz
    part = seq // 2

    z_load = pltpu.make_async_copy(z_in, z_got, load_sem)
    z_load.start()
    early = Flow(place, send_sem, recv_sem)
    peers = [("x", 1), ("x", -1), ("y", 1), ("y", -1), ("z", 1), ("z", -1), ("c", 1)]

    def share(q):
        early.send("c", 1, lambda: acts.at[q, :, :, other, :, :lo], lambda: pair_acts.at[q, :, :, :, :lo], nbytes(pair_acts, 1) * lo // cols)
        early.send("c", 1, lambda: acts.at[q, :, :, other, :, lo:], lambda: pair_acts.at[q, :, :, :, hi:], nbytes(pair_acts, 1) * ff // cols)

    def all_out():
        early.send("c", 1, lambda: z_out.at[:, :, :, other], lambda: pair_acts.at[:, :, :, :, lo:hi], nbytes(z_out, 0) // NC)

    def first(h_rows, dy_rows, w_v):
        begin, go = gated(place, early, h_all, dy_all, w_all, acts, row_sem, share, h_rows, dy_rows, w_v)
        begin()
        z_load.wait()
        attention(z_got, z_back, keys, vals, dk, dv, cos_ref, sin_ref)
        place.meet(peers)
        out_done = after(4, all_out)
        for step in ORDER[:3]:
            exchange(early, place, z_back, z_out, far_back, step, out_done)
        z_out[y] = z_back[y]
        go()
        early.run()
        early.close()

    pl.run_scoped(
        first,
        pltpu.VMEM((2, part, width), bf16),
        pltpu.VMEM((2, part, width), bf16),
        pltpu.VMEM((width, 3 * ff), bf16),
    )

    def second(p_tile, q_tile, w_v, h_plus, h_minus, dy_minus, tiles, stage):
        flow = Flow(place, send_sem, recv_sem, len(early.copies), early.now)
        grads = Grads(nz, place, flow, h_all, dy_all, acts, z_out, z_land, g_sum, far, h_plus, h_minus, dy_minus, tiles, stage, g_load_sem, stage_sem, own_sem)
        grads.begin()
        lane = lax.broadcasted_iota(jnp.int32, (rows, pair), 1)
        for_d = jnp.logical_or(lane < head, last)

        def chunk(k, i, p, xx):
            if k == 0:
                own = acts[i, p, xx, c]
                return own[:, :lo], z_out[i, p, xx, c], own[:, lo:]
            theirs = pair_acts[i, p, xx]
            return theirs[:, :lo], theirs[:, lo:hi], theirs[:, hi:]

        def for_out(k, i, p, xx):
            _, mixed, act = chunk(k, i, p, xx)
            return jnp.concatenate([jnp.where(for_d, jnp.zeros_like(mixed), mixed), act], axis=1)

        def for_in(k, i, p, xx):
            grad, mixed, _ = chunk(k, i, p, xx)
            return jnp.concatenate([grad, jnp.where(for_d, mixed, jnp.zeros_like(mixed))], axis=1)

        def over(first, count, a, b, body):
            def copy(d, slot):
                at = pl.ds(pl.multiple_of(d * block, block), block)
                return pltpu.make_async_copy(w_all.at[:, at, a:b], w_v.at[slot, :, :, a:b], w_sem.at[slot])

            for n in range(min(2, count)):
                copy(first + n, n).start()

            @pl.loop(0, count)
            def _(n):
                slot = lax.rem(n, 2)
                copy(first + n, slot).wait()
                body(first + n, w_v.at[slot])

                @pl.when(n + 2 < count)
                def _():
                    copy(first + n + 2, slot).start()

        def product(parts, w, a, b):
            total = None
            for k in range(NC):
                left = jnp.concatenate([one(k) for one in parts], axis=0)
                one = mm(left, w[k, :, a:b], 1, 1)
                total = one if total is None else total + one
            return total

        shape = (NX, 2, rows // 2, block)

        def p_rows(s):
            x = place.get("x", SETS[s])
            p, xx = lax.div(x, NX // 2), lax.rem(x, NX // 2)
            return [lambda k, i=i: for_out(k, i, p, xx) for i in range(NY)]

        def q_rows(s, make):
            i = place.get("y", SETS[s])
            return [lambda k, p=p, xx=xx: make(k, i, p, xx) for p in range(2) for xx in range(NX // 2)]

        def p_task(s):
            def do():
                if s >= 2:
                    planes[0].clear(s - 2)

                def body(d, w):
                    p_tile[s % 2, :, :, :, pl.ds(pl.multiple_of(d * block, block), block)] = product(p_rows(s), w, lo, cols).reshape(shape)

                over(0, nz - 1, lo, cols, body)
                planes[0].start(s)

            flow.task(2.8, do)

        def q_task(s):
            def do():
                if s >= 2:
                    planes[1].clear(s - 2)

                def edge(d, w):
                    q_tile[s % 2, :, :, :, width:] = product(q_rows(s, for_out), w, lo, cols).reshape(shape)

                def body(d, w):
                    q_tile[s % 2, :, :, :, pl.ds(pl.multiple_of(d * block, block), block)] = product(q_rows(s, for_in), w, 0, hi).reshape(shape)

                over(nz - 1, 1, lo, cols, edge)
                over(0, nz, 0, hi, body)
                planes[1].start(s)

            flow.task(5.5, do)

        def finish(out):
            def done(half, ref):
                out[half] = ref()[...]

            return done

        def free(task):
            return lambda s: task(s + 2) if s + 2 < len(SETS) else None

        planes = [
            Plane(place, flow, p_tile, p_land, "y", finish(p_sum), free(p_task)),
            Plane(place, flow, q_tile, q_land, "x", finish(q_sum), free(q_task)),
        ]

        grads.plus(0)
        grads.minus(0)
        p_task(0)
        q_task(0)
        grads.plus(1)
        grads.minus(1)
        p_task(1)
        q_task(1)
        flow.run()
        flow.close()
        grads.close()

    g_piece = (block, ff)
    pl.run_scoped(
        second,
        pltpu.VMEM((2, NY, 2, rows // 2, width - block), f32),
        pltpu.VMEM((2, NX, 2, rows // 2, width + block), f32),
        pltpu.VMEM((2, NC, block, cols), bf16),
        pltpu.VMEM((tokens, block), bf16),
        pltpu.VMEM((tokens, block), bf16),
        pltpu.VMEM((tokens, block), bf16),
        pltpu.VMEM((2, 4) + g_piece, f32),
        pltpu.VMEM((STAGES,) + g_piece, f32),
    )


STAGES = 6


def back(nz, z_in, h_all, dy_all, w_all, cos, sin):
    tokens, width = h_all.shape
    seq, head = cos.shape
    pair = 2 * head
    cols = w_all.shape[2]
    ff = (cols - pair) // 3
    rows = seq // (NX * NC)
    block = width // nz
    bf16, f32 = h_all.dtype, jnp.float32
    vmem = pl.BlockSpec(memory_space=pltpu.VMEM)
    dma = pltpu.SemaphoreType.DMA
    blocks = (NY, 2, NX // 2, NC, rows, pair)
    p_piece = (rows // 2, width - block)
    q_piece = (rows // 2, width + block)
    count = 6 + 2 * NY + 1 + 4 * (nz - 1) + 4 * 4 + 2 * 5 * 6
    return pl.pallas_call(
        functools.partial(back_kernel, nz),
        out_shape=(
            jax.ShapeDtypeStruct((2,) + p_piece, f32),
            jax.ShapeDtypeStruct((2,) + q_piece, f32),
            jax.ShapeDtypeStruct((NY, block // NY, cols), f32),
            jax.ShapeDtypeStruct((nz - 1, 4, block, ff), f32),
        ),
        in_specs=any_specs(4) + [vmem, vmem],
        out_specs=(vmem, vmem) + tuple(any_specs(2)),
        scratch_shapes=[
            pltpu.VMEM(z_in.shape, bf16),
            pltpu.VMEM(blocks, bf16),
            pltpu.VMEM(blocks, bf16),
            pltpu.VMEM(blocks[1:], bf16),
            pltpu.VMEM(blocks[:-1] + (3 * ff,), bf16),
            pltpu.VMEM(blocks[:3] + (rows, cols), bf16),
            pltpu.VMEM((4, block // NY, ff), f32),
            pltpu.VMEM((5, 6) + p_piece, f32),
            pltpu.VMEM((5, 6) + q_piece, f32),
            pltpu.VMEM((seq, head), bf16),
            pltpu.VMEM((seq, head), bf16),
            pltpu.VMEM((seq, head), f32),
            pltpu.VMEM((seq, head), f32),
            dma,
            dma((3, 2)),
            dma((2,)),
            dma((3,)),
            dma((STAGES,)),
            dma((4,)),
            dma((count,)),
            dma((count,)),
        ],
        compiler_params=pltpu.CompilerParams(collective_id=2, has_side_effects=True, vmem_limit_bytes=VMEM_LIMIT),
        name="back",
    )(z_in, h_all, dy_all, w_all, cos, sin)[:3]


def norm_fwd(row_vals, norm_gain):
    return row_vals * lax.rsqrt(jnp.mean(row_vals * row_vals, axis=-1, keepdims=True) + NORM_EPS) * norm_gain


def solution(mesh):
    act_spec = P("fsdp", "model", None)
    col_spec = P("fsdp", "model")
    row_spec = P("model", "fsdp")
    nz = mesh.shape["fsdp"] // NY

    def layer_body(x_in, dy_in, norm_gain, w_qkv, w_out, w_gate, w_up, w_down, rope_cos, rope_sin):
        bf16 = jnp.bfloat16
        _, rows, width = x_in.shape
        slab = w_qkv.shape[0]
        head = 2 * rope_cos.shape[1]
        group = w_out.shape[0] // head
        seq = rows * NX * NC
        ff = w_gate.shape[1] // NY

        x_rows = x_in[0].astype(jnp.float32)
        normed, norm_pull = jax.vjp(lambda row_vals: norm_fwd(row_vals, norm_gain), x_rows)
        h_loc = normed.astype(bf16).reshape(2, rows // 2, width)
        dy_loc = dy_in.reshape(2, rows // 2, width)
        q, k, v = w_qkv[:, : group * head], w_qkv[:, group * head : -head], w_qkv[:, -head:]
        out_t, down_t = w_out.T, w_down.T
        parts = []
        for i in range(NY):
            at = slice(i * head, (i + 1) * head)
            ffs = slice(i * ff, (i + 1) * ff)
            heads = [q[:, at], out_t[:, at]] if i < NY - 1 else [k, v]
            parts.append(jnp.concatenate([w_gate[:, ffs], w_up[:, ffs]] + heads + [down_t[:, ffs]], axis=1))
        w_loc = jnp.stack(parts)
        cos = jnp.concatenate([rope_cos, rope_cos], axis=1)
        sin = jnp.concatenate([-rope_sin, rope_sin], axis=1)

        h_all, dy_all, w_all = gather(nz, h_loc, dy_loc, w_loc)
        tokens = NY * seq
        cols = w_loc.shape[2]
        h_all = h_all.reshape(tokens, width)
        dy_all = dy_all.reshape(tokens, width)
        w_all = w_all.reshape(NC, width, cols)
        z_got = head_rows(nz, 2 * head, seq, h_all, dy_all, w_all)
        p_sum, q_sum, g_sum = back(nz, z_got, h_all, dy_all, w_all, cos, sin)
        p_sum = p_sum.reshape(rows, -1)
        q_sum = q_sum.reshape(rows, -1)

        y_sum = jnp.concatenate([p_sum, q_sum[:, width:]], axis=1)
        y_out = (x_rows + y_sum).astype(bf16)
        d_h = q_sum[:, :width].astype(bf16)
        dx_out = (dy_in[0].astype(jnp.float32) + norm_pull(d_h.astype(jnp.float32))[0]).astype(bf16)
        lo = 2 * ff
        mid = lo + head
        hi = mid + head

        def take(first, end, n=NY):
            return jnp.concatenate([g_sum[i, :, first:end] for i in range(n)], axis=1)

        return (
            y_out[None],
            dx_out[None],
            jnp.concatenate([take(lo, mid), g_sum[NY - 1, :, mid:hi]], axis=1),
            take(mid, hi, group).T,
            take(0, ff),
            take(ff, lo),
            take(hi, cols).T,
        )

    return jax.shard_map(
        layer_body,
        mesh=mesh,
        in_specs=(act_spec, act_spec, P(), col_spec, row_spec, col_spec, col_spec, row_spec, P(), P()),
        out_specs=(act_spec, act_spec, col_spec, row_spec, col_spec, col_spec, row_spec),
        check_vma=False,
    )
```

time: 1810 us -> 330 us (0.18)
  waiting for transfers between devices: 1650 us -> 0 us
  Pallas kernels: 0 us -> 307 us
  matrix products: 107 us -> 0 us
    reduce_scatter x7 -> x0, waiting for transfers between devices: 1210 us -> none  [the longest x1 241 us: layer_body(): lax.psum_scatter(dw_up, 'fsdp', scatter_dimension=0, tiled=True)]
    all_gather x7 -> x0, waiting for transfers between devices: 440 us -> none  [the longest x1 79.6 us: layer_body(): full_down = lax.all_gather(w_down, 'fsdp', axis=1, tiled=True)]
    pallas_call x0 -> x3, Pallas kernels: none -> 307 us  [the longest x1 199 us: back(): pl.pallas_call(functools.partial(back_kernel, nz), out_shape=(jax.ShapeDt...]
    dot_general x21 -> x0, matrix products: 107 us -> none  [the longest x1 8.62 us: layer_body(): jnp.einsum('bsd,bsf->df', h_full, d_gate, preferred_element_type=jnp.floa...]
  transfers between devices with their start and end apart: 14 -> 0, of which waited for: 13 -> 0; matrix products, arithmetic and copies ran while one was open for 6% -> 0% of each run, Pallas kernels for 0% -> 0%
where the time goes in v2:
time: 330 us; the launch traced here: 324 us
  Pallas kernels  307 us (93%)
  other arithmetic  13.7 us (4%)
    pallas_call x1, Pallas kernels, back(): pl.pallas_call(functools.partial(back_kernel, nz), out_shape=(jax.ShapeDt...  199 us
    pallas_call x1, Pallas kernels, gather(): pl.pallas_call(functools.partial(gather_kernel, nz), out_shape=(jax.Shape...  88.3 us
    pallas_call x1, Pallas kernels, head_rows(): pl.pallas_call(functools.partial(heads_kernel, nz), out_shape=jax.ShapeDt...  19.2 us

profile of v2, /device:TPU:1, one launch (start us, length us, event | category | flops | bytes accessed | tf_op | source)
XLA Modules:
  0.0 324.4 jit_solution(10919072617592215014)
XLA Ops:
  0.6 0.0 copy-start.4
  0.6 0.0 copy-start
  0.7 0.0 copy-start.9
  0.7 1.2 fusion.3
  1.9 0.0 copy-start.13
  1.9 0.0 copy-start.12
  1.9 0.1 rsqrt.15
  2.0 0.9 neg.3
  2.9 0.0 copy-start.6
  2.9 0.1 copy.23
  3.1 0.0 copy-done.13
  3.1 0.0 copy-done.12
  3.1 0.0 copy-start.7
  3.1 1.1 copy.21
  4.2 0.0 copy-done.4
  4.2 0.0 copy-start.5
  4.2 0.1 copy.24
  4.3 0.0 copy-start.10
  4.3 0.0 copy-start.8
  4.4 0.0 slice-start
  4.4 1.0 pad_maximum_fusion.3
  5.4 0.0 copy-done
  5.4 0.0 copy-done.9
  5.4 0.9 multiply_convert_fusion.h_ref
  6.3 0.0 copy-done.6
  6.3 0.0 copy-done.7
  6.3 0.0 copy-done.5
  6.4 0.0 copy-done.10
  6.4 0.0 copy-done.8
  6.5 0.0 slice-done
  6.5 1.0 pad_maximum_fusion.w_ref
  7.5 88.3 %gather.1 = (bf16[4,4,2,2,32,3072]{5,4,3,2,1,0:T(8,128)(2,1)}, bf16[4,4,2,2,32,3072]{5,4,3,2,1,0:T(8,128)(2,1)}, bf16[2,8,4,96,1024]{4,3,2,1,0:T(8,128)(2,1)}) custom-call(bf16[2,32,3072]{2,1,0:T(8,128)(2,1)} %multiply_convert_fusion.h_ref, bf16[2,32,3072]{2,1,0:T(8,128)(2,1)} %bitcast.85, bf16[4,96,1024]{2,1,0:T(8,128)(2,1)} %pad_maximum_fusion.w_ref), custom_call_target="tpu_custom_call" | custom-call | tf_op jit(solution)/shard_map/gather/pallas_call | solution.py:220
  95.8 19.2 %heads.1.z_in = bf16[4,2,256,256]{3,2,1,0:T(8,128)(2,1)} custom-call(bf16[2048,3072]{1,0:T(8,128)(2,1)} %bitcast.78, bf16[2048,3072]{1,0:T(8,128)(2,1)} %bitcast.80, bf16[2,3072,1024]{2,1,0:T(8,128)(2,1)} %bitcast.82), custom_call_target="tpu_custom_call" | custom-call | tf_op jit(solution)/shard_map/heads/pallas_call | solution.py:311
  115.0 199.4 %back.1 = (f32[2,32,2688]{2,1,0:T(8,128)}, f32[2,32,3456]{2,1,0:T(8,128)}, f32[4,96,1024]{2,1,0:T(8,128)}, f32[7,4,384,256]{3,2,1,0:T(8,128)}) custom-call(bf16[4,2,256,256]{3,2,1,0:T(8,128)(2,1)} %heads.1.z_in, bf16[2048,3072]{1,0:T(8,128)(2,1)} %bitcast.79, bf16[2048,3072]{1,0:T(8,128)(2,1)} %bitcast.81, bf16[2,3072,1024]{2,1,0:T(8,128)(2,1)} %bitcast.83, ...), custom_call_target="tpu_custom_call" | custom-call | tf_op jit(solution)/shard_map/back/pallas_call | solution.py:908
  314.4 0.0 copy-start.1
  314.4 0.0 copy-start.3
  314.4 1.6 fusion.4
  316.0 0.7 multiply_multiply_fusion
  316.7 0.9 slice_bitcast_fusion
  317.6 2.5 fusion.5
  320.1 0.0 copy-done.3
  320.1 0.8 fusion.2
  321.0 0.7 maximum_bitcast_fusion.2
  321.7 0.0 copy-start.11
  321.7 0.1 slice_bitcast_fusion.4
  321.9 0.8 maximum_bitcast_fusion
  322.6 0.8 pad_maximum_fusion.2
  323.4 0.8 pad_maximum_fusion.1
  (17 shorter events, 0.2 us)
Async XLA Ops:
  0.6 3.6 %copy-start.4 = (f32[512,64]{0,1:T(8,128)S(1)}, f32[512,64]{0,1:T(8,128)}, u32[]{:S(2)}) copy-start(f32[512,64]{0,1:T(8,128)} %param.19) | copy-start | bytes 393220
  0.6 4.7 %copy-start = (bf16[1,64,3072]{2,1,0:T(8,128)(2,1)S(1)}, bf16[1,64,3072]{2,1,0:T(8,128)(2,1)}, u32[]{:S(2)}) copy-start(bf16[1,64,3072]{2,1,0:T(8,128)(2,1)} %param.10) | copy-start | bytes 1179652
  0.7 4.7 %copy-start.9 = (f32[3072]{0:T(1024)S(1)}, f32[3072]{0:T(1024)}, u32[]{:S(2)}) copy-start(f32[3072]{0:T(1024)} %param.12) | copy-start | bytes 36868
  1.9 1.2 copy-start.13
  1.9 1.2 copy-start.12
  2.9 3.3 %copy-start.6 = (bf16[96,1024]{1,0:T(8,128)(2,1)S(1)}, bf16[96,1024]{1,0:T(8,128)(2,1)}, u32[]{:S(2)}) copy-start(bf16[96,1024]{1,0:T(8,128)(2,1)} %param.15) | copy-start | bytes 589828
  3.1 3.2 copy-start.7
  4.2 2.1 copy-start.5
  4.3 2.0 copy-start.10
  4.3 2.1 copy-start.8
  4.4 2.1 slice-start
  314.4 5.7 %copy-start.1 = (bf16[1,64,3072]{2,1,0:T(8,128)(2,1)S(1)}, bf16[1,64,3072]{2,1,0:T(8,128)(2,1)}, u32[]{:S(2)}) copy-start(bf16[1,64,3072]{2,1,0:T(8,128)(2,1)} %param.10) | copy-start | bytes 1179652
  314.4 5.7 %copy-start.3 = (f32[2,32,2688]{2,1,0:T(8,128)S(1)}, f32[2,32,2688]{2,1,0:T(8,128)}, u32[]{:S(2)}) copy-start(f32[2,32,2688]{2,1,0:T(8,128)} %get-tuple-element.16) | copy-start | bytes 2064388
  317.6 3.4 %copy-start.2 = (f32[4,96,1024]{2,1,0:T(8,128)S(1)}, f32[4,96,1024]{2,1,0:T(8,128)}, u32[]{:S(2)}) copy-start(f32[4,96,1024]{2,1,0:T(8,128)} %get-tuple-element.18) | copy-start | bytes 4718596
  321.7 0.9 copy-start.11

commit v3 on v2

--- a/solution.py
+++ b/solution.py
@@ -98,8 +98,8 @@
         while self.events or self.tasks:
             if self.tasks and (not self.events or self.events[0][0] > self.now):
                 cost, do = self.tasks.pop(0)
+                self.now += cost
                 do()
-                self.now += cost
             else:
                 self.take()
 
@@ -508,7 +508,10 @@
 
 
 class Grads:
-    def __init__(self, nz, place, flow, h_all, dy_all, acts, z_out, z_land, g_sum, far, h_plus, h_minus, dy_minus, tiles, stage, load_sem, stage_sem, own_sem):
+    flow = None
+
+
+    def __init__(self, nz, place, h_all, dy_all, acts, z_out, z_land, g_sum, far, h_plus, h_minus, dy_minus, tiles, stage, load_sem, stage_sem, own_sem):
         self.__dict__.update({k: v for k, v in locals().items() if k != "self"})
         self.ff = acts.shape[-1] // 3
         self.pair = z_out.shape[-1]
@@ -538,6 +541,16 @@
         for copy in self.loads_plus(0) + self.loads_minus(0):
             copy.start()
 
+    def gather_up(self, tiles, some):
+        seq = self.h_plus.shape[0] // NY
+        for tile, value in zip(tiles, some(0, pl.ds(0, seq))):
+            tile[...] = value
+
+        @pl.loop(1, NY)
+        def _(q):
+            for tile, value in zip(tiles, some(q, span(q, seq))):
+                tile[...] += value
+
     def set_ready(self, lane, n):
         self.ready.add((lane, n))
         for then in self.waiting.pop((lane, n), []):
@@ -554,54 +567,75 @@
         value = ref[...]
         return value.reshape(-1, value.shape[-1])
 
+    def make_plus(self, n):
+        for copy in self.loads_plus(n):
+            copy.wait()
+        lo = 2 * self.ff
+
+        def some(q, rows):
+            both = mm(self.h_plus[rows, :], self.acts[q, :, :, :, :, :lo].reshape(-1, lo), 0, 0)
+            return both[:, : self.ff], both[:, self.ff :]
+
+        self.gather_up([self.tiles.at[n % 2, 0], self.tiles.at[n % 2, 1]], some)
+        if n + 1 < self.nz:
+            for copy in self.loads_plus(n + 1):
+                copy.start()
+
+    def for_down(self, q, rows):
+        return [mm(self.dy_minus[rows, :], self.acts[q, :, :, :, :, 2 * self.ff :].reshape(-1, self.ff), 0, 0)]
+
+    def for_heads(self, q, rows):
+        last = self.place.get("y") == NY - 1
+        head = self.pair // 2
+        out = self.z_out[q].reshape(-1, self.pair)
+        both = mm(self.h_minus[rows, :], out, 0, 0)
+        right = jnp.where(last, both[:, head:], mm(self.dy_minus[rows, :], out[:, head:], 0, 0))
+        return [jnp.concatenate([both[:, :head], right], axis=1)]
+
+    def make_minus(self, n):
+        for copy in self.loads_minus(n):
+            copy.wait()
+        self.gather_up([self.tiles.at[n % 2, 2], self.tiles.at[n % 2, 3]], lambda q, rows: self.for_down(q, rows) + self.for_heads(q, rows))
+        self.load_minus_next(n)
+
+    def load_minus_next(self, n):
+        if n + 1 < self.nz:
+            for copy in self.loads_minus(n + 1):
+                copy.start()
+
+    def make_first(self):
+        self.make_plus(0)
+        for copy in self.loads_minus(0):
+            copy.wait()
+        self.gather_up([self.tiles.at[0, 2]], self.for_down)
+
+    def heads_first(self):
+        def do():
+            self.gather_up([self.tiles.at[0, 3]], self.for_heads)
+            self.load_minus_next(0)
+            self.set_ready(3, 0)
+
+        self.flow.task(1.3, do)
+
     def plus(self, n):
         def do():
             for lane in (0, 1):
                 self.clear(lane, n)
-            for copy in self.loads_plus(n):
-                copy.wait()
-            lo = 2 * self.ff
-            act = self.acts[:, :, :, :, :, :lo].reshape(-1, lo)
-            both = mm(self.h_plus[...], act, 0, 0)
-            self.tiles[n % 2, 0] = both[:, : self.ff]
-            self.tiles[n % 2, 1] = both[:, self.ff :]
-            if n + 1 < self.nz:
-                for copy in self.loads_plus(n + 1):
-                    copy.start()
-            self.set_ready(0, n)
-            self.set_ready(1, n)
-
-        self.flow.task(1.4, do)
+            self.make_plus(n)
+            for lane in (0, 1):
+                self.set_ready(lane, n)
+
+        self.flow.task(1.6, do)
 
     def minus(self, n):
         def do():
             for lane in (2, 3):
                 self.clear(lane, n)
-            for copy in self.loads_minus(n):
-                copy.wait()
-            last = self.place.get("y") == NY - 1
-            head = self.pair // 2
-            act = self.acts[:, :, :, :, :, 2 * self.ff :].reshape(-1, self.ff)
-            self.tiles[n % 2, 2] = mm(self.dy_minus[...], act, 0, 0)
-            out = self.tokens(self.z_out)
-            tile = self.tiles.at[n % 2, 3]
-
-            @pl.when(last)
-            def _():
-                tile[...] = mm(self.h_minus[...], out, 0, 0)
-
-            @pl.when(jnp.logical_not(last))
-            def _():
-                tile[:, :head] = mm(self.h_minus[...], out[:, :head], 0, 0)
-                tile[:, head:] = mm(self.dy_minus[...], out[:, head:], 0, 0)
-
-            if n + 1 < self.nz:
-                for copy in self.loads_minus(n + 1):
-                    copy.start()
-            self.set_ready(2, n)
-            self.set_ready(3, n)
-
-        self.flow.task(2.1, do)
+            self.make_minus(n)
+            for lane in (2, 3):
+                self.set_ready(lane, n)
+
+        self.flow.task(2.2, do)
 
     def need(self, lane, n, then):
         if (lane, n) in self.ready:
@@ -702,6 +736,11 @@
     vals,
     dk,
     dv,
+    h_plus,
+    h_minus,
+    dy_minus,
+    tiles,
+    stage,
     load_sem,
     row_sem,
     w_sem,
@@ -737,9 +776,12 @@
     def all_out():
         early.send("c", 1, lambda: z_out.at[:, :, :, other], lambda: pair_acts.at[:, :, :, :, lo:hi], nbytes(z_out, 0) // NC)
 
+    grads = Grads(nz, place, h_all, dy_all, acts, z_out, z_land, g_sum, far, h_plus, h_minus, dy_minus, tiles, stage, g_load_sem, stage_sem, own_sem)
+
     def first(h_rows, dy_rows, w_v):
         begin, go = gated(place, early, h_all, dy_all, w_all, acts, row_sem, share, h_rows, dy_rows, w_v)
         begin()
+        grads.begin()
         z_load.wait()
         attention(z_got, z_back, keys, vals, dk, dv, cos_ref, sin_ref)
         place.meet(peers)
@@ -748,6 +790,8 @@
             exchange(early, place, z_back, z_out, far_back, step, out_done)
         z_out[y] = z_back[y]
         go()
+        grads.make_first()
+        early.now += 2.6
         early.run()
         early.close()
 
@@ -758,10 +802,9 @@
         pltpu.VMEM((width, 3 * ff), bf16),
     )
 
-    def second(p_tile, q_tile, w_v, h_plus, h_minus, dy_minus, tiles, stage):
+    def second(p_tile, q_tile, w_v):
         flow = Flow(place, send_sem, recv_sem, len(early.copies), early.now)
-        grads = Grads(nz, place, flow, h_all, dy_all, acts, z_out, z_land, g_sum, far, h_plus, h_minus, dy_minus, tiles, stage, g_load_sem, stage_sem, own_sem)
-        grads.begin()
+        grads.flow = flow
         lane = lax.broadcasted_iota(jnp.int32, (rows, pair), 1)
         for_d = jnp.logical_or(lane < head, last)
 
@@ -780,23 +823,44 @@
             grad, mixed, _ = chunk(k, i, p, xx)
             return jnp.concatenate([grad, jnp.where(for_d, mixed, jnp.zeros_like(mixed))], axis=1)
 
-        def over(first, count, a, b, body):
-            def copy(d, slot):
-                at = pl.ds(pl.multiple_of(d * block, block), block)
-                return pltpu.make_async_copy(w_all.at[:, at, a:b], w_v.at[slot, :, :, a:b], w_sem.at[slot])
-
-            for n in range(min(2, count)):
-                copy(first + n, n).start()
-
-            @pl.loop(0, count)
-            def _(n):
-                slot = lax.rem(n, 2)
-                copy(first + n, slot).wait()
-                body(first + n, w_v.at[slot])
-
-                @pl.when(n + 2 < count)
+        depth = w_v.shape[0]
+
+        def w_copy(kind, d, slot):
+            at = pl.ds(pl.multiple_of(d * block, block), block)
+            cut = slice(lo, cols) if kind == 0 else slice(0, cols)
+            return pltpu.make_async_copy(w_all.at[:, at, cut], w_v.at[slot, :, :, cut], w_sem.at[slot])
+
+        counts = (nz - 1, nz)
+        base, total = [], 0
+        for kind, _ in PASSES:
+            base.append(total)
+            total += counts[kind]
+        kind = PASSES[0][0]
+        for n in range(depth):
+            w_copy(kind, n, n).start() if n < counts[kind] else w_copy(PASSES[1][0], n - counts[kind], n).start()
+        turn = [0]
+
+        def blocks(s, kind, first, count, body):
+            n = turn[0]
+            assert PASSES[n] == (kind, s)
+            if first + count == counts[kind]:
+                turn[0] += 1
+
+            @pl.loop(first, first + count)
+            def _(d):
+                slot = lax.rem(base[n] + d, depth)
+                w_copy(kind, d, slot).wait()
+                body(d, w_v.at[slot])
+
+                @pl.when(d + depth < counts[kind])
                 def _():
-                    copy(first + n + 2, slot).start()
+                    w_copy(kind, d + depth, slot).start()
+
+                if n + 1 < len(PASSES):
+
+                    @pl.when(d + depth >= counts[kind])
+                    def _():
+                        w_copy(PASSES[n + 1][0], d + depth - counts[kind], slot).start()
 
         def product(parts, w, a, b):
             total = None
@@ -817,35 +881,40 @@
             i = place.get("y", SETS[s])
             return [lambda k, p=p, xx=xx: make(k, i, p, xx) for p in range(2) for xx in range(NX // 2)]
 
+        def place_of(d):
+            return pl.ds(pl.multiple_of(d * block, block), block)
+
         def p_task(s):
+            def body(d, w):
+                p_tile[s % 2, :, :, :, place_of(d)] = product(p_rows(s), w, lo, cols).reshape(shape)
+
             def do():
                 if s >= 2:
                     planes[0].clear(s - 2)
-
-                def body(d, w):
-                    p_tile[s % 2, :, :, :, pl.ds(pl.multiple_of(d * block, block), block)] = product(p_rows(s), w, lo, cols).reshape(shape)
-
-                over(0, nz - 1, lo, cols, body)
+                blocks(s, 0, 0, nz - 1, body)
                 planes[0].start(s)
 
-            flow.task(2.8, do)
+            flow.task(P_TIME, do)
 
         def q_task(s):
-            def do():
+            def body(d, w):
+                q_tile[s % 2, :, :, :, place_of(d)] = product(q_rows(s, for_in), w, 0, hi).reshape(shape)
+
+                @pl.when(d == nz - 1)
+                def _():
+                    q_tile[s % 2, :, :, :, width:] = product(q_rows(s, for_out), w, lo, cols).reshape(shape)
+
+            def start():
                 if s >= 2:
                     planes[1].clear(s - 2)
-
-                def edge(d, w):
-                    q_tile[s % 2, :, :, :, width:] = product(q_rows(s, for_out), w, lo, cols).reshape(shape)
-
-                def body(d, w):
-                    q_tile[s % 2, :, :, :, pl.ds(pl.multiple_of(d * block, block), block)] = product(q_rows(s, for_in), w, 0, hi).reshape(shape)
-
-                over(nz - 1, 1, lo, cols, edge)
-                over(0, nz, 0, hi, body)
+                blocks(s, 1, 0, nz // 2, body)
+
+            def end():
+                blocks(s, 1, nz // 2, nz - nz // 2, body)
                 planes[1].start(s)
 
-            flow.task(5.5, do)
+            flow.task(Q_HALF, start)
+            flow.task(Q_HALF, end)
 
         def finish(out):
             def done(half, ref):
@@ -861,10 +930,11 @@
             Plane(place, flow, q_tile, q_land, "x", finish(q_sum), free(q_task)),
         ]
 
-        grads.plus(0)
-        grads.minus(0)
+        for lane in range(3):
+            grads.set_ready(lane, 0)
+        q_task(0)
         p_task(0)
-        q_task(0)
+        grads.heads_first()
         grads.plus(1)
         grads.minus(1)
         p_task(1)
@@ -873,21 +943,18 @@
         flow.close()
         grads.close()
 
-    g_piece = (block, ff)
     pl.run_scoped(
         second,
         pltpu.VMEM((2, NY, 2, rows // 2, width - block), f32),
         pltpu.VMEM((2, NX, 2, rows // 2, width + block), f32),
-        pltpu.VMEM((2, NC, block, cols), bf16),
-        pltpu.VMEM((tokens, block), bf16),
-        pltpu.VMEM((tokens, block), bf16),
-        pltpu.VMEM((tokens, block), bf16),
-        pltpu.VMEM((2, 4) + g_piece, f32),
-        pltpu.VMEM((STAGES,) + g_piece, f32),
+        pltpu.VMEM((3, NC, block, cols), bf16),
     )
 
 
 STAGES = 6
+PASSES = ((1, 0), (0, 0), (0, 1), (1, 1), (1, 2), (0, 2), (0, 3), (1, 3))
+P_TIME = 3.0
+Q_HALF = 2.6
 
 
 def back(nz, z_in, h_all, dy_all, w_all, cos, sin):
@@ -929,9 +996,14 @@
             pltpu.VMEM((seq, head), bf16),
             pltpu.VMEM((seq, head), f32),
             pltpu.VMEM((seq, head), f32),
+            pltpu.VMEM((tokens, block), bf16),
+            pltpu.VMEM((tokens, block), bf16),
+            pltpu.VMEM((tokens, block), bf16),
+            pltpu.VMEM((2, 4, block, ff), f32),
+            pltpu.VMEM((STAGES, block, ff), f32),
             dma,
             dma((3, 2)),
-            dma((2,)),
+            dma((3,)),
             dma((3,)),
             dma((STAGES,)),
             dma((4,)),

time: 330 us -> 311 us (0.942); the launches traced: 324 us -> 310 us
  Pallas kernels: 307 us -> 293 us
    pallas_call x1, Pallas kernels: 199 us -> 185 us  [back(): pl.pallas_call(functools.partial(back_kernel, nz), out_shape=(jax.ShapeDt...]
where the time goes in v3:
time: 311 us; the launch traced here: 310 us
  Pallas kernels  293 us (94%)
  other arithmetic  13.7 us (4%)
    pallas_call x1, Pallas kernels, back(): pl.pallas_call(functools.partial(back_kernel, nz), out_shape=(jax.ShapeDt...  185 us
    pallas_call x1, Pallas kernels, gather(): pl.pallas_call(functools.partial(gather_kernel, nz), out_shape=(jax.Shape...  88.3 us
    pallas_call x1, Pallas kernels, head_rows(): pl.pallas_call(functools.partial(heads_kernel, nz), out_shape=jax.ShapeDt...  19.1 us

profile of v3, /device:TPU:1, one launch (start us, length us, event | category | flops | bytes accessed | tf_op | source)
XLA Modules:
  0.0 309.9 jit_solution(769931067483546002)
XLA Ops:
  0.6 0.0 copy-start.4
  0.6 0.0 copy-start
  0.7 0.0 copy-start.9
  0.7 1.2 fusion.3
  1.9 0.0 copy-start.13
  1.9 0.0 copy-start.12
  1.9 0.1 rsqrt.15
  2.0 0.9 neg.3
  2.9 0.0 copy-start.6
  2.9 0.1 copy.23
  3.1 0.0 copy-done.13
  3.1 0.0 copy-done.12
  3.1 0.0 copy-start.7
  3.1 1.1 copy.21
  4.2 0.0 copy-done.4
  4.2 0.0 copy-start.5
  4.2 0.1 copy.24
  4.3 0.0 copy-start.10
  4.3 0.0 copy-start.8
  4.4 0.0 slice-start
  4.4 1.0 pad_maximum_fusion.3
  5.4 0.0 copy-done
  5.4 0.0 copy-done.9
  5.4 0.9 multiply_convert_fusion.h_ref
  6.3 0.0 copy-done.6
  6.3 0.0 copy-done.7
  6.3 0.0 copy-done.5
  6.4 0.0 copy-done.10
  6.4 0.0 copy-done.8
  6.5 0.0 slice-done
  6.5 1.0 pad_maximum_fusion.w_ref
  7.5 88.3 %gather.1 = (bf16[4,4,2,2,32,3072]{5,4,3,2,1,0:T(8,128)(2,1)}, bf16[4,4,2,2,32,3072]{5,4,3,2,1,0:T(8,128)(2,1)}, bf16[2,8,4,96,1024]{4,3,2,1,0:T(8,128)(2,1)}) custom-call(bf16[2,32,3072]{2,1,0:T(8,128)(2,1)} %multiply_convert_fusion.h_ref, bf16[2,32,3072]{2,1,0:T(8,128)(2,1)} %bitcast.85, bf16[4,96,1024]{2,1,0:T(8,128)(2,1)} %pad_maximum_fusion.w_ref), custom_call_target="tpu_custom_call" | custom-call | tf_op jit(solution)/shard_map/gather/pallas_call | solution.py:220
  95.8 19.1 %heads.1.z_in = bf16[4,2,256,256]{3,2,1,0:T(8,128)(2,1)} custom-call(bf16[2048,3072]{1,0:T(8,128)(2,1)} %bitcast.78, bf16[2048,3072]{1,0:T(8,128)(2,1)} %bitcast.80, bf16[2,3072,1024]{2,1,0:T(8,128)(2,1)} %bitcast.82), custom_call_target="tpu_custom_call" | custom-call | tf_op jit(solution)/shard_map/heads/pallas_call | solution.py:311
  114.9 185.3 %back.1 = (f32[2,32,2688]{2,1,0:T(8,128)}, f32[2,32,3456]{2,1,0:T(8,128)}, f32[4,96,1024]{2,1,0:T(8,128)}, f32[7,4,384,256]{3,2,1,0:T(8,128)}) custom-call(bf16[4,2,256,256]{3,2,1,0:T(8,128)(2,1)} %heads.1.z_in, bf16[2048,3072]{1,0:T(8,128)(2,1)} %bitcast.79, bf16[2048,3072]{1,0:T(8,128)(2,1)} %bitcast.81, bf16[2,3072,1024]{2,1,0:T(8,128)(2,1)} %bitcast.83, ...), custom_call_target="tpu_custom_call" | custom-call | tf_op jit(solution)/shard_map/back/pallas_call | solution.py:975
  300.2 0.0 copy-start.1
  300.2 1.6 fusion.4
  301.7 0.7 multiply_multiply_fusion
  302.4 0.9 slice_bitcast_fusion
  303.3 2.5 fusion.5
  305.9 0.8 fusion.2
  306.7 0.0 copy-done.2
  306.7 0.7 maximum_bitcast_fusion.2
  307.5 0.0 copy-start.11
  307.5 0.1 slice_bitcast_fusion.4
  307.6 0.8 maximum_bitcast_fusion
  308.4 0.0 copy-done.11
  308.4 0.8 pad_maximum_fusion.2
  309.2 0.8 pad_maximum_fusion.1
  (17 shorter events, 0.2 us)
Async XLA Ops:
  0.6 3.6 %copy-start.4 = (f32[512,64]{0,1:T(8,128)S(1)}, f32[512,64]{0,1:T(8,128)}, u32[]{:S(2)}) copy-start(f32[512,64]{0,1:T(8,128)} %param.19) | copy-start | bytes 393220
  0.6 4.7 %copy-start = (bf16[1,64,3072]{2,1,0:T(8,128)(2,1)S(1)}, bf16[1,64,3072]{2,1,0:T(8,128)(2,1)}, u32[]{:S(2)}) copy-start(bf16[1,64,3072]{2,1,0:T(8,128)(2,1)} %param.10) | copy-start | bytes 1179652
  0.7 4.7 %copy-start.9 = (f32[3072]{0:T(1024)S(1)}, f32[3072]{0:T(1024)}, u32[]{:S(2)}) copy-start(f32[3072]{0:T(1024)} %param.12) | copy-start | bytes 36868
  1.9 1.2 copy-start.13
  1.9 1.2 copy-start.12
  2.9 3.3 %copy-start.6 = (bf16[96,1024]{1,0:T(8,128)(2,1)S(1)}, bf16[96,1024]{1,0:T(8,128)(2,1)}, u32[]{:S(2)}) copy-start(bf16[96,1024]{1,0:T(8,128)(2,1)} %param.15) | copy-start | bytes 589828
  3.1 3.2 %copy-start.7 = (bf16[96,1024]{1,0:T(8,128)(2,1)S(1)}, bf16[96,1024]{1,0:T(8,128)(2,1)}, u32[]{:S(2)}) copy-start(bf16[96,1024]{1,0:T(8,128)(2,1)} %param.16) | copy-start | bytes 589828
  4.2 2.1 copy-start.5
  4.3 2.0 copy-start.10
  4.3 2.1 copy-start.8
  4.4 2.1 slice-start
  300.2 5.7 %copy-start.1 = (bf16[1,64,3072]{2,1,0:T(8,128)(2,1)S(1)}, bf16[1,64,3072]{2,1,0:T(8,128)(2,1)}, u32[]{:S(2)}) copy-start(bf16[1,64,3072]{2,1,0:T(8,128)(2,1)} %param.10) | copy-start | bytes 1179652
  300.2 5.7 %copy-start.3 = (f32[2,32,2688]{2,1,0:T(8,128)S(1)}, f32[2,32,2688]{2,1,0:T(8,128)}, u32[]{:S(2)}) copy-start(f32[2,32,2688]{2,1,0:T(8,128)} %get-tuple-element.16) | copy-start | bytes 2064388
  303.3 3.4 %copy-start.2 = (f32[4,96,1024]{2,1,0:T(8,128)S(1)}, f32[4,96,1024]{2,1,0:T(8,128)}, u32[]{:S(2)}) copy-start(f32[4,96,1024]{2,1,0:T(8,128)} %get-tuple-element.18) | copy-start | bytes 4718596
  307.5 0.9 copy-start.11

commit v4 on v3

--- a/solution.py
+++ b/solution.py
@@ -70,6 +70,9 @@
         self.event(self.free[link] + lag, copy.wait_recv, then)
         return k
 
+    def at(self, when, then):
+        self.event(when, lambda: None, then)
+
     def local(self, copy, size, then):
         copy.start()
         self.event(self.now + size / LOCAL + 1.0, copy.wait, then)
@@ -126,110 +129,8 @@
     return n * jnp.dtype(ref.dtype).itemsize
 
 
-def gather_kernel(nz, h_ref, dy_ref, w_ref, h_all, dy_all, w_all, send_sem, recv_sem, own_sem):
-    place = Place(nz)
-    y, x, c, z = place.get("y"), place.get("x"), place.get("c"), place.get("z")
-    place.meet([("x", 1), ("x", -1), ("y", 1), ("y", -1), ("y", 2), ("z", 1), ("z", -1), ("c", 1)])
-    flow = Flow(place, send_sem, recv_sem)
-    own = [
-        pltpu.make_async_copy(h_ref, h_all.at[y, x, c], own_sem.at[0]),
-        pltpu.make_async_copy(dy_ref, dy_all.at[y, x, c], own_sem.at[1]),
-        pltpu.make_async_copy(w_ref.at[y], w_all.at[0, z, y], own_sem.at[2]),
-    ]
-    for copy in own:
-        copy.start()
-    piece = nbytes(h_ref, 1)
-
-    def spot(ref, dy, dx, half):
-        return lambda: ref.at[place.get("y", dy), place.get("x", dx), c, half]
-
-    def spread(axis, half, offset, src, got):
-        def come(step, onward):
-            def then():
-                if onward:
-                    flow.send(axis, -step, got.spot(axis, step, offset, half), got.spot(axis, step, offset, half), piece, lambda: got(axis, 2, offset, half))
-                got(axis, step, offset, half)
-
-            return then
-
-        flow.send(axis, 1, src, got.spot(axis, 0, offset, half), piece, come(-1, half == 0))
-        flow.send(axis, -1, src, got.spot(axis, 0, offset, half), piece, come(1, half == 1))
-
-    class Got:
-        def __init__(self, ref, first):
-            self.ref, self.first, self.second = ref, first, "y" if first == "x" else "x"
-
-        def spot(self, axis, step, offset, half):
-            d = {axis: step, ("y" if axis == "x" else "x"): offset}
-            return spot(self.ref, d["y"], d["x"], half)
-
-        def __call__(self, axis, step, offset, half):
-            here = self.spot(axis, step, offset, half)
-            if axis == self.first:
-                spread(self.second, half, step, here, self)
-            flow.send("c", 1, here, here, piece)
-
-    size = nbytes(w_ref, 1)
-
-    def w_spot(who, dz, dy):
-        return lambda: w_all.at[who, place.get("z", dz), place.get("y", dy)]
-
-    def ring(step, dy, src=None):
-        def hop(n):
-            def then():
-                here = src if src and n == 0 else w_spot(0, -step * n, dy)
-                if n < nz - 1:
-                    flow.send("z", step, here, w_spot(0, -step * n, dy), size, hop(n + 1))
-                flow.send("c", 1, here, w_spot(1, -step * n, dy), size)
-
-            return then
-
-        return hop(0)
-
-    def w_at(dy):
-        return lambda: w_ref.at[place.get("y", dy)]
-
-    flow.send("y", -1, w_at(-1), w_spot(0, 0, 0), size, ring(1, 1))
-    flow.send("y", 1, w_at(1), w_spot(0, 0, 0), size, ring(-1, -1))
-    flow.send("y", 2, w_at(2), w_spot(0, 0, 0), size, ring(-1, 2), link=("y", 1))
-    ring(1, 0, w_at(0))()
-    arrays = [(h_ref, Got(h_all, "x")), (dy_ref, Got(dy_all, "y"))]
-    for ref, got in arrays:
-        for half in (0, 1):
-            spread(got.first, half, 0, lambda ref=ref, half=half: ref.at[half], got)
-    for ref, got in arrays:
-        for half in (0, 1):
-            src = lambda ref=ref, half=half: ref.at[half]
-            spread(got.second, half, 0, src, got)
-            flow.send("c", 1, src, got.spot(got.second, 0, 0, half), piece)
-    flow.run()
-    flow.close()
-    for copy in own:
-        copy.wait()
-
-
 def any_specs(n):
     return [pl.BlockSpec(memory_space=pl.ANY)] * n
-
-
-def gather(nz, h, dy, w):
-    half, rows, width = h.shape
-    everywhere = (NY, NX, NC) + h.shape
-    count = 60 + 64 + 3 + 4 * (nz - 1) + 4 * nz
-    vmem = pl.BlockSpec(memory_space=pltpu.VMEM)
-    return pl.pallas_call(
-        functools.partial(gather_kernel, nz),
-        out_shape=(
-            jax.ShapeDtypeStruct(everywhere, h.dtype),
-            jax.ShapeDtypeStruct(everywhere, dy.dtype),
-            jax.ShapeDtypeStruct((NC, nz) + w.shape, w.dtype),
-        ),
-        in_specs=[vmem] * 3,
-        out_specs=tuple(any_specs(3)),
-        scratch_shapes=[pltpu.SemaphoreType.DMA((count,)), pltpu.SemaphoreType.DMA((count,)), pltpu.SemaphoreType.DMA((3,))],
-        compiler_params=pltpu.CompilerParams(collective_id=0, has_side_effects=True),
-        name="gather",
-    )(h, dy, w)
 
 
 def mm(a, b, ca, cb):
@@ -259,74 +160,272 @@
 ORDER = (2, 1, -1, 0)
 
 
-def heads_kernel(nz, h_all, dy_all, w_all, z_got, h_v, dy_v, w_v, z_in, far, load_sem, own_sem, send_sem, recv_sem):
+class Gather:
+    def __init__(self, place, flow, own, full, first, cut, arrive):
+        self.place, self.flow, self.own, self.full, self.first, self.cut, self.arrive = place, flow, own, full, first, cut, arrive
+        self.second = "y" if first == "x" else "x"
+        self.size = nbytes(own, 1) * (cut.stop - cut.start) // own.shape[-1]
+
+    def mine(self, half):
+        return lambda: self.own.at[half, :, self.cut]
+
+    def spot(self, at, half):
+        y, x, c = (self.place.get(axis, at.get(axis, 0)) for axis in "yxc")
+        return lambda: self.full.at[y, x, c, half, :, self.cut]
+
+    def spread(self, axis, at, half, src):
+        def come(step, onward):
+            def then():
+                here = dict(at, **{axis: step})
+                if onward:
+                    far = dict(at, **{axis: 2})
+                    self.flow.send(axis, -step, self.spot(here, half), self.spot(here, half), self.size, lambda: self.got(axis, far, half))
+                self.got(axis, here, half)
+
+            return then
+
+        self.flow.send(axis, 1, src, self.spot(at, half), self.size, come(-1, half == 0))
+        self.flow.send(axis, -1, src, self.spot(at, half), self.size, come(1, half == 1))
+
+    def got(self, axis, at, half):
+        if axis == self.first:
+            self.spread(self.second, at, half, self.spot(at, half))
+        self.pair(at, half, self.spot(at, half))
+        self.arrive(at.get("y", 0), at.get("x", 0))
+
+    def pair(self, at, half, src):
+        there = lambda: self.arrive(at.get("y", 0), at.get("x", 0))
+        self.flow.send("c", 1, src, self.spot(at, half), self.size, there)
+
+    def start_first(self):
+        for half in (0, 1):
+            self.spread(self.first, {}, half, self.mine(half))
+
+    def start_second(self):
+        for half in (0, 1):
+            self.spread(self.second, {}, half, self.mine(half))
+            self.pair({}, half, self.mine(half))
+
+
+def front_kernel(nz, h_ref, dy_ref, w_ref, h_all, dy_all, w_all, z_got, w_heads, rows_v, z_in, far, send_sem, recv_sem, own_sem, rows_sem):
     bf16 = jnp.bfloat16
     place = Place(nz)
-    y = place.get("y")
+    y, x, c, z = (place.get(axis) for axis in "yxcz")
     last = y == NY - 1
     pair = z_in.shape[-1]
     head = pair // 2
-    seq = h_v.shape[1]
-    part = seq // 2
-    lo = (w_all.shape[2] - pair) * 2 // 3
-    w_load = pltpu.make_async_copy(w_all.at[0, :, lo : lo + pair], w_v, load_sem.at[0])
-    w_load.start()
-    loads = []
-    for n, step in enumerate(ORDER):
-        at = span(place.get("y", step), seq)
-        loads.append([pltpu.make_async_copy(a.at[at], b.at[n], load_sem.at[1 + 2 * n + m]) for m, (a, b) in enumerate(((h_all, h_v), (dy_all, dy_v)))])
-        for copy in loads[n]:
+    width = h_ref.shape[-1]
+    cols = w_ref.shape[-1]
+    lo = (cols - pair) * 2 // 3
+    hi = lo + pair
+    rows = z_in.shape[2]
+    flow = Flow(place, send_sem, recv_sem)
+    w_own = pltpu.make_async_copy(w_ref.at[y], w_all.at[0, z, y], own_sem.at[2])
+    w_own.start()
+    w_heads[z, y] = w_ref[y, :, lo:hi]
+    place.meet([("x", 1), ("x", -1), ("y", 1), ("y", -1), ("y", 2), ("z", 1), ("z", -1), ("c", 1)])
+
+    slots = rows_v.shape[0]
+    free, queue, ready = list(range(slots)), [], []
+    pieces = {}
+    parts_done = {}
+    weights = [4 * nz]
+
+    def load():
+        while free and queue and weights[0] == 0:
+            kind, dy, dx = queue.pop(0)
+            slot = free.pop(0)
+            src = (h_all, dy_all)[kind].at[place.get("y", dy), place.get("x", dx)]
+            copy = pltpu.make_async_copy(src, rows_v.at[slot], rows_sem.at[slot])
+            flow.local(copy, nbytes(rows_v, 1), lambda slot=slot, kind=kind, dy=dy, dx=dx: flow.task(CHUNK_TIME, lambda: product(kind, dy, dx, slot)))
+
+    def arrive(kind):
+        need = (8, 4)[kind]
+
+        def one(dy, dx):
+            key = (kind, dy, dx)
+            pieces[key] = pieces.get(key, 0) + 1
+            if pieces[key] == need:
+                queue.append(key)
+                load()
+
+        return one
+
+    def weight_come():
+        weights[0] -= 1
+        if weights[0] == 0:
+            load()
+
+    def product(kind, dy, dx, slot):
+        at = place.get("y", dy), place.get("x", dx)
+        step = 2 if nz % 2 == 0 else 1
+        deep = step * (width // nz)
+
+        def dot(first):
+            def some(i, total):
+                left = rows_v[slot, :, :, :, span(i, deep)].reshape(rows, deep)
+                right = w_heads[pl.ds(i * step, step), :, :, first:].reshape(deep, pair - first)
+                return total + mm(left, right, 1, 0)
+
+            return lax.fori_loop(0, nz // step, some, jnp.zeros((rows, pair - first), jnp.float32))
+
+        if kind == 0:
+            made = dot(0).astype(bf16)
+            z_in[at[0], at[1], :, :head] = made[:, :head]
+
+            @pl.when(last)
+            def _():
+                z_in[at[0], at[1], :, head:] = made[:, head:]
+
+        else:
+
+            @pl.when(jnp.logical_not(last))
+            def _():
+                z_in[at[0], at[1], :, head:] = dot(head).astype(bf16)
+
+        free.append(slot)
+        load()
+        parts_done[dy, dx] = parts_done.get((dy, dx), 0) + 1
+        if parts_done[dy, dx] == 2:
+            deliver(dy, dx)
+
+    own_copies = []
+
+    def deliver(dy, dx):
+        at = lambda: z_in.at[place.get("y", dy), place.get("x", dx)]
+        size = nbytes(z_in, 2)
+
+        def there(step=0):
+            return lambda: z_got.at[place.get("y", step), place.get("x", dx)]
+
+        if dy == 0:
+            copy = pltpu.make_async_copy(at(), there()(), own_sem.at[4 + dx % NX])
             copy.start()
-    place.meet([("y", 1), ("y", -1)])
-    flow = Flow(place, send_sem, recv_sem)
-    w_load.wait()
-    for n, step in enumerate(ORDER):
-        for copy in loads[n]:
-            copy.wait()
-        q = place.get("y", step)
-
-        @pl.loop(0, 2)
-        def _(p):
-            at = span(p, part)
-            from_h = mm(h_v[n, at, :], w_v[...], 1, 0)
-            from_dy = mm(dy_v[n, at, :], w_v[:, head:], 1, 0)
-            z_in[q, p, :, :head] = from_h[:, :head].astype(bf16)
-            z_in[q, p, :, head:] = jnp.where(last, from_h[:, head:], from_dy).astype(bf16)
-
-        flow.spend(2.3)
-        if step:
-            exchange(flow, place, z_in, z_got, far, step)
-    own = pltpu.make_async_copy(z_in.at[y], z_got.at[y], own_sem)
-    own.start()
+            own_copies.append(copy)
+        elif dy == 2:
+            way = 1 if dx in (0, 2) else -1
+
+            def onward():
+                flow.send("y", way, lambda: far.at[dx % NX], there(-way), size)
+
+            flow.send("y", way, at, lambda: far.at[dx % NX], size, onward)
+        else:
+            flow.send("y", dy, at, there(), size)
+
+    def w_part(ref, who, dz, dy, cut):
+        if ref is None:
+            return lambda: w_heads.at[place.get("z", dz), place.get("y", dy)]
+        return lambda: w_all.at[who, place.get("z", dz), place.get("y", dy), :, cut]
+
+    cuts = [slice(lo, hi), slice(0, lo), slice(hi, cols)]
+
+    def ring(step, dy, n_cut, src=None, hops=nz - 1, lead=True):
+        cut = cuts[n_cut]
+        home = None if n_cut == 0 else w_all
+        size = nbytes(w_ref, 1) * (cut.stop - cut.start) // cols
+
+        def hop(n):
+            def then():
+                here = src if src and n == 0 else w_part(home, 0, -step * n, dy, cut)
+                if n < hops:
+                    flow.send("z", step, here, w_part(home, 0, -step * n, dy, cut), size, hop(n + 1))
+                if n or lead:
+                    flow.send("c", 1, here, w_part(w_all, 1, -step * n, dy, cut), size)
+                    if n_cut == 0:
+                        weight_come()
+
+            return then
+
+        return hop(0)
+
+    def rings(dy, n_cut, src=None):
+        if n_cut:
+            return ring(1 if dy in (0, 1) else -1, dy, n_cut, src)
+        both = [ring(1, dy, 0, src, nz // 2), ring(-1, dy, 0, src, (nz - 1) // 2, False)]
+        return lambda: [one() for one in both]
+
+    def w_at(dy, cut):
+        return lambda: w_ref.at[place.get("y", dy), :, cut]
+
+    tail = width // nz * H_TAIL
+    gathers = [
+        Gather(place, flow, h_ref, h_all, "x", slice(0, width - tail), arrive(0)),
+        Gather(place, flow, dy_ref, dy_all, "y", slice(0, width), arrive(1)),
+        Gather(place, flow, h_ref, h_all, "y", slice(width - tail, width), arrive(0)),
+    ]
+    def w_start(n_cut, dys):
+        cut = cuts[n_cut]
+        home = None if n_cut == 0 else w_all
+        size = nbytes(w_ref, 1) * (cut.stop - cut.start) // cols
+        there = w_part(home, 0, 0, 0, cut)
+        for dy in dys:
+            if dy == 0:
+                rings(0, n_cut, w_at(0, cut))()
+            elif dy == 2:
+                flow.send("y", 2, w_at(2, cut), there, size, rings(2, n_cut), link=("y", 1))
+            else:
+                flow.send("y", -dy, w_at(-dy, cut), there, size, rings(dy, n_cut))
+
+    w_start(0, (0, 1, -1, 2))
+    for one in gathers:
+        one.start_first()
+    flow.at(W_TIMES[0], lambda: [w_start(1, (0, -1)), w_start(2, (0, -1))])
+    flow.at(W_TIMES[1], lambda: [w_start(1, (1, 2)), w_start(2, (1, 2))])
+    for one in gathers:
+        one.start_second()
+    for n, (ref, full) in enumerate(((h_ref, h_all), (dy_ref, dy_all))):
+        copy = pltpu.make_async_copy(ref, full.at[y, x, c], own_sem.at[n])
+        there = arrive(n)
+        flow.local(copy, nbytes(ref, 0), lambda n=n, there=there: [there(0, 0) for _ in range((4, 2)[n])])
     flow.run()
+    heads_home = pltpu.make_async_copy(w_heads, w_all.at[0, :, :, :, lo:hi], own_sem.at[3])
+    w_own.wait()
+    heads_home.start()
     flow.close()
-    own.wait()
-
-
-def head_rows(nz, pair, seq, h_all, dy_all, w_all):
-    tokens, width = h_all.shape
-    bf16 = h_all.dtype
+    for copy in own_copies:
+        copy.wait()
+    heads_home.wait()
+
+
+CHUNK_TIME = 1.0
+W_TIMES = (0.0, 0.0)
+H_TAIL = 1
+
+
+def front(nz, pair, h, dy, w):
+    half, rows, width = h.shape
+    everywhere = (NY, NX, NC) + h.shape
+    cols = w.shape[-1]
+    gathers = 3 * (30 + 32)
+    count = gathers + 3 * 3 + 3 * 4 * (nz - 1) + 3 * 4 * nz + 2 * NX + 2 * NX
+    vmem = pl.BlockSpec(memory_space=pltpu.VMEM)
     dma = pltpu.SemaphoreType.DMA
-    halves = (NY, 2, seq // 2, pair)
+    chunk = NC * half * rows
+    z_shape = (NY, NX, chunk, pair)
+    slots = 8
     return pl.pallas_call(
-        functools.partial(heads_kernel, nz),
-        out_shape=jax.ShapeDtypeStruct(halves, bf16),
-        in_specs=any_specs(3),
-        out_specs=pl.BlockSpec(memory_space=pl.ANY),
+        functools.partial(front_kernel, nz),
+        out_shape=(
+            jax.ShapeDtypeStruct(everywhere, h.dtype),
+            jax.ShapeDtypeStruct(everywhere, dy.dtype),
+            jax.ShapeDtypeStruct((NC, nz) + w.shape, w.dtype),
+            jax.ShapeDtypeStruct(z_shape, h.dtype),
+        ),
+        in_specs=[vmem] * 3,
+        out_specs=tuple(any_specs(4)),
         scratch_shapes=[
-            pltpu.VMEM((NY, seq, width), bf16),
-            pltpu.VMEM((NY, seq, width), bf16),
-            pltpu.VMEM((width, pair), bf16),
-            pltpu.VMEM(halves, bf16),
-            pltpu.VMEM(halves[1:], bf16),
-            dma((1 + 2 * NY,)),
-            dma,
-            dma((6,)),
-            dma((6,)),
+            pltpu.VMEM((nz,) + w.shape[:-1] + (pair,), w.dtype),
+            pltpu.VMEM((slots, NC) + h.shape, h.dtype),
+            pltpu.VMEM(z_shape, h.dtype),
+            pltpu.VMEM((NX, chunk, pair), h.dtype),
+            dma((count,)),
+            dma((count,)),
+            dma((4 + NX,)),
+            dma((slots,)),
         ],
-        compiler_params=pltpu.CompilerParams(collective_id=1, has_side_effects=True, vmem_limit_bytes=VMEM_LIMIT),
-        name="heads",
-    )(h_all, dy_all, w_all)
+        compiler_params=pltpu.CompilerParams(collective_id=0, has_side_effects=True, vmem_limit_bytes=VMEM_LIMIT),
+        name="front",
+    )(h, dy, w)
 
 
 SETS = (2, 1, -1, 0)
@@ -543,10 +642,10 @@
 
     def gather_up(self, tiles, some):
         seq = self.h_plus.shape[0] // NY
-        for tile, value in zip(tiles, some(0, pl.ds(0, seq))):
-            tile[...] = value
-
-        @pl.loop(1, NY)
+        for tile in tiles:
+            tile[...] = jnp.zeros_like(tile)
+
+        @pl.loop(0, NY)
         def _(q):
             for tile, value in zip(tiles, some(q, span(q, seq))):
                 tile[...] += value
@@ -1050,13 +1149,13 @@
         cos = jnp.concatenate([rope_cos, rope_cos], axis=1)
         sin = jnp.concatenate([-rope_sin, rope_sin], axis=1)
 
-        h_all, dy_all, w_all = gather(nz, h_loc, dy_loc, w_loc)
+        h_all, dy_all, w_all, z_got = front(nz, 2 * head, h_loc, dy_loc, w_loc)
         tokens = NY * seq
         cols = w_loc.shape[2]
         h_all = h_all.reshape(tokens, width)
         dy_all = dy_all.reshape(tokens, width)
         w_all = w_all.reshape(NC, width, cols)
-        z_got = head_rows(nz, 2 * head, seq, h_all, dy_all, w_all)
+        z_got = z_got.reshape(NY, 2, seq // 2, 2 * head)
         p_sum, q_sum, g_sum = back(nz, z_got, h_all, dy_all, w_all, cos, sin)
         p_sum = p_sum.reshape(rows, -1)
         q_sum = q_sum.reshape(rows, -1)

time: 311 us -> 307 us (0.987)
  Pallas kernels: 293 us -> 289 us
    pallas_call x2 -> x1, Pallas kernels: 107 us -> 106 us  [front(): pl.pallas_call(functools.partial(front_kernel, nz), out_shape=(jax.ShapeD...]
where the time goes in v4:
time: 307 us; the launch traced here: 306 us
  Pallas kernels  289 us (94%)
  other arithmetic  13.6 us (4%)
    pallas_call x1, Pallas kernels, back(): pl.pallas_call(functools.partial(back_kernel, nz), out_shape=(jax.ShapeDt...  183 us
    pallas_call x1, Pallas kernels, front(): pl.pallas_call(functools.partial(front_kernel, nz), out_shape=(jax.ShapeD...  106 us

profile of v4, /device:TPU:1, one launch (start us, length us, event | category | flops | bytes accessed | tf_op | source)
XLA Modules:
  0.0 306.2 jit_solution(16216899496764323672)
XLA Ops:
  0.6 0.0 copy-start.4
  0.6 0.0 copy-start
  0.7 0.0 copy-start.9
  0.7 1.2 fusion.3
  1.9 0.0 copy-start.13
  1.9 0.0 copy-start.12
  1.9 0.1 rsqrt.15
  2.0 0.9 neg.3
  2.9 0.0 copy-start.6
  2.9 0.1 copy.23
  3.1 0.0 copy-done.13
  3.1 0.0 copy-done.12
  3.1 0.0 copy-start.7
  3.1 1.1 copy.21
  4.2 0.0 copy-done.4
  4.2 0.0 copy-start.5
  4.2 0.1 copy.24
  4.3 0.0 copy-start.10
  4.3 0.0 copy-start.8
  4.4 0.0 slice-start
  4.4 1.0 pad_maximum_fusion.3
  5.4 0.0 copy-done
  5.4 0.0 copy-done.9
  5.4 0.9 multiply_convert_fusion.h_ref
  6.3 0.0 copy-done.6
  6.3 0.0 copy-done.7
  6.3 0.0 copy-done.5
  6.4 0.0 copy-done.10
  6.4 0.0 copy-done.8
  6.5 0.0 slice-done
  6.5 1.0 pad_maximum_fusion.w_ref
  7.5 106.0 %front.1 = (bf16[4,4,2,2,32,3072]{5,4,3,2,1,0:T(8,128)(2,1)}, bf16[4,4,2,2,32,3072]{5,4,3,2,1,0:T(8,128)(2,1)}, bf16[2,8,4,96,1024]{4,3,2,1,0:T(8,128)(2,1)}, bf16[4,4,128,256]{3,2,1,0:T(8,128)(2,1)}) custom-call(bf16[2,32,3072]{2,1,0:T(8,128)(2,1)} %multiply_convert_fusion.h_ref, bf16[2,32,3072]{2,1,0:T(8,128)(2,1)} %bitcast.83, ...), custom_call_target="tpu_custom_call" | custom-call | tf_op jit(solution)/shard_map/front/pallas_call | solution.py:406
  113.4 183.0 %back.1 = (f32[2,32,2688]{2,1,0:T(8,128)}, f32[2,32,3456]{2,1,0:T(8,128)}, f32[4,96,1024]{2,1,0:T(8,128)}, f32[7,4,384,256]{3,2,1,0:T(8,128)}) custom-call(bf16[4,2,256,256]{3,2,1,0:T(8,128)(2,1)} %bitcast.84, bf16[2048,3072]{1,0:T(8,128)(2,1)} %bitcast.79, bf16[2048,3072]{1,0:T(8,128)(2,1)} %bitcast.80, bf16[2,3072,1024]{2,1,0:T(8,128)(2,1)} %bitcast.81, ...), custom_call_target="tpu_custom_call" | custom-call | tf_op jit(solution)/shard_map/back/pallas_call | solution.py:1074
  296.4 0.0 copy-start.1
  296.4 0.0 copy-start.3
  296.4 1.6 fusion.4
  298.0 0.7 multiply_multiply_fusion
  298.7 0.9 slice_bitcast_fusion
  299.6 2.5 fusion.5
  302.1 0.0 copy-done.1
  302.1 0.0 copy-done.3
  302.1 0.8 fusion.2
  303.0 0.7 maximum_bitcast_fusion.2
  303.7 0.0 copy-start.11
  303.7 0.1 slice_bitcast_fusion.4
  303.9 0.8 maximum_bitcast_fusion
  304.6 0.8 pad_maximum_fusion.2
  305.4 0.8 pad_maximum_fusion.1
  (16 shorter events, 0.2 us)
Async XLA Ops:
  0.6 3.6 %copy-start.4 = (f32[512,64]{0,1:T(8,128)S(1)}, f32[512,64]{0,1:T(8,128)}, u32[]{:S(2)}) copy-start(f32[512,64]{0,1:T(8,128)} %param.19) | copy-start | bytes 393220
  0.6 4.7 %copy-start = (bf16[1,64,3072]{2,1,0:T(8,128)(2,1)S(1)}, bf16[1,64,3072]{2,1,0:T(8,128)(2,1)}, u32[]{:S(2)}) copy-start(bf16[1,64,3072]{2,1,0:T(8,128)(2,1)} %param.10) | copy-start | bytes 1179652
  0.7 4.7 %copy-start.9 = (f32[3072]{0:T(1024)S(1)}, f32[3072]{0:T(1024)}, u32[]{:S(2)}) copy-start(f32[3072]{0:T(1024)} %param.12) | copy-start | bytes 36868
  1.9 1.2 copy-start.13
  1.9 1.2 copy-start.12
  2.9 3.3 %copy-start.6 = (bf16[96,1024]{1,0:T(8,128)(2,1)S(1)}, bf16[96,1024]{1,0:T(8,128)(2,1)}, u32[]{:S(2)}) copy-start(bf16[96,1024]{1,0:T(8,128)(2,1)} %param.15) | copy-start | bytes 589828
  3.1 3.2 %copy-start.7 = (bf16[96,1024]{1,0:T(8,128)(2,1)S(1)}, bf16[96,1024]{1,0:T(8,128)(2,1)}, u32[]{:S(2)}) copy-start(bf16[96,1024]{1,0:T(8,128)(2,1)} %param.16) | copy-start | bytes 589828
  4.2 2.1 copy-start.5
  4.3 2.0 copy-start.10
  4.3 2.1 copy-start.8
  4.4 2.1 slice-start
  296.4 5.7 %copy-start.1 = (bf16[1,64,3072]{2,1,0:T(8,128)(2,1)S(1)}, bf16[1,64,3072]{2,1,0:T(8,128)(2,1)}, u32[]{:S(2)}) copy-start(bf16[1,64,3072]{2,1,0:T(8,128)(2,1)} %param.10) | copy-start | bytes 1179652
  296.4 5.7 %copy-start.3 = (f32[2,32,2688]{2,1,0:T(8,128)S(1)}, f32[2,32,2688]{2,1,0:T(8,128)}, u32[]{:S(2)}) copy-start(f32[2,32,2688]{2,1,0:T(8,128)} %get-tuple-element.18) | copy-start | bytes 2064388
  299.6 3.4 %copy-start.2 = (f32[4,96,1024]{2,1,0:T(8,128)S(1)}, f32[4,96,1024]{2,1,0:T(8,128)}, u32[]{:S(2)}) copy-start(f32[4,96,1024]{2,1,0:T(8,128)} %get-tuple-element.20) | copy-start | bytes 4718596
  303.7 0.9 copy-start.11

commit v5 on v4

--- a/solution.py
+++ b/solution.py
@@ -51,21 +51,30 @@
         heapq.heappush(self.events, (when, self.order, wait, then))
         self.order += 1
 
-    def send(self, axis, step, src, dst, size, then=None, link=None):
+    def send(self, axis, step, src, dst, size, then=None, link=None, alt=None):
         k = len(self.copies)
         link = link or (axis, step)
         begin = max(self.now, self.free.get(link, 0.0))
         rate, lag = (PAIR, 1.5) if axis == "c" else (LINK, HOP)
         self.free[link] = begin + size / rate
-        copy = pltpu.make_async_remote_copy(
-            src_ref=src(),
-            dst_ref=dst(),
-            send_sem=self.send_sem.at[self.base + k],
-            recv_sem=self.recv_sem.at[self.base + k],
-            device_id=self.place.device(axis, step),
-            device_id_type=MESH,
-        )
-        copy.start()
+
+        def make(dst):
+            return pltpu.make_async_remote_copy(
+                src_ref=src(),
+                dst_ref=dst(),
+                send_sem=self.send_sem.at[self.base + k],
+                recv_sem=self.recv_sem.at[self.base + k],
+                device_id=self.place.device(axis, step),
+                device_id_type=MESH,
+            )
+
+        copy = make(dst)
+        if alt is None:
+            copy.start()
+        else:
+            when, other = alt
+            pl.when(jnp.logical_not(when))(copy.start)
+            pl.when(when)(make(other).start)
         self.copies.append(copy)
         self.event(self.free[link] + lag, copy.wait_recv, then)
         return k
@@ -207,9 +216,24 @@
             self.pair({}, half, self.mine(half))
 
 
-def front_kernel(nz, h_ref, dy_ref, w_ref, h_all, dy_all, w_all, z_got, w_heads, rows_v, z_in, far, send_sem, recv_sem, own_sem, rows_sem):
+def front_kernel(
+    nz, x_ref, dy_ref, gain, w_qkv, w_out, w_gate, w_up, w_down, h_all, dy_all, w_all, z_got, h_ref, w_ref, w_heads, rows_v, z_in, far, send_sem, recv_sem, own_sem, rows_sem
+):
     bf16 = jnp.bfloat16
     place = Place(nz)
+    for half in range(2):
+        wide = x_ref[half].astype(jnp.float32)
+        h_ref[half] = (wide * lax.rsqrt(jnp.mean(wide * wide, axis=-1, keepdims=True) + NORM_EPS) * gain[...]).astype(bf16)
+    wide_ff = w_gate.shape[1] // NY
+    one = w_out.shape[1] // (NY - 1)
+    for q in range(NY):
+        ffs = slice(q * wide_ff, (q + 1) * wide_ff)
+        w_ref[q, :, :wide_ff] = w_gate[:, ffs]
+        w_ref[q, :, wide_ff : 2 * wide_ff] = w_up[:, ffs]
+        at = 2 * wide_ff
+        w_ref[q, :, at : at + one] = w_qkv[:, q * one : (q + 1) * one]
+        w_ref[q, :, at + one : at + 2 * one] = w_out[:, q * one : (q + 1) * one] if q < NY - 1 else w_qkv[:, NY * one :]
+        w_ref[q, :, at + 2 * one :] = w_down[:, ffs]
     y, x, c, z = (place.get(axis) for axis in "yxcz")
     last = y == NY - 1
     pair = z_in.shape[-1]
@@ -392,10 +416,14 @@
 H_TAIL = 1
 
 
-def front(nz, pair, h, dy, w):
-    half, rows, width = h.shape
-    everywhere = (NY, NX, NC) + h.shape
-    cols = w.shape[-1]
+def front(nz, x, dy, gain, w_qkv, w_out, w_gate, w_up, w_down):
+    half, rows, width = x.shape
+    everywhere = (NY, NX, NC) + x.shape
+    slab = w_qkv.shape[0]
+    pair = 2 * w_out.shape[1] // (NY - 1)
+    cols = pair + 3 * w_gate.shape[1] // NY
+    w_shape = (NY, slab, cols)
+    bf16 = x.dtype
     gathers = 3 * (30 + 32)
     count = gathers + 3 * 3 + 3 * 4 * (nz - 1) + 3 * 4 * nz + 2 * NX + 2 * NX
     vmem = pl.BlockSpec(memory_space=pltpu.VMEM)
@@ -406,18 +434,20 @@
     return pl.pallas_call(
         functools.partial(front_kernel, nz),
         out_shape=(
-            jax.ShapeDtypeStruct(everywhere, h.dtype),
-            jax.ShapeDtypeStruct(everywhere, dy.dtype),
-            jax.ShapeDtypeStruct((NC, nz) + w.shape, w.dtype),
-            jax.ShapeDtypeStruct(z_shape, h.dtype),
+            jax.ShapeDtypeStruct(everywhere, bf16),
+            jax.ShapeDtypeStruct(everywhere, bf16),
+            jax.ShapeDtypeStruct((NC, nz) + w_shape, bf16),
+            jax.ShapeDtypeStruct(z_shape, bf16),
         ),
-        in_specs=[vmem] * 3,
+        in_specs=[vmem] * 8,
         out_specs=tuple(any_specs(4)),
         scratch_shapes=[
-            pltpu.VMEM((nz,) + w.shape[:-1] + (pair,), w.dtype),
-            pltpu.VMEM((slots, NC) + h.shape, h.dtype),
-            pltpu.VMEM(z_shape, h.dtype),
-            pltpu.VMEM((NX, chunk, pair), h.dtype),
+            pltpu.VMEM(x.shape, bf16),
+            pltpu.VMEM(w_shape, bf16),
+            pltpu.VMEM((nz,) + w_shape[:-1] + (pair,), bf16),
+            pltpu.VMEM((slots, NC) + x.shape, bf16),
+            pltpu.VMEM(z_shape, bf16),
+            pltpu.VMEM((NX, chunk, pair), bf16),
             dma((count,)),
             dma((count,)),
             dma((4 + NX,)),
@@ -425,7 +455,7 @@
         ],
         compiler_params=pltpu.CompilerParams(collective_id=0, has_side_effects=True, vmem_limit_bytes=VMEM_LIMIT),
         name="front",
-    )(h, dy, w)
+    )(x, dy, gain, w_qkv, w_out, w_gate, w_up, w_down)
 
 
 SETS = (2, 1, -1, 0)
@@ -610,7 +640,7 @@
     flow = None
 
 
-    def __init__(self, nz, place, h_all, dy_all, acts, z_out, z_land, g_sum, far, h_plus, h_minus, dy_minus, tiles, stage, load_sem, stage_sem, own_sem):
+    def __init__(self, nz, place, h_all, dy_all, acts, z_out, z_land, outs, far, h_plus, h_minus, dy_minus, tiles, stage, load_sem, stage_sem, own_sem):
         self.__dict__.update({k: v for k, v in locals().items() if k != "self"})
         self.ff = acts.shape[-1] // 3
         self.pair = z_out.shape[-1]
@@ -784,25 +814,49 @@
     def home(self, lane, slot):
         flow, place = self.flow, self.place
         slab = self.block // NY
-        first, end = self.cols[lane]
-
-        def rows(step):
-            return lambda: self.stage.at[slot, pl.ds(pl.multiple_of(place.get("y", step) * slab, slab), slab)]
-
-        def mine(step=0):
-            return lambda: self.g_sum.at[place.get("y", step), :, first:end]
-
+        way = self.far_way[lane]
         size = self.size // NY
-        way = self.far_way[lane]
-
-        def onward():
-            flow.send("y", way, lambda: self.far.at[lane], mine(-way), size)
-
-        sent = [flow.send("y", way, rows(2), lambda: self.far.at[lane], size, onward)]
-        sent += [flow.send("y", step, rows(step), mine(), size) for step in (1, -1)]
-        copy = pltpu.make_async_copy(rows(0)(), mine()(), self.own_sem.at[lane])
-        copy.start()
-        self.users[slot] += [functools.partial(flow.wait_sent, k) for k in sent] + [copy.wait]
+
+        def rows(step, cut=slice(None)):
+            return lambda: self.stage.at[slot, pl.ds(pl.multiple_of(place.get("y", step) * slab, slab), slab), cut]
+
+        def columns(out, step, wide):
+            at = place.get("y", step) * wide
+            return lambda: self.outs[out].at[:, pl.ds(pl.multiple_of(at, wide), wide)]
+
+        def deliver(size, src, far, dst, n, other=None):
+            def alt(step):
+                return None if other is None else (place.get("y", step) == NY - 1, other(step))
+
+            def onward():
+                flow.send("y", way, far, dst(-way), size, alt=alt(-way))
+
+            sent = [flow.send("y", way, src(2), far, size, onward)]
+            sent += [flow.send("y", step, src(step), dst(0), size, alt=alt(0)) for step in (1, -1)]
+            copies = [(None, pltpu.make_async_copy(src(0)(), dst(0)(), self.own_sem.at[n]))]
+            if other is not None:
+                last = place.get("y") == NY - 1
+                copies = [(jnp.logical_not(last), copies[0][1]), (last, pltpu.make_async_copy(src(0)(), other(0)(), self.own_sem.at[n]))]
+            for when, copy in copies:
+                if when is None:
+                    copy.start()
+                else:
+                    pl.when(when)(copy.start)
+            self.users[slot] += [functools.partial(flow.wait_sent, k) for k in sent] + [copies[0][1].wait]
+
+        if lane < 3:
+            deliver(size, rows, lambda: self.far.at[lane], lambda step: columns(lane, step, self.ff), lane)
+            return
+        head = self.pair // 2
+        first, second = slice(0, head), slice(head, self.pair)
+        deliver(size // 2, lambda step: rows(step, first), lambda: self.far.at[3, :, first], lambda step: columns(3, step, head), 3)
+        value = lambda: self.outs[3].at[:, NY * head :]
+
+        def out_rows(step):
+            at = lax.rem(place.get("y", step), NY - 1) * head
+            return lambda: self.outs[4].at[:, pl.ds(pl.multiple_of(at, head), head)]
+
+        deliver(size // 2, lambda step: rows(step, second), lambda: self.far.at[3, :, second], out_rows, 4, lambda step: value)
 
     def close(self):
         for users in self.users:
@@ -816,12 +870,21 @@
     h_all,
     dy_all,
     w_all,
+    cos_in,
+    sin_in,
+    x_ref,
+    dy_ref,
+    gain,
+    y_out,
+    dx_out,
+    g_qkv,
+    g_out,
+    g_gate,
+    g_up,
+    g_down,
+    z_land,
     cos_ref,
     sin_ref,
-    p_sum,
-    q_sum,
-    g_sum,
-    z_land,
     z_got,
     z_back,
     z_out,
@@ -865,6 +928,8 @@
 
     z_load = pltpu.make_async_copy(z_in, z_got, load_sem)
     z_load.start()
+    cos_ref[...] = jnp.concatenate([cos_in[...], cos_in[...]], axis=0).T
+    sin_ref[...] = jnp.concatenate([-sin_in[...], sin_in[...]], axis=0).T
     early = Flow(place, send_sem, recv_sem)
     peers = [("x", 1), ("x", -1), ("y", 1), ("y", -1), ("z", 1), ("z", -1), ("c", 1)]
 
@@ -875,7 +940,7 @@
     def all_out():
         early.send("c", 1, lambda: z_out.at[:, :, :, other], lambda: pair_acts.at[:, :, :, :, lo:hi], nbytes(z_out, 0) // NC)
 
-    grads = Grads(nz, place, h_all, dy_all, acts, z_out, z_land, g_sum, far, h_plus, h_minus, dy_minus, tiles, stage, g_load_sem, stage_sem, own_sem)
+    grads = Grads(nz, place, h_all, dy_all, acts, z_out, z_land, (g_gate, g_up, g_down, g_qkv, g_out), far, h_plus, h_minus, dy_minus, tiles, stage, g_load_sem, stage_sem, own_sem)
 
     def first(h_rows, dy_rows, w_v):
         begin, go = gated(place, early, h_all, dy_all, w_all, acts, row_sem, share, h_rows, dy_rows, w_v)
@@ -1015,18 +1080,25 @@
             flow.task(Q_HALF, start)
             flow.task(Q_HALF, end)
 
-        def finish(out):
-            def done(half, ref):
-                out[half] = ref()[...]
-
-            return done
+        edge = width - block
+        def p_finish(half, ref):
+            y_out[half, :, :edge] = (x_ref[half, :, :edge].astype(f32) + ref()[...]).astype(bf16)
+
+        def q_finish(half, ref):
+            y_out[half, :, edge:] = (x_ref[half, :, edge:].astype(f32) + ref()[:, width:]).astype(bf16)
+            wide = x_ref[half].astype(f32)
+            scale = lax.rsqrt(jnp.mean(wide * wide, axis=-1, keepdims=True) + NORM_EPS)
+            d_normed = ref()[:, :width].astype(bf16).astype(f32) * gain[...]
+            mean = jnp.mean(d_normed * wide, axis=-1, keepdims=True)
+            grad = d_normed * scale - wide * (scale * scale * scale * mean)
+            dx_out[half] = (dy_ref[half].astype(f32) + grad).astype(bf16)
 
         def free(task):
             return lambda s: task(s + 2) if s + 2 < len(SETS) else None
 
         planes = [
-            Plane(place, flow, p_tile, p_land, "y", finish(p_sum), free(p_task)),
-            Plane(place, flow, q_tile, q_land, "x", finish(q_sum), free(q_task)),
+            Plane(place, flow, p_tile, p_land, "y", p_finish, free(p_task)),
+            Plane(place, flow, q_tile, q_land, "x", q_finish, free(q_task)),
         ]
 
         for lane in range(3):
@@ -1056,9 +1128,9 @@
 Q_HALF = 2.6
 
 
-def back(nz, z_in, h_all, dy_all, w_all, cos, sin):
+def back(nz, z_in, h_all, dy_all, w_all, cos, sin, x, dy, gain):
     tokens, width = h_all.shape
-    seq, head = cos.shape
+    seq, head = cos.shape[1], 2 * cos.shape[0]
     pair = 2 * head
     cols = w_all.shape[2]
     ff = (cols - pair) // 3
@@ -1070,18 +1142,26 @@
     blocks = (NY, 2, NX // 2, NC, rows, pair)
     p_piece = (rows // 2, width - block)
     q_piece = (rows // 2, width + block)
-    count = 6 + 2 * NY + 1 + 4 * (nz - 1) + 4 * 4 + 2 * 5 * 6
+    count = 6 + 2 * NY + 1 + 4 * (nz - 1) + 5 * 4 + 2 * 5 * 6
+    slab = block // NY
+    weight = jax.ShapeDtypeStruct((slab, NY * ff), f32)
     return pl.pallas_call(
         functools.partial(back_kernel, nz),
         out_shape=(
-            jax.ShapeDtypeStruct((2,) + p_piece, f32),
-            jax.ShapeDtypeStruct((2,) + q_piece, f32),
-            jax.ShapeDtypeStruct((NY, block // NY, cols), f32),
+            jax.ShapeDtypeStruct(x.shape, bf16),
+            jax.ShapeDtypeStruct(x.shape, bf16),
+            jax.ShapeDtypeStruct((slab, (NY + 1) * head), f32),
+            jax.ShapeDtypeStruct((slab, (NY - 1) * head), f32),
+            weight,
+            weight,
+            weight,
             jax.ShapeDtypeStruct((nz - 1, 4, block, ff), f32),
         ),
-        in_specs=any_specs(4) + [vmem, vmem],
-        out_specs=(vmem, vmem) + tuple(any_specs(2)),
+        in_specs=any_specs(4) + [vmem] * 5,
+        out_specs=(vmem, vmem) + tuple(any_specs(6)),
         scratch_shapes=[
+            pltpu.VMEM((seq, head), f32),
+            pltpu.VMEM((seq, head), f32),
             pltpu.VMEM(z_in.shape, bf16),
             pltpu.VMEM(blocks, bf16),
             pltpu.VMEM(blocks, bf16),
@@ -1105,17 +1185,13 @@
             dma((3,)),
             dma((3,)),
             dma((STAGES,)),
-            dma((4,)),
+            dma((5,)),
             dma((count,)),
             dma((count,)),
         ],
         compiler_params=pltpu.CompilerParams(collective_id=2, has_side_effects=True, vmem_limit_bytes=VMEM_LIMIT),
         name="back",
-    )(z_in, h_all, dy_all, w_all, cos, sin)[:3]
-
-
-def norm_fwd(row_vals, norm_gain):
-    return row_vals * lax.rsqrt(jnp.mean(row_vals * row_vals, axis=-1, keepdims=True) + NORM_EPS) * norm_gain
+    )(z_in, h_all, dy_all, w_all, cos, sin, x, dy, gain)[:7]
 
 
 def solution(mesh):
@@ -1125,61 +1201,27 @@
     nz = mesh.shape["fsdp"] // NY
 
     def layer_body(x_in, dy_in, norm_gain, w_qkv, w_out, w_gate, w_up, w_down, rope_cos, rope_sin):
-        bf16 = jnp.bfloat16
         _, rows, width = x_in.shape
-        slab = w_qkv.shape[0]
         head = 2 * rope_cos.shape[1]
-        group = w_out.shape[0] // head
         seq = rows * NX * NC
-        ff = w_gate.shape[1] // NY
-
-        x_rows = x_in[0].astype(jnp.float32)
-        normed, norm_pull = jax.vjp(lambda row_vals: norm_fwd(row_vals, norm_gain), x_rows)
-        h_loc = normed.astype(bf16).reshape(2, rows // 2, width)
-        dy_loc = dy_in.reshape(2, rows // 2, width)
-        q, k, v = w_qkv[:, : group * head], w_qkv[:, group * head : -head], w_qkv[:, -head:]
-        out_t, down_t = w_out.T, w_down.T
-        parts = []
-        for i in range(NY):
-            at = slice(i * head, (i + 1) * head)
-            ffs = slice(i * ff, (i + 1) * ff)
-            heads = [q[:, at], out_t[:, at]] if i < NY - 1 else [k, v]
-            parts.append(jnp.concatenate([w_gate[:, ffs], w_up[:, ffs]] + heads + [down_t[:, ffs]], axis=1))
-        w_loc = jnp.stack(parts)
-        cos = jnp.concatenate([rope_cos, rope_cos], axis=1)
-        sin = jnp.concatenate([-rope_sin, rope_sin], axis=1)
-
-        h_all, dy_all, w_all, z_got = front(nz, 2 * head, h_loc, dy_loc, w_loc)
         tokens = NY * seq
-        cols = w_loc.shape[2]
-        h_all = h_all.reshape(tokens, width)
-        dy_all = dy_all.reshape(tokens, width)
-        w_all = w_all.reshape(NC, width, cols)
-        z_got = z_got.reshape(NY, 2, seq // 2, 2 * head)
-        p_sum, q_sum, g_sum = back(nz, z_got, h_all, dy_all, w_all, cos, sin)
-        p_sum = p_sum.reshape(rows, -1)
-        q_sum = q_sum.reshape(rows, -1)
-
-        y_sum = jnp.concatenate([p_sum, q_sum[:, width:]], axis=1)
-        y_out = (x_rows + y_sum).astype(bf16)
-        d_h = q_sum[:, :width].astype(bf16)
-        dx_out = (dy_in[0].astype(jnp.float32) + norm_pull(d_h.astype(jnp.float32))[0]).astype(bf16)
-        lo = 2 * ff
-        mid = lo + head
-        hi = mid + head
-
-        def take(first, end, n=NY):
-            return jnp.concatenate([g_sum[i, :, first:end] for i in range(n)], axis=1)
-
-        return (
-            y_out[None],
-            dx_out[None],
-            jnp.concatenate([take(lo, mid), g_sum[NY - 1, :, mid:hi]], axis=1),
-            take(mid, hi, group).T,
-            take(0, ff),
-            take(ff, lo),
-            take(hi, cols).T,
+        x = x_in.reshape(2, rows // 2, width)
+        dy = dy_in.reshape(2, rows // 2, width)
+        gain = norm_gain.reshape(1, width)
+        h_all, dy_all, w_all, z_got = front(nz, x, dy, gain, w_qkv, w_out.T, w_gate, w_up, w_down.T)
+        y_out, dx_out, g_qkv, g_out, g_gate, g_up, g_down = back(
+            nz,
+            z_got.reshape(NY, 2, seq // 2, 2 * head),
+            h_all.reshape(tokens, width),
+            dy_all.reshape(tokens, width),
+            w_all.reshape(NC, width, -1),
+            rope_cos.T,
+            rope_sin.T,
+            x,
+            dy,
+            gain,
         )
+        return y_out.reshape(x_in.shape), dx_out.reshape(x_in.shape), g_qkv, g_out.T, g_gate, g_up, g_down.T
 
     return jax.shard_map(
         layer_body,

time: 307 us -> 304 us (level)
  other arithmetic: 13.6 us -> 0 us
  local copies, waits for them, and re-layouts: 2.66 us -> 12.1 us
    unnamed x38 -> x7, local copies, waits for them, and re-layouts: 1.39 us -> 12.1 us
where the time goes in v5:
time: 304 us; the launch traced here: 302 us
  Pallas kernels  289 us (95%)
  local copies, waits for them, and re-layouts  12.1 us (4%)
    pallas_call x1, Pallas kernels, back(): pl.pallas_call(functools.partial(back_kernel, nz), out_shape=(jax.ShapeDt...  183 us
    pallas_call x1, Pallas kernels, front(): pl.pallas_call(functools.partial(front_kernel, nz), out_shape=(jax.ShapeD...  106 us
    unnamed x7, local copies, waits for them, and re-layouts  12.1 us

profile of v5, /device:TPU:1, one launch (start us, length us, event | category | flops | bytes accessed | tf_op | source)
XLA Modules:
  0.0 302.2 jit_solution(15356135067072178114)
XLA Ops:
  0.6 106.3 %front.1 = (bf16[4,4,2,2,32,3072]{5,4,3,2,1,0:T(8,128)(2,1)}, bf16[4,4,2,2,32,3072]{5,4,3,2,1,0:T(8,128)(2,1)}, bf16[2,8,4,96,1024]{4,3,2,1,0:T(8,128)(2,1)}, bf16[4,4,128,256]{3,2,1,0:T(8,128)(2,1)}) custom-call(bf16[2,32,3072]{2,1,0:T(8,128)(2,1)} %bitcast.18, bf16[2,32,3072]{2,1,0:T(8,128)(2,1)} %bitcast.20, f32[1,3072]{1,0:T(1,128)} %bitcast.31, ...), custom_call_target="tpu_custom_call" | custom-call | tf_op jit(solution)/shard_map/front/pallas_call | solution.py:434
  107.0 183.2 %back.1 = (bf16[2,32,3072]{2,1,0:T(8,128)(2,1)}, bf16[2,32,3072]{2,1,0:T(8,128)(2,1)}, f32[96,640]{1,0:T(8,128)}, f32[96,384]{1,0:T(8,128)}, f32[96,1024]{1,0:T(...) custom-call(bf16[4,2,256,256]{3,2,1,0:T(8,128)(2,1)} %bitcast.22, ...), custom_call_target="tpu_custom_call" | custom-call | tf_op jit(solution)/shard_map/back/pallas_call | solution.py:1148
  290.1 1.8 copy.24
  291.9 1.8 copy.25
  293.7 1.7 copy.26
  295.3 1.6 copy.27
  296.9 1.8 copy.28
  298.7 1.8 copy.29
  300.4 1.8 copy.30

commit v6 on v5

--- a/solution.py
+++ b/solution.py
@@ -150,12 +150,12 @@
     return pl.ds(pl.multiple_of(q * n, n), n)
 
 
-def exchange(flow, place, src, dst, far, step, done=None):
+def exchange(flow, place, src, dst, far, step, done):
     size = nbytes(src, 1)
 
     def onward(way, half):
         def then():
-            flow.send("y", way, lambda: far.at[half], lambda: dst.at[place.get("y", -way), half], size // 2, done)
+            flow.send("y", way, lambda: far.at[half], lambda: dst.at[place.get("y", -way), half], size // 2, lambda: done(2, half))
 
         return then
 
@@ -163,7 +163,7 @@
         flow.send("y", 1, lambda: src.at[place.get("y", 2), 0], lambda: far.at[0], size // 2, onward(1, 0))
         flow.send("y", -1, lambda: src.at[place.get("y", 2), 1], lambda: far.at[1], size // 2, onward(-1, 1))
     else:
-        flow.send("y", step, lambda: src.at[place.get("y", step)], lambda: dst.at[place.get("y")], size, done)
+        flow.send("y", step, lambda: src.at[place.get("y", step)], lambda: dst.at[place.get("y")], size, lambda: done(-step, None))
 
 
 ORDER = (2, 1, -1, 0)
@@ -182,7 +182,7 @@
         y, x, c = (self.place.get(axis, at.get(axis, 0)) for axis in "yxc")
         return lambda: self.full.at[y, x, c, half, :, self.cut]
 
-    def spread(self, axis, at, half, src):
+    def moves(self, axis, at, half, src):
         def come(step, onward):
             def then():
                 here = dict(at, **{axis: step})
@@ -193,8 +193,14 @@
 
             return then
 
-        self.flow.send(axis, 1, src, self.spot(at, half), self.size, come(-1, half == 0))
-        self.flow.send(axis, -1, src, self.spot(at, half), self.size, come(1, half == 1))
+        return {
+            1: lambda: self.flow.send(axis, 1, src, self.spot(at, half), self.size, come(-1, half == 0)),
+            -1: lambda: self.flow.send(axis, -1, src, self.spot(at, half), self.size, come(1, half == 1)),
+        }
+
+    def spread(self, axis, at, half, src):
+        for move in self.moves(axis, at, half, src).values():
+            move()
 
     def got(self, axis, at, half):
         if axis == self.first:
@@ -207,13 +213,17 @@
         self.flow.send("c", 1, src, self.spot(at, half), self.size, there)
 
     def start_first(self):
+        self.spread_own(self.first)
+
+    def start_second(self):
+        self.spread_own(self.second)
         for half in (0, 1):
-            self.spread(self.first, {}, half, self.mine(half))
-
-    def start_second(self):
-        for half in (0, 1):
-            self.spread(self.second, {}, half, self.mine(half))
             self.pair({}, half, self.mine(half))
+
+    def spread_own(self, axis):
+        sends = {(half, step): move for half in (0, 1) for step, move in self.moves(axis, {}, half, self.mine(half)).items()}
+        for key in ((0, 1), (1, -1), (1, 1), (0, -1)):
+            sends[key]()
 
 
 def front_kernel(
@@ -244,8 +254,11 @@
     hi = lo + pair
     rows = z_in.shape[2]
     flow = Flow(place, send_sem, recv_sem)
-    w_own = pltpu.make_async_copy(w_ref.at[y], w_all.at[0, z, y], own_sem.at[2])
+    w_own = pltpu.make_async_copy(w_ref.at[y, :, :lo], w_all.at[0, z, y, :, :lo], own_sem.at[2])
+    w_own_down = pltpu.make_async_copy(w_ref.at[y, :, hi:], w_all.at[0, z, y, :, hi:], own_sem.at[4 + NX])
     w_own.start()
+    w_own_down.start()
+    heads_home = pltpu.make_async_copy(w_heads, w_all.at[0, :, :, :, lo:hi], own_sem.at[3])
     w_heads[z, y] = w_ref[y, :, lo:hi]
     place.meet([("x", 1), ("x", -1), ("y", 1), ("y", -1), ("y", 2), ("z", 1), ("z", -1), ("c", 1)])
 
@@ -278,6 +291,7 @@
     def weight_come():
         weights[0] -= 1
         if weights[0] == 0:
+            heads_home.start()
             load()
 
     def product(kind, dy, dx, slot):
@@ -326,6 +340,8 @@
             copy = pltpu.make_async_copy(at(), there()(), own_sem.at[4 + dx % NX])
             copy.start()
             own_copies.append(copy)
+        elif dy == 2 and dx in DIRECT:
+            flow.send("y", 2, at, there(), size, link=("y", 1))
         elif dy == 2:
             way = 1 if dx in (0, 2) else -1
 
@@ -402,9 +418,8 @@
         there = arrive(n)
         flow.local(copy, nbytes(ref, 0), lambda n=n, there=there: [there(0, 0) for _ in range((4, 2)[n])])
     flow.run()
-    heads_home = pltpu.make_async_copy(w_heads, w_all.at[0, :, :, :, lo:hi], own_sem.at[3])
     w_own.wait()
-    heads_home.start()
+    w_own_down.wait()
     flow.close()
     for copy in own_copies:
         copy.wait()
@@ -413,6 +428,7 @@
 
 CHUNK_TIME = 1.0
 W_TIMES = (0.0, 0.0)
+DIRECT = (2, 1, -1)
 H_TAIL = 1
 
 
@@ -450,7 +466,7 @@
             pltpu.VMEM((NX, chunk, pair), bf16),
             dma((count,)),
             dma((count,)),
-            dma((4 + NX,)),
+            dma((5 + NX,)),
             dma((slots,)),
         ],
         compiler_params=pltpu.CompilerParams(collective_id=0, has_side_effects=True, vmem_limit_bytes=VMEM_LIMIT),
@@ -872,9 +888,9 @@
     w_all,
     cos_in,
     sin_in,
-    x_ref,
-    dy_ref,
     gain,
+    x_in,
+    dy_in,
     y_out,
     dx_out,
     g_qkv,
@@ -883,6 +899,8 @@
     g_up,
     g_down,
     z_land,
+    x_ref,
+    dy_ref,
     cos_ref,
     sin_ref,
     z_got,
@@ -928,6 +946,7 @@
 
     z_load = pltpu.make_async_copy(z_in, z_got, load_sem)
     z_load.start()
+    row_loads = [pltpu.make_async_copy(a, b, own_sem.at[5 + n]) for n, (a, b) in enumerate(((x_in, x_ref), (dy_in, dy_ref)))]
     cos_ref[...] = jnp.concatenate([cos_in[...], cos_in[...]], axis=0).T
     sin_ref[...] = jnp.concatenate([-sin_in[...], sin_in[...]], axis=0).T
     early = Flow(place, send_sem, recv_sem)
@@ -937,8 +956,11 @@
         early.send("c", 1, lambda: acts.at[q, :, :, other, :, :lo], lambda: pair_acts.at[q, :, :, :, :lo], nbytes(pair_acts, 1) * lo // cols)
         early.send("c", 1, lambda: acts.at[q, :, :, other, :, lo:], lambda: pair_acts.at[q, :, :, :, hi:], nbytes(pair_acts, 1) * ff // cols)
 
-    def all_out():
-        early.send("c", 1, lambda: z_out.at[:, :, :, other], lambda: pair_acts.at[:, :, :, :, lo:hi], nbytes(z_out, 0) // NC)
+    def out_come(step, half):
+        cut = slice(None) if half is None else half
+        part = nbytes(z_out, 1) // NC // (1 if half is None else 2)
+        src = lambda: z_out.at[place.get("y", step), cut, :, other]
+        early.send("c", 1, src, lambda: pair_acts.at[place.get("y", step), cut, :, :, lo:hi], part)
 
     grads = Grads(nz, place, h_all, dy_all, acts, z_out, z_land, (g_gate, g_up, g_down, g_qkv, g_out), far, h_plus, h_minus, dy_minus, tiles, stage, g_load_sem, stage_sem, own_sem)
 
@@ -946,18 +968,22 @@
         begin, go = gated(place, early, h_all, dy_all, w_all, acts, row_sem, share, h_rows, dy_rows, w_v)
         begin()
         grads.begin()
+        for copy in row_loads:
+            copy.start()
         z_load.wait()
         attention(z_got, z_back, keys, vals, dk, dv, cos_ref, sin_ref)
         place.meet(peers)
-        out_done = after(4, all_out)
         for step in ORDER[:3]:
-            exchange(early, place, z_back, z_out, far_back, step, out_done)
+            exchange(early, place, z_back, z_out, far_back, step, out_come)
         z_out[y] = z_back[y]
+        early.send("c", 1, lambda: z_back.at[y, :, :, other], lambda: pair_acts.at[y, :, :, :, lo:hi], nbytes(z_out, 1) // NC)
         go()
         grads.make_first()
         early.now += 2.6
         early.run()
         early.close()
+        for copy in row_loads:
+            copy.wait()
 
     pl.run_scoped(
         first,
@@ -1122,7 +1148,7 @@
     )
 
 
-STAGES = 6
+STAGES = 5
 PASSES = ((1, 0), (0, 0), (0, 1), (1, 1), (1, 2), (0, 2), (0, 3), (1, 3))
 P_TIME = 3.0
 Q_HALF = 2.6
@@ -1142,7 +1168,7 @@
     blocks = (NY, 2, NX // 2, NC, rows, pair)
     p_piece = (rows // 2, width - block)
     q_piece = (rows // 2, width + block)
-    count = 6 + 2 * NY + 1 + 4 * (nz - 1) + 5 * 4 + 2 * 5 * 6
+    count = 6 + 2 * NY + 5 + 4 * (nz - 1) + 5 * 4 + 2 * 5 * 6
     slab = block // NY
     weight = jax.ShapeDtypeStruct((slab, NY * ff), f32)
     return pl.pallas_call(
@@ -1157,9 +1183,11 @@
             weight,
             jax.ShapeDtypeStruct((nz - 1, 4, block, ff), f32),
         ),
-        in_specs=any_specs(4) + [vmem] * 5,
+        in_specs=any_specs(4) + [vmem] * 3 + any_specs(2),
         out_specs=(vmem, vmem) + tuple(any_specs(6)),
         scratch_shapes=[
+            pltpu.VMEM(x.shape, bf16),
+            pltpu.VMEM(x.shape, bf16),
             pltpu.VMEM((seq, head), f32),
             pltpu.VMEM((seq, head), f32),
             pltpu.VMEM(z_in.shape, bf16),
@@ -1185,13 +1213,40 @@
             dma((3,)),
             dma((3,)),
             dma((STAGES,)),
-            dma((5,)),
+            dma((7,)),
             dma((count,)),
             dma((count,)),
         ],
         compiler_params=pltpu.CompilerParams(collective_id=2, has_side_effects=True, vmem_limit_bytes=VMEM_LIMIT),
         name="back",
-    )(z_in, h_all, dy_all, w_all, cos, sin, x, dy, gain)[:7]
+    )(z_in, h_all, dy_all, w_all, cos, sin, gain, x, dy)[:7]
+
+
+def settle_kernel(*refs):
+    n = len(refs) // 3
+    ins, outs, held = refs[:n], refs[n : 2 * n], refs[2 * n : 3 * n]
+    in_sem, out_sem = refs[3 * n :]
+    come = [pltpu.make_async_copy(a, b, in_sem.at[i]) for i, (a, b) in enumerate(zip(ins, held))]
+    go = [pltpu.make_async_copy(a, b, out_sem.at[i]) for i, (a, b) in enumerate(zip(held, outs))]
+    for copy in come:
+        copy.start()
+    for first, second in zip(come, go):
+        first.wait()
+        second.start()
+    for copy in go:
+        copy.wait()
+
+
+def settle(arrays):
+    n = len(arrays)
+    return pl.pallas_call(
+        settle_kernel,
+        out_shape=tuple(jax.ShapeDtypeStruct(a.shape, a.dtype) for a in arrays),
+        in_specs=any_specs(n),
+        out_specs=tuple(any_specs(n)),
+        scratch_shapes=[pltpu.VMEM(a.shape, a.dtype) for a in arrays] + [pltpu.SemaphoreType.DMA((n,))] * 2,
+        name="settle",
+    )(*arrays)
 
 
 def solution(mesh):
@@ -1209,7 +1264,7 @@
         dy = dy_in.reshape(2, rows // 2, width)
         gain = norm_gain.reshape(1, width)
         h_all, dy_all, w_all, z_got = front(nz, x, dy, gain, w_qkv, w_out.T, w_gate, w_up, w_down.T)
-        y_out, dx_out, g_qkv, g_out, g_gate, g_up, g_down = back(
+        results = back(
             nz,
             z_got.reshape(NY, 2, seq // 2, 2 * head),
             h_all.reshape(tokens, width),
@@ -1221,6 +1276,7 @@
             dy,
             gain,
         )
+        y_out, dx_out, g_qkv, g_out, g_gate, g_up, g_down = settle(results)
         return y_out.reshape(x_in.shape), dx_out.reshape(x_in.shape), g_qkv, g_out.T, g_gate, g_up, g_down.T
 
     return jax.shard_map(

time: 304 us -> 292 us (0.961)
  local copies, waits for them, and re-layouts: 12.1 us -> 0 us
    unnamed x7 -> x0, local copies, waits for them, and re-layouts: 12.1 us -> none
    pallas_call x1, Pallas kernels: 106 us -> 102 us  [front(): pl.pallas_call(functools.partial(front_kernel, nz), out_shape=(jax.ShapeD...]
where the time goes in v6:
time: 292 us; the launch traced here: 291 us
  Pallas kernels  290 us (99%)
    pallas_call x1, Pallas kernels, back(): pl.pallas_call(functools.partial(back_kernel, nz), out_shape=(jax.ShapeDt...  185 us
    pallas_call x1, Pallas kernels, front(): pl.pallas_call(functools.partial(front_kernel, nz), out_shape=(jax.ShapeD...  102 us

profile of v6, /device:TPU:1, one launch (start us, length us, event | category | flops | bytes accessed | tf_op | source)
XLA Modules:
  0.0 290.7 jit_solution(5472167726429925842)
XLA Ops:
  0.6 102.0 %front.1 = (bf16[4,4,2,2,32,3072]{5,4,3,2,1,0:T(8,128)(2,1)}, bf16[4,4,2,2,32,3072]{5,4,3,2,1,0:T(8,128)(2,1)}, bf16[2,8,4,96,1024]{4,3,2,1,0:T(8,128)(2,1)}, bf16[4,4,128,256]{3,2,1,0:T(8,128)(2,1)}) custom-call(bf16[2,32,3072]{2,1,0:T(8,128)(2,1)} %bitcast.18, bf16[2,32,3072]{2,1,0:T(8,128)(2,1)} %bitcast.20, f32[1,3072]{1,0:T(1,128)} %bitcast.27, ...), custom_call_target="tpu_custom_call" | custom-call | tf_op jit(solution)/shard_map/front/pallas_call | solution.py:450
  102.7 185.3 %back.1 = (bf16[2,32,3072]{2,1,0:T(8,128)(2,1)}, bf16[2,32,3072]{2,1,0:T(8,128)(2,1)}, f32[96,640]{1,0:T(8,128)}, f32[96,384]{1,0:T(8,128)}, f32[96,1024]{1,0:T(...) custom-call(bf16[4,2,256,256]{3,2,1,0:T(8,128)(2,1)} %bitcast.22, ...), custom_call_target="tpu_custom_call" | custom-call | tf_op jit(solution)/shard_map/back/pallas_call | solution.py:1174
  288.0 2.5 settle.1

commit v7 on v6

--- a/solution.py
+++ b/solution.py
@@ -12,9 +12,9 @@
 NY, NX, NC = 4, 4, 2
 MESH = pl.DeviceIdType.MESH
 LINK = 46.6e3
-PAIR = 330e3
+PAIR = 450e3
 LOCAL = 1500e3
-HOP = 3.5
+HOP = 3.1
 ADD = 0.4
 VMEM_LIMIT = 67043328
 
@@ -227,7 +227,7 @@
 
 
 def front_kernel(
-    nz, x_ref, dy_ref, gain, w_qkv, w_out, w_gate, w_up, w_down, h_all, dy_all, w_all, z_got, h_ref, w_ref, w_heads, rows_v, z_in, far, send_sem, recv_sem, own_sem, rows_sem
+    nz, x_ref, dy_ref, gain, w_qkv, w_out, w_gate, w_up, w_down, h_all, dy_all, w_all, z_got, h_ref, w_ref, w_heads, h_v, dy_v, z_in, far, send_sem, recv_sem, own_sem, rows_sem
 ):
     bf16 = jnp.bfloat16
     place = Place(nz)
@@ -262,19 +262,26 @@
     w_heads[z, y] = w_ref[y, :, lo:hi]
     place.meet([("x", 1), ("x", -1), ("y", 1), ("y", -1), ("y", 2), ("z", 1), ("z", -1), ("c", 1)])
 
-    slots = rows_v.shape[0]
-    free, queue, ready = list(range(slots)), [], []
+    queue = []
     pieces = {}
     parts_done = {}
     weights = [4 * nz]
+    writes = []
 
     def load():
-        while free and queue and weights[0] == 0:
-            kind, dy, dx = queue.pop(0)
-            slot = free.pop(0)
-            src = (h_all, dy_all)[kind].at[place.get("y", dy), place.get("x", dx)]
-            copy = pltpu.make_async_copy(src, rows_v.at[slot], rows_sem.at[slot])
-            flow.local(copy, nbytes(rows_v, 1), lambda slot=slot, kind=kind, dy=dy, dx=dx: flow.task(CHUNK_TIME, lambda: product(kind, dy, dx, slot)))
+        while queue and weights[0] == 0:
+            key = queue.pop(0)
+            flow.task(CHUNK_TIME, lambda key=key: product(*key))
+
+    def complete(key):
+        kind, dy, dx = key
+        src, dst = ((h_v, h_all), (dy_v, dy_all))[kind]
+        at = place.get("y", dy), place.get("x", dx)
+        copy = pltpu.make_async_copy(src.at[at], dst.at[at], rows_sem.at[len(writes)])
+        copy.start()
+        writes.append(copy)
+        queue.append(key)
+        load()
 
     def arrive(kind):
         need = (8, 4)[kind]
@@ -283,8 +290,7 @@
             key = (kind, dy, dx)
             pieces[key] = pieces.get(key, 0) + 1
             if pieces[key] == need:
-                queue.append(key)
-                load()
+                complete(key)
 
         return one
 
@@ -294,14 +300,15 @@
             heads_home.start()
             load()
 
-    def product(kind, dy, dx, slot):
+    def product(kind, dy, dx):
+        rows_v = (h_v, dy_v)[kind]
         at = place.get("y", dy), place.get("x", dx)
         step = 2 if nz % 2 == 0 else 1
         deep = step * (width // nz)
 
         def dot(first):
             def some(i, total):
-                left = rows_v[slot, :, :, :, span(i, deep)].reshape(rows, deep)
+                left = rows_v[at[0], at[1], :, :, :, span(i, deep)].reshape(rows, deep)
                 right = w_heads[pl.ds(i * step, step), :, :, first:].reshape(deep, pair - first)
                 return total + mm(left, right, 1, 0)
 
@@ -321,8 +328,6 @@
             def _():
                 z_in[at[0], at[1], :, head:] = dot(head).astype(bf16)
 
-        free.append(slot)
-        load()
         parts_done[dy, dx] = parts_done.get((dy, dx), 0) + 1
         if parts_done[dy, dx] == 2:
             deliver(dy, dx)
@@ -389,9 +394,9 @@
 
     tail = width // nz * H_TAIL
     gathers = [
-        Gather(place, flow, h_ref, h_all, "x", slice(0, width - tail), arrive(0)),
-        Gather(place, flow, dy_ref, dy_all, "y", slice(0, width), arrive(1)),
-        Gather(place, flow, h_ref, h_all, "y", slice(width - tail, width), arrive(0)),
+        Gather(place, flow, h_ref, h_v, "x", slice(0, width - tail), arrive(0)),
+        Gather(place, flow, dy_ref, dy_v, "y", slice(0, width), arrive(1)),
+        Gather(place, flow, h_ref, h_v, "y", slice(width - tail, width), arrive(0)),
     ]
     def w_start(n_cut, dys):
         cut = cuts[n_cut]
@@ -413,22 +418,22 @@
     flow.at(W_TIMES[1], lambda: [w_start(1, (1, 2)), w_start(2, (1, 2))])
     for one in gathers:
         one.start_second()
-    for n, (ref, full) in enumerate(((h_ref, h_all), (dy_ref, dy_all))):
-        copy = pltpu.make_async_copy(ref, full.at[y, x, c], own_sem.at[n])
-        there = arrive(n)
-        flow.local(copy, nbytes(ref, 0), lambda n=n, there=there: [there(0, 0) for _ in range((4, 2)[n])])
+    for n, (ref, full) in enumerate(((h_ref, h_v), (dy_ref, dy_v))):
+        full[y, x, c] = ref[...]
+        for _ in range((4, 2)[n]):
+            arrive(n)(0, 0)
     flow.run()
     w_own.wait()
     w_own_down.wait()
     flow.close()
-    for copy in own_copies:
+    for copy in own_copies + writes:
         copy.wait()
     heads_home.wait()
 
 
 CHUNK_TIME = 1.0
 W_TIMES = (0.0, 0.0)
-DIRECT = (2, 1, -1)
+DIRECT = (2,)
 H_TAIL = 1
 
 
@@ -446,7 +451,6 @@
     dma = pltpu.SemaphoreType.DMA
     chunk = NC * half * rows
     z_shape = (NY, NX, chunk, pair)
-    slots = 8
     return pl.pallas_call(
         functools.partial(front_kernel, nz),
         out_shape=(
@@ -461,13 +465,14 @@
             pltpu.VMEM(x.shape, bf16),
             pltpu.VMEM(w_shape, bf16),
             pltpu.VMEM((nz,) + w_shape[:-1] + (pair,), bf16),
-            pltpu.VMEM((slots, NC) + x.shape, bf16),
+            pltpu.VMEM(everywhere, bf16),
+            pltpu.VMEM(everywhere, bf16),
             pltpu.VMEM(z_shape, bf16),
             pltpu.VMEM((NX, chunk, pair), bf16),
             dma((count,)),
             dma((count,)),
             dma((5 + NX,)),
-            dma((slots,)),
+            dma((2 * NY * NX,)),
         ],
         compiler_params=pltpu.CompilerParams(collective_id=0, has_side_effects=True, vmem_limit_bytes=VMEM_LIMIT),
         name="front",

time: 292 us -> 290 us (level)
  no operation moved by 1% of the time
where the time goes in v7:
time: 290 us; the launch traced here: 289 us
  Pallas kernels  288 us (99%)
    pallas_call x1, Pallas kernels, back(): pl.pallas_call(functools.partial(back_kernel, nz), out_shape=(jax.ShapeDt...  184 us
    pallas_call x1, Pallas kernels, front(): pl.pallas_call(functools.partial(front_kernel, nz), out_shape=(jax.ShapeD...  102 us

profile of v7, /device:TPU:1, one launch (start us, length us, event | category | flops | bytes accessed | tf_op | source)
XLA Modules:
  0.0 288.6 jit_solution(17179295434062769224)
XLA Ops:
  0.6 101.7 %front.1 = (bf16[4,4,2,2,32,3072]{5,4,3,2,1,0:T(8,128)(2,1)}, bf16[4,4,2,2,32,3072]{5,4,3,2,1,0:T(8,128)(2,1)}, bf16[2,8,4,96,1024]{4,3,2,1,0:T(8,128)(2,1)}, bf16[4,4,128,256]{3,2,1,0:T(8,128)(2,1)}) custom-call(bf16[2,32,3072]{2,1,0:T(8,128)(2,1)} %bitcast.18, bf16[2,32,3072]{2,1,0:T(8,128)(2,1)} %bitcast.20, f32[1,3072]{1,0:T(1,128)} %bitcast.27, ...), custom_call_target="tpu_custom_call" | custom-call | tf_op jit(solution)/shard_map/front/pallas_call | solution.py:454
  102.4 183.6 %back.1 = (bf16[2,32,3072]{2,1,0:T(8,128)(2,1)}, bf16[2,32,3072]{2,1,0:T(8,128)(2,1)}, f32[96,640]{1,0:T(8,128)}, f32[96,384]{1,0:T(8,128)}, f32[96,1024]{1,0:T(...) custom-call(bf16[4,2,256,256]{3,2,1,0:T(8,128)(2,1)} %bitcast.22, ...), custom_call_target="tpu_custom_call" | custom-call | tf_op jit(solution)/shard_map/back/pallas_call | solution.py:1179
  285.9 2.5 settle.1

commit v8 on v7

--- a/solution.py
+++ b/solution.py
@@ -14,6 +14,7 @@
 LINK = 46.6e3
 PAIR = 450e3
 LOCAL = 1500e3
+LEFT = 2.0
 HOP = 3.1
 ADD = 0.4
 VMEM_LIMIT = 67043328
@@ -34,18 +35,21 @@
         at[axis] = self.get(axis, step)
         return {"fsdp": at["z"] * NY + at["y"], "model": at["x"] * NC + at["c"]}
 
-    def meet(self, peers):
+    def greet(self, peers):
         barrier = pltpu.get_barrier_semaphore()
         for axis, step in peers:
             pl.semaphore_signal(barrier, inc=1, device_id=self.device(axis, step), device_id_type=MESH)
-        pl.semaphore_wait(barrier, len(peers))
+        self.met = len(peers)
+
+    def meet(self):
+        pl.semaphore_wait(pltpu.get_barrier_semaphore(), self.met)
 
 
 class Flow:
     def __init__(self, place, send_sem, recv_sem, base=0, now=0.0):
         self.place, self.send_sem, self.recv_sem, self.base = place, send_sem, recv_sem, base
         self.now, self.free, self.events, self.copies, self.tasks, self.order = now, {}, [], [], [], 0
-        self.sent = set()
+        self.sent, self.leaving = set(), []
 
     def event(self, when, wait, then):
         heapq.heappush(self.events, (when, self.order, wait, then))
@@ -76,6 +80,7 @@
             pl.when(jnp.logical_not(when))(copy.start)
             pl.when(when)(make(other).start)
         self.copies.append(copy)
+        heapq.heappush(self.leaving, (self.free[link] + LEFT, k))
         self.event(self.free[link] + lag, copy.wait_recv, then)
         return k
 
@@ -91,6 +96,9 @@
 
     def take(self):
         when, _, wait, then = heapq.heappop(self.events)
+        if when > self.now:
+            while self.leaving and self.leaving[0][0] <= self.now:
+                self.wait_sent(heapq.heappop(self.leaving)[1])
         self.now = max(self.now, when)
         wait()
         if then is not None:
@@ -231,6 +239,7 @@
 ):
     bf16 = jnp.bfloat16
     place = Place(nz)
+    place.greet([("x", 1), ("x", -1), ("y", 1), ("y", -1), ("y", 2), ("z", 1), ("z", -1), ("c", 1)])
     for half in range(2):
         wide = x_ref[half].astype(jnp.float32)
         h_ref[half] = (wide * lax.rsqrt(jnp.mean(wide * wide, axis=-1, keepdims=True) + NORM_EPS) * gain[...]).astype(bf16)
@@ -260,7 +269,9 @@
     w_own_down.start()
     heads_home = pltpu.make_async_copy(w_heads, w_all.at[0, :, :, :, lo:hi], own_sem.at[3])
     w_heads[z, y] = w_ref[y, :, lo:hi]
-    place.meet([("x", 1), ("x", -1), ("y", 1), ("y", -1), ("y", 2), ("z", 1), ("z", -1), ("c", 1)])
+    for full, ref in ((h_v, h_ref), (dy_v, dy_ref)):
+        full[y, x, c] = ref[...]
+    place.meet()
 
     queue = []
     pieces = {}
@@ -418,8 +429,7 @@
     flow.at(W_TIMES[1], lambda: [w_start(1, (1, 2)), w_start(2, (1, 2))])
     for one in gathers:
         one.start_second()
-    for n, (ref, full) in enumerate(((h_ref, h_v), (dy_ref, dy_v))):
-        full[y, x, c] = ref[...]
+    for n in range(2):
         for _ in range((4, 2)[n]):
             arrive(n)(0, 0)
     flow.run()
@@ -949,13 +959,13 @@
     block = width // nz
     part = seq // 2
 
+    place.greet([("x", 1), ("x", -1), ("y", 1), ("y", -1), ("z", 1), ("z", -1), ("c", 1)])
     z_load = pltpu.make_async_copy(z_in, z_got, load_sem)
     z_load.start()
     row_loads = [pltpu.make_async_copy(a, b, own_sem.at[5 + n]) for n, (a, b) in enumerate(((x_in, x_ref), (dy_in, dy_ref)))]
     cos_ref[...] = jnp.concatenate([cos_in[...], cos_in[...]], axis=0).T
     sin_ref[...] = jnp.concatenate([-sin_in[...], sin_in[...]], axis=0).T
     early = Flow(place, send_sem, recv_sem)
-    peers = [("x", 1), ("x", -1), ("y", 1), ("y", -1), ("z", 1), ("z", -1), ("c", 1)]
 
     def share(q):
         early.send("c", 1, lambda: acts.at[q, :, :, other, :, :lo], lambda: pair_acts.at[q, :, :, :, :lo], nbytes(pair_acts, 1) * lo // cols)
@@ -977,7 +987,7 @@
             copy.start()
         z_load.wait()
         attention(z_got, z_back, keys, vals, dk, dv, cos_ref, sin_ref)
-        place.meet(peers)
+        place.meet()
         for step in ORDER[:3]:
             exchange(early, place, z_back, z_out, far_back, step, out_come)
         z_out[y] = z_back[y]

time: 290 us -> 286 us (0.986)
  Pallas kernels: 288 us -> 284 us
where the time goes in v8:
time: 286 us; the launch traced here: 285 us
  Pallas kernels  284 us (99%)
    pallas_call x1, Pallas kernels, back(): pl.pallas_call(functools.partial(back_kernel, nz), out_shape=(jax.ShapeDt...  181 us
    pallas_call x1, Pallas kernels, front(): pl.pallas_call(functools.partial(front_kernel, nz), out_shape=(jax.ShapeD...  101 us

profile of v8, /device:TPU:1, one launch (start us, length us, event | category | flops | bytes accessed | tf_op | source)
XLA Modules:
  0.0 285.1 jit_solution(11131858148917734754)
XLA Ops:
  0.6 100.9 %front.1 = (bf16[4,4,2,2,32,3072]{5,4,3,2,1,0:T(8,128)(2,1)}, bf16[4,4,2,2,32,3072]{5,4,3,2,1,0:T(8,128)(2,1)}, bf16[2,8,4,96,1024]{4,3,2,1,0:T(8,128)(2,1)}, bf16[4,4,128,256]{3,2,1,0:T(8,128)(2,1)}) custom-call(bf16[2,32,3072]{2,1,0:T(8,128)(2,1)} %bitcast.18, bf16[2,32,3072]{2,1,0:T(8,128)(2,1)} %bitcast.20, f32[1,3072]{1,0:T(1,128)} %bitcast.27, ...), custom_call_target="tpu_custom_call" | custom-call | tf_op jit(solution)/shard_map/front/pallas_call | solution.py:464
  101.5 180.9 %back.1 = (bf16[2,32,3072]{2,1,0:T(8,128)(2,1)}, bf16[2,32,3072]{2,1,0:T(8,128)(2,1)}, f32[96,640]{1,0:T(8,128)}, f32[96,384]{1,0:T(8,128)}, f32[96,1024]{1,0:T(...) custom-call(bf16[4,2,256,256]{3,2,1,0:T(8,128)(2,1)} %bitcast.22, ...), custom_call_target="tpu_custom_call" | custom-call | tf_op jit(solution)/shard_map/back/pallas_call | solution.py:1189
  282.4 2.5 settle.1

commit v9 on v8

--- a/solution.py
+++ b/solution.py
@@ -235,14 +235,29 @@
 
 
 def front_kernel(
-    nz, x_ref, dy_ref, gain, w_qkv, w_out, w_gate, w_up, w_down, h_all, dy_all, w_all, z_got, h_ref, w_ref, w_heads, h_v, dy_v, z_in, far, send_sem, recv_sem, own_sem, rows_sem
+    nz, x_in, dy_in, gain, *refs
 ):
+    args, refs = refs[:5], refs[5:]
+    held, refs = refs[-8:-1], refs[:-8] + refs[-1:]
+    front_body(nz, (x_in, dy_in) + args, held, gain, *refs)
+
+
+def front_body(
+    nz, ins, held, gain, h_all, dy_all, w_all, z_got, h_ref, w_ref, w_heads, h_v, dy_v, z_in, far, send_sem, recv_sem, own_sem, rows_sem, in_sem
+):
+    x_ref, dy_ref, w_qkv, w_out, w_gate, w_up, w_down = held
+    in_copies = [pltpu.make_async_copy(a, b, in_sem.at[n]) for n, (a, b) in enumerate(zip(ins, held))]
+    for copy in in_copies:
+        copy.start()
     bf16 = jnp.bfloat16
     place = Place(nz)
     place.greet([("x", 1), ("x", -1), ("y", 1), ("y", -1), ("y", 2), ("z", 1), ("z", -1), ("c", 1)])
+    in_copies[0].wait()
     for half in range(2):
         wide = x_ref[half].astype(jnp.float32)
         h_ref[half] = (wide * lax.rsqrt(jnp.mean(wide * wide, axis=-1, keepdims=True) + NORM_EPS) * gain[...]).astype(bf16)
+    for copy in in_copies[1:]:
+        copy.wait()
     wide_ff = w_gate.shape[1] // NY
     one = w_out.shape[1] // (NY - 1)
     for q in range(NY):
@@ -469,7 +484,7 @@
             jax.ShapeDtypeStruct((NC, nz) + w_shape, bf16),
             jax.ShapeDtypeStruct(z_shape, bf16),
         ),
-        in_specs=[vmem] * 8,
+        in_specs=any_specs(2) + [vmem] + any_specs(5),
         out_specs=tuple(any_specs(4)),
         scratch_shapes=[
             pltpu.VMEM(x.shape, bf16),
@@ -483,6 +498,10 @@
             dma((count,)),
             dma((5 + NX,)),
             dma((2 * NY * NX,)),
+        ]
+        + [pltpu.VMEM(a.shape, bf16) for a in (x, dy, w_qkv, w_out, w_gate, w_up, w_down)]
+        + [
+            dma((7,)),
         ],
         compiler_params=pltpu.CompilerParams(collective_id=0, has_side_effects=True, vmem_limit_bytes=VMEM_LIMIT),
         name="front",
@@ -936,12 +955,16 @@
     dy_minus,
     tiles,
     stage,
+    w_v,
+    y_v,
+    dx_v,
     load_sem,
     row_sem,
     w_sem,
     g_load_sem,
     stage_sem,
     own_sem,
+    out_sem,
     send_sem,
     recv_sem,
 ):
@@ -967,6 +990,21 @@
     sin_ref[...] = jnp.concatenate([-sin_in[...], sin_in[...]], axis=0).T
     early = Flow(place, send_sem, recv_sem)
 
+    depth = w_v.shape[0]
+
+    def w_copy(kind, d, slot):
+        at = pl.ds(pl.multiple_of(d * block, block), block)
+        cut = slice(lo, cols) if kind == 0 else slice(0, cols)
+        return pltpu.make_async_copy(w_all.at[:, at, cut], w_v.at[slot, :, :, cut], w_sem.at[slot])
+
+    counts = (nz - 1, nz)
+    base, total = [], 0
+    for kind, _ in PASSES:
+        base.append(total)
+        total += counts[kind]
+    kind = PASSES[0][0]
+    for n in range(depth):
+        w_copy(kind, n, n).start() if n < counts[kind] else w_copy(PASSES[1][0], n - counts[kind], n).start()
     def share(q):
         early.send("c", 1, lambda: acts.at[q, :, :, other, :, :lo], lambda: pair_acts.at[q, :, :, :, :lo], nbytes(pair_acts, 1) * lo // cols)
         early.send("c", 1, lambda: acts.at[q, :, :, other, :, lo:], lambda: pair_acts.at[q, :, :, :, hi:], nbytes(pair_acts, 1) * ff // cols)
@@ -1007,7 +1045,7 @@
         pltpu.VMEM((width, 3 * ff), bf16),
     )
 
-    def second(p_tile, q_tile, w_v):
+    def second(p_tile, q_tile):
         flow = Flow(place, send_sem, recv_sem, len(early.copies), early.now)
         grads.flow = flow
         lane = lax.broadcasted_iota(jnp.int32, (rows, pair), 1)
@@ -1028,21 +1066,6 @@
             grad, mixed, _ = chunk(k, i, p, xx)
             return jnp.concatenate([grad, jnp.where(for_d, mixed, jnp.zeros_like(mixed))], axis=1)
 
-        depth = w_v.shape[0]
-
-        def w_copy(kind, d, slot):
-            at = pl.ds(pl.multiple_of(d * block, block), block)
-            cut = slice(lo, cols) if kind == 0 else slice(0, cols)
-            return pltpu.make_async_copy(w_all.at[:, at, cut], w_v.at[slot, :, :, cut], w_sem.at[slot])
-
-        counts = (nz - 1, nz)
-        base, total = [], 0
-        for kind, _ in PASSES:
-            base.append(total)
-            total += counts[kind]
-        kind = PASSES[0][0]
-        for n in range(depth):
-            w_copy(kind, n, n).start() if n < counts[kind] else w_copy(PASSES[1][0], n - counts[kind], n).start()
         turn = [0]
 
         def blocks(s, kind, first, count, body):
@@ -1122,17 +1145,29 @@
             flow.task(Q_HALF, end)
 
         edge = width - block
+        result_copies = []
+
+        def leave(n, half):
+            copy = pltpu.make_async_copy((y_v, dx_v)[n].at[half], (y_out, dx_out)[n].at[half], out_sem.at[n, half])
+            copy.start()
+            result_copies.append(copy)
+
+        y_done = [after(2, functools.partial(leave, 0, half)) for half in range(2)]
+
         def p_finish(half, ref):
-            y_out[half, :, :edge] = (x_ref[half, :, :edge].astype(f32) + ref()[...]).astype(bf16)
+            y_v[half, :, :edge] = (x_ref[half, :, :edge].astype(f32) + ref()[...]).astype(bf16)
+            y_done[half]()
 
         def q_finish(half, ref):
-            y_out[half, :, edge:] = (x_ref[half, :, edge:].astype(f32) + ref()[:, width:]).astype(bf16)
+            y_v[half, :, edge:] = (x_ref[half, :, edge:].astype(f32) + ref()[:, width:]).astype(bf16)
+            y_done[half]()
             wide = x_ref[half].astype(f32)
             scale = lax.rsqrt(jnp.mean(wide * wide, axis=-1, keepdims=True) + NORM_EPS)
             d_normed = ref()[:, :width].astype(bf16).astype(f32) * gain[...]
             mean = jnp.mean(d_normed * wide, axis=-1, keepdims=True)
             grad = d_normed * scale - wide * (scale * scale * scale * mean)
-            dx_out[half] = (dy_ref[half].astype(f32) + grad).astype(bf16)
+            dx_v[half] = (dy_ref[half].astype(f32) + grad).astype(bf16)
+            leave(1, half)
 
         def free(task):
             return lambda s: task(s + 2) if s + 2 < len(SETS) else None
@@ -1154,12 +1189,13 @@
         flow.run()
         flow.close()
         grads.close()
+        for copy in result_copies:
+            copy.wait()
 
     pl.run_scoped(
         second,
         pltpu.VMEM((2, NY, 2, rows // 2, width - block), f32),
         pltpu.VMEM((2, NX, 2, rows // 2, width + block), f32),
-        pltpu.VMEM((3, NC, block, cols), bf16),
     )
 
 
@@ -1199,7 +1235,7 @@
             jax.ShapeDtypeStruct((nz - 1, 4, block, ff), f32),
         ),
         in_specs=any_specs(4) + [vmem] * 3 + any_specs(2),
-        out_specs=(vmem, vmem) + tuple(any_specs(6)),
+        out_specs=tuple(any_specs(8)),
         scratch_shapes=[
             pltpu.VMEM(x.shape, bf16),
             pltpu.VMEM(x.shape, bf16),
@@ -1223,12 +1259,16 @@
             pltpu.VMEM((tokens, block), bf16),
             pltpu.VMEM((2, 4, block, ff), f32),
             pltpu.VMEM((STAGES, block, ff), f32),
+            pltpu.VMEM((3, NC, block, cols), bf16),
+            pltpu.VMEM(x.shape, bf16),
+            pltpu.VMEM(x.shape, bf16),
             dma,
             dma((3, 2)),
             dma((3,)),
             dma((3,)),
             dma((STAGES,)),
             dma((7,)),
+            dma((2, 2)),
             dma((count,)),
             dma((count,)),
         ],

time: 286 us -> 285 us (level)
  no operation moved by 1% of the time
where the time goes in v9:
time: 285 us; the launch traced here: 284 us
  Pallas kernels  283 us (99%)
    pallas_call x1, Pallas kernels, back(): pl.pallas_call(functools.partial(back_kernel, nz), out_shape=(jax.ShapeDt...  180 us
    pallas_call x1, Pallas kernels, front(): pl.pallas_call(functools.partial(front_kernel, nz), out_shape=(jax.ShapeD...  100 us

profile of v9, /device:TPU:1, one launch (start us, length us, event | category | flops | bytes accessed | tf_op | source)
XLA Modules:
  0.0 283.7 jit_solution(4592558406034958291)
XLA Ops:
  0.6 100.2 %front.1 = (bf16[4,4,2,2,32,3072]{5,4,3,2,1,0:T(8,128)(2,1)}, bf16[4,4,2,2,32,3072]{5,4,3,2,1,0:T(8,128)(2,1)}, bf16[2,8,4,96,1024]{4,3,2,1,0:T(8,128)(2,1)}, bf16[4,4,128,256]{3,2,1,0:T(8,128)(2,1)}) custom-call(bf16[2,32,3072]{2,1,0:T(8,128)(2,1)} %bitcast.18, bf16[2,32,3072]{2,1,0:T(8,128)(2,1)} %bitcast.20, f32[1,3072]{1,0:T(1,128)} %bitcast.27, ...), custom_call_target="tpu_custom_call" | custom-call | tf_op jit(solution)/shard_map/front/pallas_call | solution.py:479
  100.9 180.1 %back.1 = (bf16[2,32,3072]{2,1,0:T(8,128)(2,1)}, bf16[2,32,3072]{2,1,0:T(8,128)(2,1)}, f32[96,640]{1,0:T(8,128)}, f32[96,384]{1,0:T(8,128)}, f32[96,1024]{1,0:T(...) custom-call(bf16[4,2,256,256]{3,2,1,0:T(8,128)(2,1)} %bitcast.22, ...), custom_call_target="tpu_custom_call" | custom-call | tf_op jit(solution)/shard_map/back/pallas_call | solution.py:1225
  281.0 2.5 settle.1

commit v10 on v9

--- a/solution.py
+++ b/solution.py
@@ -158,23 +158,16 @@
     return pl.ds(pl.multiple_of(q * n, n), n)
 
 
-def exchange(flow, place, src, dst, far, step, done):
-    size = nbytes(src, 1)
-
-    def onward(way, half):
-        def then():
-            flow.send("y", way, lambda: far.at[half], lambda: dst.at[place.get("y", -way), half], size // 2, lambda: done(2, half))
-
-        return then
-
-    if step == 2:
-        flow.send("y", 1, lambda: src.at[place.get("y", 2), 0], lambda: far.at[0], size // 2, onward(1, 0))
-        flow.send("y", -1, lambda: src.at[place.get("y", 2), 1], lambda: far.at[1], size // 2, onward(-1, 1))
-    else:
-        flow.send("y", step, lambda: src.at[place.get("y", step)], lambda: dst.at[place.get("y")], size, lambda: done(-step, None))
-
-
-ORDER = (2, 1, -1, 0)
+def exchange(flow, place, src, dst, far, half, done):
+    size = nbytes(src, 2)
+    way = (1, -1)[half]
+
+    def onward():
+        flow.send("y", way, lambda: far.at[half], lambda: dst.at[place.get("y", -way), half], size, lambda: done(2, half))
+
+    flow.send("y", way, lambda: src.at[place.get("y", 2), half], lambda: far.at[half], size, onward)
+    for step in (-way, way):
+        flow.send("y", step, lambda step=step: src.at[place.get("y", step), half], lambda: dst.at[place.get("y"), half], size, lambda step=step: done(-step, half))
 
 
 class Gather:
@@ -511,7 +504,7 @@
 SETS = (2, 1, -1, 0)
 
 
-def attention(z_got, z_back, keys, vals, dk, dv, cos_ref, sin_ref):
+def attention(z_got, z_back, keys, vals, dk, dv, cos_ref, sin_ref, leave):
     bf16 = jnp.bfloat16
     seq, head = keys.shape
     part = seq // 2
@@ -531,10 +524,11 @@
     dk[...] = jnp.zeros_like(dk)
     dv[...] = jnp.zeros_like(dv)
 
-    @pl.loop(0, count)
-    def _(i):
-        for p in range(2):
-            n = (p + 1) * part
+    for p in (1, 0):
+        n = (p + 1) * part
+
+        @pl.loop(0, count)
+        def _(i):
             query = turn(z_got[i, p, :, :head], halves[p], 1.0)
             d_out = z_got[i, p, :, head:]
             scores = mm(query, keys[:n, :], 1, 1) * scale
@@ -550,9 +544,9 @@
             dk[:n, :] += mm(d_scores, query, 0, 0)
             dv[:n, :] += mm(probs_low, d_out, 0, 0)
 
-    for p in range(2):
         z_back[count, p, :, :, :, :head] = turn(dk[halves[p], :].astype(bf16), halves[p], -1.0).reshape(spread)
         z_back[count, p, :, :, :, head:] = dv[halves[p], :].astype(bf16).reshape(spread)
+        leave(p)
 
 
 def gated(place, flow, h_all, dy_all, w_all, acts, row_sem, share, h_rows, dy_rows, w_v):
@@ -957,7 +951,6 @@
     stage,
     w_v,
     y_v,
-    dx_v,
     load_sem,
     row_sem,
     w_sem,
@@ -1010,10 +1003,8 @@
         early.send("c", 1, lambda: acts.at[q, :, :, other, :, lo:], lambda: pair_acts.at[q, :, :, :, hi:], nbytes(pair_acts, 1) * ff // cols)
 
     def out_come(step, half):
-        cut = slice(None) if half is None else half
-        part = nbytes(z_out, 1) // NC // (1 if half is None else 2)
-        src = lambda: z_out.at[place.get("y", step), cut, :, other]
-        early.send("c", 1, src, lambda: pair_acts.at[place.get("y", step), cut, :, :, lo:hi], part)
+        src = lambda: z_out.at[place.get("y", step), half, :, other]
+        early.send("c", 1, src, lambda: pair_acts.at[place.get("y", step), half, :, :, lo:hi], nbytes(z_out, 2) // NC)
 
     grads = Grads(nz, place, h_all, dy_all, acts, z_out, z_land, (g_gate, g_up, g_down, g_qkv, g_out), far, h_plus, h_minus, dy_minus, tiles, stage, g_load_sem, stage_sem, own_sem)
 
@@ -1024,10 +1015,15 @@
         for copy in row_loads:
             copy.start()
         z_load.wait()
-        attention(z_got, z_back, keys, vals, dk, dv, cos_ref, sin_ref)
-        place.meet()
-        for step in ORDER[:3]:
-            exchange(early, place, z_back, z_out, far_back, step, out_come)
+
+        def leave(p):
+            if p:
+                place.meet()
+            else:
+                early.spend(1.5)
+            exchange(early, place, z_back, z_out, far_back, p, out_come)
+
+        attention(z_got, z_back, keys, vals, dk, dv, cos_ref, sin_ref, leave)
         z_out[y] = z_back[y]
         early.send("c", 1, lambda: z_back.at[y, :, :, other], lambda: pair_acts.at[y, :, :, :, lo:hi], nbytes(z_out, 1) // NC)
         go()
@@ -1148,7 +1144,7 @@
         result_copies = []
 
         def leave(n, half):
-            copy = pltpu.make_async_copy((y_v, dx_v)[n].at[half], (y_out, dx_out)[n].at[half], out_sem.at[n, half])
+            copy = pltpu.make_async_copy((y_v, dy_ref)[n].at[half], (y_out, dx_out)[n].at[half], out_sem.at[n, half])
             copy.start()
             result_copies.append(copy)
 
@@ -1166,7 +1162,7 @@
             d_normed = ref()[:, :width].astype(bf16).astype(f32) * gain[...]
             mean = jnp.mean(d_normed * wide, axis=-1, keepdims=True)
             grad = d_normed * scale - wide * (scale * scale * scale * mean)
-            dx_v[half] = (dy_ref[half].astype(f32) + grad).astype(bf16)
+            dy_ref[half] = (dy_ref[half].astype(f32) + grad).astype(bf16)
             leave(1, half)
 
         def free(task):
@@ -1199,7 +1195,7 @@
     )
 
 
-STAGES = 5
+STAGES = 6
 PASSES = ((1, 0), (0, 0), (0, 1), (1, 1), (1, 2), (0, 2), (0, 3), (1, 3))
 P_TIME = 3.0
 Q_HALF = 2.6
@@ -1219,7 +1215,7 @@
     blocks = (NY, 2, NX // 2, NC, rows, pair)
     p_piece = (rows // 2, width - block)
     q_piece = (rows // 2, width + block)
-    count = 6 + 2 * NY + 5 + 4 * (nz - 1) + 5 * 4 + 2 * 5 * 6
+    count = 8 + 2 * NY + 7 + 4 * (nz - 1) + 5 * 4 + 2 * 5 * 6
     slab = block // NY
     weight = jax.ShapeDtypeStruct((slab, NY * ff), f32)
     return pl.pallas_call(
@@ -1261,7 +1257,6 @@
             pltpu.VMEM((STAGES, block, ff), f32),
             pltpu.VMEM((3, NC, block, cols), bf16),
             pltpu.VMEM(x.shape, bf16),
-            pltpu.VMEM(x.shape, bf16),
             dma,
             dma((3, 2)),
             dma((3,)),

time: 285 us -> 285 us (level)
  no operation moved by 1% of the time
where the time goes in v10:
time: 285 us; the launch traced here: 284 us
  Pallas kernels  284 us (100%)
    pallas_call x1, Pallas kernels, back(): pl.pallas_call(functools.partial(back_kernel, nz), out_shape=(jax.ShapeDt...  181 us
    pallas_call x1, Pallas kernels, front(): pl.pallas_call(functools.partial(front_kernel, nz), out_shape=(jax.ShapeD...  100 us

profile of v10, /device:TPU:1, one launch (start us, length us, event | category | flops | bytes accessed | tf_op | source)
XLA Modules:
  0.0 284.4 jit_solution(13118353568853801325)
XLA Ops:
  0.6 100.2 %front.1 = (bf16[4,4,2,2,32,3072]{5,4,3,2,1,0:T(8,128)(2,1)}, bf16[4,4,2,2,32,3072]{5,4,3,2,1,0:T(8,128)(2,1)}, bf16[2,8,4,96,1024]{4,3,2,1,0:T(8,128)(2,1)}, bf16[4,4,128,256]{3,2,1,0:T(8,128)(2,1)}) custom-call(bf16[2,32,3072]{2,1,0:T(8,128)(2,1)} %bitcast.18, bf16[2,32,3072]{2,1,0:T(8,128)(2,1)} %bitcast.20, f32[1,3072]{1,0:T(1,128)} %bitcast.27, ...), custom_call_target="tpu_custom_call" | custom-call | tf_op jit(solution)/shard_map/front/pallas_call | solution.py:472
  100.9 180.9 %back.1 = (bf16[2,32,3072]{2,1,0:T(8,128)(2,1)}, bf16[2,32,3072]{2,1,0:T(8,128)(2,1)}, f32[96,640]{1,0:T(8,128)}, f32[96,384]{1,0:T(8,128)}, f32[96,1024]{1,0:T(...) custom-call(bf16[4,2,256,256]{3,2,1,0:T(8,128)(2,1)} %bitcast.22, ...), custom_call_target="tpu_custom_call" | custom-call | tf_op jit(solution)/shard_map/back/pallas_call | solution.py:1221
  281.8 2.5 settle.1
